TPU v7x, 128 devices: a whole 4x4x4 slice. The times are simulated.
128 devices in a mesh: prompt: 4 (over x), resp: 32 (over y, z, core).
Axes of the slice: x: 4, y: 4, z: 4, core: 2. Of those that a mesh axis runs over, the one named last changes fastest.
Arguments:
- embeddings: bfloat16 [32, 1024, 3584], P('prompt', 'resp'), parts along dimension 0, may hold values from -6 to 6
- head_weight: bfloat16 [3584, 3584], P('resp'), may hold values from -0.0017089844 to 0.0017089844
- valid_mask: int32 [32, 1024], P('prompt', 'resp'), parts along dimension 0, may hold values from 0 to 1, as said below
Outputs:
- preferences: float32 [32, 1024, 1024], P('prompt', 'resp'), parts along dimension 0
- win_rates: float32 [32, 1024], P('prompt', 'resp'), parts along dimension 0
There are 4 independent parts, one for each index of `prompt`. A program takes and returns all parts, laid end to end along the dimension named above; an argument that names none is the same for every part. Nothing has to cross between parts.
Inputs may be any that keep to these rules, and one draw needn't show every extreme that they name: `valid_mask`: for each prompt the ones are its first response slots, between 256 and 1024 of them; in every draw some prompt has all 1024 slots filled.
All inputs are finite; a program needn't handle non-finite values.
Results may differ from a plain program's by a relative error of at most 0.003.
Values may be sent and summed in bfloat16 or wider, within the bound.
No kernel may reach another device: no remote copies, remote signals or barrier semaphores. Data moves between devices by JAX's collectives and lax.ppermute only.
A program may use at most 128 MiB of HBM per device.

v0:
```python
import jax
import jax.numpy as jnp
from jax import lax
from jax.sharding import PartitionSpec as P


def from_everyone(array, axis):
    copies = jnp.broadcast_to(array, (lax.axis_size(axis), *array.shape))
    return lax.all_to_all(copies, axis, split_axis=0, concat_axis=0, tiled=True)


def of_everyone(array, axis):
    everything = from_everyone(array, axis)
    return jnp.sum(everything, axis=0)


def from_behind(value, axis, steps):
    count = lax.axis_size(axis)
    pairs = [(source, (source + steps) % count) for source in range(count)]
    return lax.ppermute(value, axis, pairs)


def shards(embeddings, head_weight, valid_mask):
    group_size = lax.axis_size("resp")
    own_index = lax.axis_index("resp")
    prompts, block_rows, features = embeddings.shape
    halfway = group_size // 2
    quarter = group_size // 4
    valid_rows = valid_mask.astype(jnp.float32)
    counts = of_everyone(jnp.sum(valid_rows, axis=1), "resp")
    flat_rows = embeddings.reshape(prompts * block_rows, features)
    rows_in = lax.all_gather(head_weight, "resp", axis=0, tiled=True)
    direct = jnp.dot(flat_rows, rows_in, preferred_element_type=jnp.float32)
    partial_value = lax.dot_general(
        flat_rows, rows_in, (((1,), (1,)), ((), ())), preferred_element_type=jnp.float32
    )
    mirror = partial_value
    direct, mirror = (direct, mirror)
    projected = (direct - mirror).astype(jnp.bfloat16).reshape(prompts, block_rows, features)
    is_giver = own_index < halfway

    def pair_scores(block):
        return -jnp.einsum("prd,pqd->prq", embeddings, block, preferred_element_type=jnp.float32)

    def score_pair(block):
        return pair_scores(block)

    def record(scores_acc, outbox, block, distance):
        column = jnp.mod(own_index + distance, group_size)
        pair_tile = score_pair(block)
        at_middle = distance == halfway
        keep_it = jnp.logical_or(jnp.logical_not(at_middle), is_giver)
        kept_tile = jnp.where(keep_it, pair_tile, 0.0)
        scores_acc = lax.dynamic_update_slice_in_dim(
            scores_acc, kept_tile[:, :, None, :], column, 2
        )
        send_near = jnp.logical_and(distance > 0, distance < halfway)
        send_it = jnp.logical_or(send_near, jnp.logical_and(at_middle, is_giver))
        mirrored_tile = jnp.where(send_it, -jnp.swapaxes(pair_tile, 1, 2), 0.0)
        outbox = lax.dynamic_update_slice_in_dim(outbox, mirrored_tile[None], column, 0)
        return (scores_acc, outbox)

    scores_acc = jnp.zeros((prompts, block_rows, group_size, block_rows), jnp.float32)
    outbox = jnp.zeros((group_size, prompts, block_rows, block_rows), jnp.float32)
    scores_acc, outbox = record(scores_acc, outbox, projected, jnp.int32(0))
    farther = from_behind(projected, "resp", -(halfway + 1))

    def advance_both(turn, loop_state):
        nearer, farther_now, scores_now, outbox_now = loop_state
        nearer = from_behind(nearer, "resp", -1)
        farther_now = from_behind(farther_now, "resp", 1)
        scores_now, outbox_now = record(scores_now, outbox_now, nearer, turn + 1)
        scores_now, outbox_now = record(scores_now, outbox_now, farther_now, halfway - turn)
        return (nearer, farther_now, scores_now, outbox_now)

    final_state = lax.fori_loop(0, quarter, advance_both, (projected, farther, scores_acc, outbox))
    scores_acc, outbox = (final_state[2], final_state[3])
    returned = lax.all_to_all(
        outbox.astype(jnp.bfloat16), "resp", split_axis=0, concat_axis=0, tiled=True
    ).astype(outbox.dtype)
    combined = scores_acc + jnp.transpose(returned, (1, 2, 0, 3))
    combined = combined.reshape(prompts, block_rows, group_size * block_rows)
    column_ids = jnp.arange(group_size * block_rows, dtype=jnp.float32)
    valid_cols = (column_ids[None, :] < counts[:, None]).astype(jnp.float32)
    preferences = jax.nn.sigmoid(combined) * valid_rows[:, :, None] * valid_cols[:, None, :]
    totals = jnp.sum(preferences, axis=2) - 0.5 * valid_rows
    win_rates = valid_rows * totals / jnp.maximum(counts - 1.0, 1.0)[:, None]
    return (preferences, win_rates)


def solution(mesh):
    return jax.shard_map(
        shards,
        mesh=mesh,
        in_specs=(P("prompt", "resp", None), P("resp", None), P("prompt", "resp")),
        out_specs=(P("prompt", "resp", None), P("prompt", "resp")),
        check_vma=False,
    )
```

profile of v0, /device:TPU:1, one launch (start us, length us, event | category | flops | bytes accessed | tf_op | source)
XLA Modules:
  0.0 532.9 jit_solution(13282028840175158981)
XLA Ops:
  7.9 99.3 %all-gather.2.cloned.1.call-done = bf16[3584,3584]{1,0:T(8,128)(2,1)} async-done(((bf16[112,3584]{1,0:T(8,128)(2,1)}), bf16[3584,3584]{1,0:T(8,128)(2,1)}) %all-gather.2.cloned.1.call-update) | async-done | bytes 25690128 | tf_op jit(solution)/shard_map/all_gather | solution.py:32
  107.2 17.1 %fusion.8 = f32[256,3584]{1,0:T(8,128)} fusion(bf16[256,3584]{1,0:T(8,128)(2,1)} %bitcast.60, bf16[3584,3584]{1,0:T(8,128)(2,1)} %all-gather.2.cloned.1.call-done), kind=kOutput, calls=%fused_computation.24 | convolution fusion | flops 6576668672 | bytes 31195136 | tf_op jit(solution)/shard_map/dot_general | solution.py:33
  124.3 14.7 %fusion = bf16[256,3584]{1,0:T(8,128)(2,1)} fusion(f32[256,3584]{1,0:T(8,128)} %fusion.8, bf16[256,3584]{1,0:T(8,128)(2,1)S(1)} %bitcast.61, bf16[3584,3584]{1,0:T(8,128)(2,1)} %all-gather.2.cloned.1.call-done), kind=kOutput, calls=%fused_computation.5 | convolution fusion | flops 6578503680 | bytes 33030144 | tf_op jit(solution)/shard_map/dot_general | solution.py:34
  142.6 4.0 all-to-all-start.1
  149.1 35.5 %all-to-all-done.1 = f32[32,1,8]{2,1,0:T(1,128)S(1)} async-done(((f32[32,1,8]{2,1,0:T(1,128)}), f32[32,1,8]{2,1,0:T(1,128)S(1)}, u32[]{:S(2)}, u32[]{:S(2)}) %all-to-all-start.1) | async-done | bytes 1056 | tf_op jit(solution)/shard_map/all_to_all | solution.py:9
  189.9 287.4 %while.21 = (s32[]{:T(128)}, bf16[8,32,3584]{2,1,0:T(8,128)(2,1)}, bf16[8,32,3584]{2,1,0:T(8,128)(2,1)}, f32[8,32,32,32]{3,1,0,2:T(8,128)}, bf16[32,8,32,32]{2,3...) while((s32[]{:T(128)}, bf16[8,32,3584]{2,1,0:T(8,128)(2,1)}, ...), condition=%wide.region_1.0_spmd, body=%wide.region_0.0_spmd.sunk | while | flops 117506064 | bytes 37159556 | solution.py:76
  191.7 21.5 %collective-permute-done = bf16[8,32,3584]{2,1,0:T(8,128)(2,1)S(1)} collective-permute-done((bf16[8,32,3584]{2,1,0:T(8,128)(2,1)}, bf16[8,32,3584]{2,1,0:T(8,128)(2,1)S(1)}, u32[]{:S(2)}, u32[]{:S(2)}) %collective-permute-start) | collective-permute-done | bytes 1835040 | tf_op jit(solution)/shard_map/while/body/eval_jaxpr/ppermute | solution.py:20
  221.3 2.9 copy.34
  226.3 21.2 %collective-permute-done = bf16[8,32,3584]{2,1,0:T(8,128)(2,1)S(1)} collective-permute-done((bf16[8,32,3584]{2,1,0:T(8,128)(2,1)}, bf16[8,32,3584]{2,1,0:T(8,128)(2,1)S(1)}, u32[]{:S(2)}, u32[]{:S(2)}) %collective-permute-start) | collective-permute-done | bytes 1835040 | tf_op jit(solution)/shard_map/while/body/eval_jaxpr/ppermute | solution.py:20
  255.5 2.9 copy.34
  258.4 5.0 collective-permute-start
  263.5 18.2 %collective-permute-done = bf16[8,32,3584]{2,1,0:T(8,128)(2,1)S(1)} collective-permute-done((bf16[8,32,3584]{2,1,0:T(8,128)(2,1)}, bf16[8,32,3584]{2,1,0:T(8,128)(2,1)S(1)}, u32[]{:S(2)}, u32[]{:S(2)}) %collective-permute-start) | collective-permute-done | bytes 1835040 | tf_op jit(solution)/shard_map/while/body/eval_jaxpr/ppermute | solution.py:20
  289.8 2.9 copy.34
  292.7 7.9 %collective-permute-start = (bf16[8,32,3584]{2,1,0:T(8,128)(2,1)}, bf16[8,32,3584]{2,1,0:T(8,128)(2,1)S(1)}, u32[]{:S(2)}, u32[]{:S(2)}) collective-permute-start(bf16[8,32,3584]{2,1,0:T(8,128)(2,1)} %get-tuple-element.301), channel_id=1, source_target_pairs={{0,31},{1,0},{2,1},{3,2},{4,3},{5,4},{6,5},{7,6},{8,7},{9,8},{10,9... | collective-permute-start | bytes 5505032 | tf_op jit(solution)/shard_map/while/body/eval_jaxpr/ppermute | solution.py:20
  300.6 15.3 %collective-permute-done = bf16[8,32,3584]{2,1,0:T(8,128)(2,1)S(1)} collective-permute-done((bf16[8,32,3584]{2,1,0:T(8,128)(2,1)}, bf16[8,32,3584]{2,1,0:T(8,128)(2,1)S(1)}, u32[]{:S(2)}, u32[]{:S(2)}) %collective-permute-start) | collective-permute-done | bytes 1835040 | tf_op jit(solution)/shard_map/while/body/eval_jaxpr/ppermute | solution.py:20
  328.7 9.1 %collective-permute-start = (bf16[8,32,3584]{2,1,0:T(8,128)(2,1)}, bf16[8,32,3584]{2,1,0:T(8,128)(2,1)S(1)}, u32[]{:S(2)}, u32[]{:S(2)}) collective-permute-start(bf16[8,32,3584]{2,1,0:T(8,128)(2,1)} %get-tuple-element.301), channel_id=1, source_target_pairs={{0,31},{1,0},{2,1},{3,2},{4,3},{5,4},{6,5},{7,6},{8,7},{9,8},{10,9... | collective-permute-start | bytes 5505032 | tf_op jit(solution)/shard_map/while/body/eval_jaxpr/ppermute | solution.py:20
  337.8 14.9 %collective-permute-done = bf16[8,32,3584]{2,1,0:T(8,128)(2,1)S(1)} collective-permute-done((bf16[8,32,3584]{2,1,0:T(8,128)(2,1)}, bf16[8,32,3584]{2,1,0:T(8,128)(2,1)S(1)}, u32[]{:S(2)}, u32[]{:S(2)}) %collective-permute-start) | collective-permute-done | bytes 1835040 | tf_op jit(solution)/shard_map/while/body/eval_jaxpr/ppermute | solution.py:20
  365.9 9.1 %collective-permute-start = (bf16[8,32,3584]{2,1,0:T(8,128)(2,1)}, bf16[8,32,3584]{2,1,0:T(8,128)(2,1)S(1)}, u32[]{:S(2)}, u32[]{:S(2)}) collective-permute-start(bf16[8,32,3584]{2,1,0:T(8,128)(2,1)} %get-tuple-element.301), channel_id=1, source_target_pairs={{0,31},{1,0},{2,1},{3,2},{4,3},{5,4},{6,5},{7,6},{8,7},{9,8},{10,9... | collective-permute-start | bytes 5505032 | tf_op jit(solution)/shard_map/while/body/eval_jaxpr/ppermute | solution.py:20
  375.0 14.9 %collective-permute-done = bf16[8,32,3584]{2,1,0:T(8,128)(2,1)S(1)} collective-permute-done((bf16[8,32,3584]{2,1,0:T(8,128)(2,1)}, bf16[8,32,3584]{2,1,0:T(8,128)(2,1)S(1)}, u32[]{:S(2)}, u32[]{:S(2)}) %collective-permute-start) | collective-permute-done | bytes 1835040 | tf_op jit(solution)/shard_map/while/body/eval_jaxpr/ppermute | solution.py:20
  400.1 2.9 copy.34
  403.1 9.1 %collective-permute-start = (bf16[8,32,3584]{2,1,0:T(8,128)(2,1)}, bf16[8,32,3584]{2,1,0:T(8,128)(2,1)S(1)}, u32[]{:S(2)}, u32[]{:S(2)}) collective-permute-start(bf16[8,32,3584]{2,1,0:T(8,128)(2,1)} %get-tuple-element.301), channel_id=1, source_target_pairs={{0,31},{1,0},{2,1},{3,2},{4,3},{5,4},{6,5},{7,6},{8,7},{9,8},{10,9... | collective-permute-start | bytes 5505032 | tf_op jit(solution)/shard_map/while/body/eval_jaxpr/ppermute | solution.py:20
  412.1 14.9 %collective-permute-done = bf16[8,32,3584]{2,1,0:T(8,128)(2,1)S(1)} collective-permute-done((bf16[8,32,3584]{2,1,0:T(8,128)(2,1)}, bf16[8,32,3584]{2,1,0:T(8,128)(2,1)S(1)}, u32[]{:S(2)}, u32[]{:S(2)}) %collective-permute-start) | collective-permute-done | bytes 1835040 | tf_op jit(solution)/shard_map/while/body/eval_jaxpr/ppermute | solution.py:20
  437.3 2.9 copy.34
  440.2 9.1 %collective-permute-start = (bf16[8,32,3584]{2,1,0:T(8,128)(2,1)}, bf16[8,32,3584]{2,1,0:T(8,128)(2,1)S(1)}, u32[]{:S(2)}, u32[]{:S(2)}) collective-permute-start(bf16[8,32,3584]{2,1,0:T(8,128)(2,1)} %get-tuple-element.301), channel_id=1, source_target_pairs={{0,31},{1,0},{2,1},{3,2},{4,3},{5,4},{6,5},{7,6},{8,7},{9,8},{10,9... | collective-permute-start | bytes 5505032 | tf_op jit(solution)/shard_map/while/body/eval_jaxpr/ppermute | solution.py:20
  449.3 14.9 %collective-permute-done = bf16[8,32,3584]{2,1,0:T(8,128)(2,1)S(1)} collective-permute-done((bf16[8,32,3584]{2,1,0:T(8,128)(2,1)}, bf16[8,32,3584]{2,1,0:T(8,128)(2,1)S(1)}, u32[]{:S(2)}, u32[]{:S(2)}) %collective-permute-start) | collective-permute-done | bytes 1835040 | tf_op jit(solution)/shard_map/while/body/eval_jaxpr/ppermute | solution.py:20
  477.4 4.4 reshape.52
  481.8 13.8 %all-to-all-start = ((bf16[32,2,4096]{2,1,0:T(2,128)(2,1)}), bf16[32,2,4096]{2,1,0:T(2,128)(2,1)S(1)}, u32[]{:S(2)}, u32[]{:S(2)}) async-start(bf16[32,2,4096]{2,1,0:T(2,128)(2,1)} %reshape.52), calls=%async_computation | async-start | bytes 1048576 | tf_op jit(solution)/shard_map/all_to_all | solution.py:78
  495.8 5.6 %copy.12 = f32[8,32,32,32]{1,3,0,2:T(8,128)} copy(f32[8,32,32,32]{3,1,0,2:T(8,128)} %get-tuple-element.202) | data formatting | bytes 2097152 | tf_op jit(solution)/shard_map/while | solution.py:76
  501.5 5.8 %all-to-all-done = bf16[32,2,4096]{2,1,0:T(2,128)(2,1)S(1)} async-done(((bf16[32,2,4096]{2,1,0:T(2,128)(2,1)}), bf16[32,2,4096]{2,1,0:T(2,128)(2,1)S(1)}, u32[]{:S(2)}, u32[]{:S(2)}) %all-to-all-start) | async-done | bytes 524320 | tf_op jit(solution)/shard_map/all_to_all | solution.py:78
  508.3 5.8 %multiply_reduce_fusion = (f32[8,32]{1,0:T(8,128)S(1)}, f32[8,32,32,32]{1,3,0,2:T(8,128)}) fusion(f32[8,32,32]{2,0,1:T(8,128)S(1)} %compare_convert_fusion, f32[8,32]{1,0:T(8,128)S(1)} %convert_element_type.22, f32[8,32,32,32]{1,3,0,2:T(8,128)} %copy.12, bf16[32,8,32,32]{3,2,1,0:T(8,128)(2,1)S(1)} %reshape.53), kind=kLoop, calls=%fused_computation.11 | loop fusion | flops 2096896 | bytes 2656256 | tf_op jit(solution)/shard_map/reduce_sum | solution.py:86
  514.1 6.4 %copy.13 = f32[8,32,32,32]{3,2,1,0:T(8,128)} copy(f32[8,32,32,32]{1,3,0,2:T(8,128)} %get-tuple-element.221) | data formatting | bytes 2097152 | tf_op jit(solution)/shard_map/div | solution.py:85
  520.5 3.7 div.16
  (104 shorter events, 102.7 us)
Async XLA Ops:
  7.2 100.1 %all-gather.2.cloned.1.call-start = ((), (), s32[]{:S(2)}) async-start(), calls=%async_computation.2 | async-start | bytes 26492928 | tf_op jit(solution)/shard_map/all_gather | solution.py:32
  107.2 17.1 %copy-start.2 = (bf16[8,32,3584]{2,1,0:T(8,128)(2,1)S(1)}, bf16[8,32,3584]{2,1,0:T(8,128)(2,1)}, u32[]{:S(2)}) copy-start(bf16[8,32,3584]{2,1,0:T(8,128)(2,1)} %param.5) | copy-start | bytes 5505028
  124.3 17.5 %copy-start.1 = (s32[8,32]{1,0:T(8,128)S(1)}, s32[8,32]{1,0:T(8,128)}, u32[]{:S(2)}) copy-start(s32[8,32]{1,0:T(8,128)} %param.7) | copy-start | bytes 3076
  139.0 49.0 %collective-permute-start.2 = (bf16[8,32,3584]{2,1,0:T(8,128)(2,1)}, bf16[8,32,3584]{2,1,0:T(8,128)(2,1)}, u32[]{:S(2)}, u32[]{:S(2)}) collective-permute-start(bf16[8,32,3584]{2,1,0:T(8,128)(2,1)} %bitcast.62), channel_id=1, source_target_pairs={{0,15},{1,16},{2,17},{3,18},{4,19},{5,20},{6,21},{7,22},{8,23},{9,... | collective-permute-start | bytes 5505032 | tf_op jit(solution)/shard_map/ppermute | solution.py:20
  142.6 42.0 %all-to-all-start.1 = ((f32[32,1,8]{2,1,0:T(1,128)}), f32[32,1,8]{2,1,0:T(1,128)S(1)}, u32[]{:S(2)}, u32[]{:S(2)}) async-start(f32[32,1,8]{2,1,0:T(1,128)} %broadcast_in_dim.80), calls=%async_computation.1 | async-start | bytes 32768 | tf_op jit(solution)/shard_map/all_to_all | solution.py:9
  188.0 1.9 copy-start
  189.9 23.3 %collective-permute-start = (bf16[8,32,3584]{2,1,0:T(8,128)(2,1)}, bf16[8,32,3584]{2,1,0:T(8,128)(2,1)S(1)}, u32[]{:S(2)}, u32[]{:S(2)}) collective-permute-start(bf16[8,32,3584]{2,1,0:T(8,128)(2,1)} %get-tuple-element.301), channel_id=1, source_target_pairs={{0,31},{1,0},{2,1},{3,2},{4,3},{5,4},{6,5},{7,6},{8,7},{9,8},{10,9... | collective-permute-start | bytes 5505032 | tf_op jit(solution)/shard_map/while/body/eval_jaxpr/ppermute | solution.py:20
  190.6 26.0 %collective-permute-start.1 = (bf16[8,32,3584]{2,1,0:T(8,128)(2,1)}, bf16[8,32,3584]{2,1,0:T(8,128)(2,1)}, u32[]{:S(2)}, u32[]{:S(2)}) collective-permute-start(bf16[8,32,3584]{2,1,0:T(8,128)(2,1)} %get-tuple-element.302), channel_id=1, source_target_pairs={{0,1},{1,2},{2,3},{3,4},{4,5},{5,6},{6,7},{7,8},{8,9},{9,10},{10,1... | collective-permute-start | bytes 5505032 | tf_op jit(solution)/shard_map/while/body/eval_jaxpr/ppermute | solution.py:20
  191.7 24.9 %copy-start.3 = (bf16[8,32,3584]{2,1,0:T(8,128)(2,1)S(1)}, bf16[8,32,3584]{2,1,0:T(8,128)(2,1)}, u32[]{:S(2)}) copy-start(bf16[8,32,3584]{2,1,0:T(8,128)(2,1)} %get-tuple-element.319) | copy-start | bytes 5505028 | tf_op jit(solution)/shard_map/while
  224.2 23.3 %collective-permute-start = (bf16[8,32,3584]{2,1,0:T(8,128)(2,1)}, bf16[8,32,3584]{2,1,0:T(8,128)(2,1)S(1)}, u32[]{:S(2)}, u32[]{:S(2)}) collective-permute-start(bf16[8,32,3584]{2,1,0:T(8,128)(2,1)} %get-tuple-element.301), channel_id=1, source_target_pairs={{0,31},{1,0},{2,1},{3,2},{4,3},{5,4},{6,5},{7,6},{8,7},{9,8},{10,9... | collective-permute-start | bytes 5505032 | tf_op jit(solution)/shard_map/while/body/eval_jaxpr/ppermute | solution.py:20
  226.3 24.6 %collective-permute-start.1 = (bf16[8,32,3584]{2,1,0:T(8,128)(2,1)}, bf16[8,32,3584]{2,1,0:T(8,128)(2,1)}, u32[]{:S(2)}, u32[]{:S(2)}) collective-permute-start(bf16[8,32,3584]{2,1,0:T(8,128)(2,1)} %get-tuple-element.302), channel_id=1, source_target_pairs={{0,1},{1,2},{2,3},{3,4},{4,5},{5,6},{6,7},{7,8},{8,9},{9,10},{10,1... | collective-permute-start | bytes 5505032 | tf_op jit(solution)/shard_map/while/body/eval_jaxpr/ppermute | solution.py:20
  226.3 24.6 %copy-start.3 = (bf16[8,32,3584]{2,1,0:T(8,128)(2,1)S(1)}, bf16[8,32,3584]{2,1,0:T(8,128)(2,1)}, u32[]{:S(2)}) copy-start(bf16[8,32,3584]{2,1,0:T(8,128)(2,1)} %get-tuple-element.319) | copy-start | bytes 5505028 | tf_op jit(solution)/shard_map/while
  258.4 23.3 %collective-permute-start = (bf16[8,32,3584]{2,1,0:T(8,128)(2,1)}, bf16[8,32,3584]{2,1,0:T(8,128)(2,1)S(1)}, u32[]{:S(2)}, u32[]{:S(2)}) collective-permute-start(bf16[8,32,3584]{2,1,0:T(8,128)(2,1)} %get-tuple-element.301), channel_id=1, source_target_pairs={{0,31},{1,0},{2,1},{3,2},{4,3},{5,4},{6,5},{7,6},{8,7},{9,8},{10,9... | collective-permute-start | bytes 5505032 | tf_op jit(solution)/shard_map/while/body/eval_jaxpr/ppermute | solution.py:20
  263.5 21.6 %collective-permute-start.1 = (bf16[8,32,3584]{2,1,0:T(8,128)(2,1)}, bf16[8,32,3584]{2,1,0:T(8,128)(2,1)}, u32[]{:S(2)}, u32[]{:S(2)}) collective-permute-start(bf16[8,32,3584]{2,1,0:T(8,128)(2,1)} %get-tuple-element.302), channel_id=1, source_target_pairs={{0,1},{1,2},{2,3},{3,4},{4,5},{5,6},{6,7},{7,8},{8,9},{9,10},{10,1... | collective-permute-start | bytes 5505032 | tf_op jit(solution)/shard_map/while/body/eval_jaxpr/ppermute | solution.py:20
  263.5 21.6 %copy-start.3 = (bf16[8,32,3584]{2,1,0:T(8,128)(2,1)S(1)}, bf16[8,32,3584]{2,1,0:T(8,128)(2,1)}, u32[]{:S(2)}) copy-start(bf16[8,32,3584]{2,1,0:T(8,128)(2,1)} %get-tuple-element.319) | copy-start | bytes 5505028 | tf_op jit(solution)/shard_map/while
  292.7 23.3 %collective-permute-start = (bf16[8,32,3584]{2,1,0:T(8,128)(2,1)}, bf16[8,32,3584]{2,1,0:T(8,128)(2,1)S(1)}, u32[]{:S(2)}, u32[]{:S(2)}) collective-permute-start(bf16[8,32,3584]{2,1,0:T(8,128)(2,1)} %get-tuple-element.301), channel_id=1, source_target_pairs={{0,31},{1,0},{2,1},{3,2},{4,3},{5,4},{6,5},{7,6},{8,7},{9,8},{10,9... | collective-permute-start | bytes 5505032 | tf_op jit(solution)/shard_map/while/body/eval_jaxpr/ppermute | solution.py:20
  300.6 20.5 %collective-permute-start.1 = (bf16[8,32,3584]{2,1,0:T(8,128)(2,1)}, bf16[8,32,3584]{2,1,0:T(8,128)(2,1)}, u32[]{:S(2)}, u32[]{:S(2)}) collective-permute-start(bf16[8,32,3584]{2,1,0:T(8,128)(2,1)} %get-tuple-element.302), channel_id=1, source_target_pairs={{0,1},{1,2},{2,3},{3,4},{4,5},{5,6},{6,7},{7,8},{8,9},{9,10},{10,1... | collective-permute-start | bytes 5505032 | tf_op jit(solution)/shard_map/while/body/eval_jaxpr/ppermute | solution.py:20
  300.6 20.5 %copy-start.3 = (bf16[8,32,3584]{2,1,0:T(8,128)(2,1)S(1)}, bf16[8,32,3584]{2,1,0:T(8,128)(2,1)}, u32[]{:S(2)}) copy-start(bf16[8,32,3584]{2,1,0:T(8,128)(2,1)} %get-tuple-element.319) | copy-start | bytes 5505028 | tf_op jit(solution)/shard_map/while
  328.7 24.0 %collective-permute-start = (bf16[8,32,3584]{2,1,0:T(8,128)(2,1)}, bf16[8,32,3584]{2,1,0:T(8,128)(2,1)S(1)}, u32[]{:S(2)}, u32[]{:S(2)}) collective-permute-start(bf16[8,32,3584]{2,1,0:T(8,128)(2,1)} %get-tuple-element.301), channel_id=1, source_target_pairs={{0,31},{1,0},{2,1},{3,2},{4,3},{5,4},{6,5},{7,6},{8,7},{9,8},{10,9... | collective-permute-start | bytes 5505032 | tf_op jit(solution)/shard_map/while/body/eval_jaxpr/ppermute | solution.py:20
  337.8 20.5 %collective-permute-start.1 = (bf16[8,32,3584]{2,1,0:T(8,128)(2,1)}, bf16[8,32,3584]{2,1,0:T(8,128)(2,1)}, u32[]{:S(2)}, u32[]{:S(2)}) collective-permute-start(bf16[8,32,3584]{2,1,0:T(8,128)(2,1)} %get-tuple-element.302), channel_id=1, source_target_pairs={{0,1},{1,2},{2,3},{3,4},{4,5},{5,6},{6,7},{7,8},{8,9},{9,10},{10,1... | collective-permute-start | bytes 5505032 | tf_op jit(solution)/shard_map/while/body/eval_jaxpr/ppermute | solution.py:20
  337.8 20.5 %copy-start.3 = (bf16[8,32,3584]{2,1,0:T(8,128)(2,1)S(1)}, bf16[8,32,3584]{2,1,0:T(8,128)(2,1)}, u32[]{:S(2)}) copy-start(bf16[8,32,3584]{2,1,0:T(8,128)(2,1)} %get-tuple-element.319) | copy-start | bytes 5505028 | tf_op jit(solution)/shard_map/while
  365.9 24.0 %collective-permute-start = (bf16[8,32,3584]{2,1,0:T(8,128)(2,1)}, bf16[8,32,3584]{2,1,0:T(8,128)(2,1)S(1)}, u32[]{:S(2)}, u32[]{:S(2)}) collective-permute-start(bf16[8,32,3584]{2,1,0:T(8,128)(2,1)} %get-tuple-element.301), channel_id=1, source_target_pairs={{0,31},{1,0},{2,1},{3,2},{4,3},{5,4},{6,5},{7,6},{8,7},{9,8},{10,9... | collective-permute-start | bytes 5505032 | tf_op jit(solution)/shard_map/while/body/eval_jaxpr/ppermute | solution.py:20
  375.0 20.5 %collective-permute-start.1 = (bf16[8,32,3584]{2,1,0:T(8,128)(2,1)}, bf16[8,32,3584]{2,1,0:T(8,128)(2,1)}, u32[]{:S(2)}, u32[]{:S(2)}) collective-permute-start(bf16[8,32,3584]{2,1,0:T(8,128)(2,1)} %get-tuple-element.302), channel_id=1, source_target_pairs={{0,1},{1,2},{2,3},{3,4},{4,5},{5,6},{6,7},{7,8},{8,9},{9,10},{10,1... | collective-permute-start | bytes 5505032 | tf_op jit(solution)/shard_map/while/body/eval_jaxpr/ppermute | solution.py:20
  375.0 20.5 %copy-start.3 = (bf16[8,32,3584]{2,1,0:T(8,128)(2,1)S(1)}, bf16[8,32,3584]{2,1,0:T(8,128)(2,1)}, u32[]{:S(2)}) copy-start(bf16[8,32,3584]{2,1,0:T(8,128)(2,1)} %get-tuple-element.319) | copy-start | bytes 5505028 | tf_op jit(solution)/shard_map/while
  403.1 24.0 %collective-permute-start = (bf16[8,32,3584]{2,1,0:T(8,128)(2,1)}, bf16[8,32,3584]{2,1,0:T(8,128)(2,1)S(1)}, u32[]{:S(2)}, u32[]{:S(2)}) collective-permute-start(bf16[8,32,3584]{2,1,0:T(8,128)(2,1)} %get-tuple-element.301), channel_id=1, source_target_pairs={{0,31},{1,0},{2,1},{3,2},{4,3},{5,4},{6,5},{7,6},{8,7},{9,8},{10,9... | collective-permute-start | bytes 5505032 | tf_op jit(solution)/shard_map/while/body/eval_jaxpr/ppermute | solution.py:20
  412.1 20.5 %collective-permute-start.1 = (bf16[8,32,3584]{2,1,0:T(8,128)(2,1)}, bf16[8,32,3584]{2,1,0:T(8,128)(2,1)}, u32[]{:S(2)}, u32[]{:S(2)}) collective-permute-start(bf16[8,32,3584]{2,1,0:T(8,128)(2,1)} %get-tuple-element.302), channel_id=1, source_target_pairs={{0,1},{1,2},{2,3},{3,4},{4,5},{5,6},{6,7},{7,8},{8,9},{9,10},{10,1... | collective-permute-start | bytes 5505032 | tf_op jit(solution)/shard_map/while/body/eval_jaxpr/ppermute | solution.py:20
  412.1 20.5 %copy-start.3 = (bf16[8,32,3584]{2,1,0:T(8,128)(2,1)S(1)}, bf16[8,32,3584]{2,1,0:T(8,128)(2,1)}, u32[]{:S(2)}) copy-start(bf16[8,32,3584]{2,1,0:T(8,128)(2,1)} %get-tuple-element.319) | copy-start | bytes 5505028 | tf_op jit(solution)/shard_map/while
  440.2 24.0 %collective-permute-start = (bf16[8,32,3584]{2,1,0:T(8,128)(2,1)}, bf16[8,32,3584]{2,1,0:T(8,128)(2,1)S(1)}, u32[]{:S(2)}, u32[]{:S(2)}) collective-permute-start(bf16[8,32,3584]{2,1,0:T(8,128)(2,1)} %get-tuple-element.301), channel_id=1, source_target_pairs={{0,31},{1,0},{2,1},{3,2},{4,3},{5,4},{6,5},{7,6},{8,7},{9,8},{10,9... | collective-permute-start | bytes 5505032 | tf_op jit(solution)/shard_map/while/body/eval_jaxpr/ppermute | solution.py:20
  449.3 20.5 %collective-permute-start.1 = (bf16[8,32,3584]{2,1,0:T(8,128)(2,1)}, bf16[8,32,3584]{2,1,0:T(8,128)(2,1)}, u32[]{:S(2)}, u32[]{:S(2)}) collective-permute-start(bf16[8,32,3584]{2,1,0:T(8,128)(2,1)} %get-tuple-element.302), channel_id=1, source_target_pairs={{0,1},{1,2},{2,3},{3,4},{4,5},{5,6},{6,7},{7,8},{8,9},{9,10},{10,1... | collective-permute-start | bytes 5505032 | tf_op jit(solution)/shard_map/while/body/eval_jaxpr/ppermute | solution.py:20
  449.3 20.5 %copy-start.3 = (bf16[8,32,3584]{2,1,0:T(8,128)(2,1)S(1)}, bf16[8,32,3584]{2,1,0:T(8,128)(2,1)}, u32[]{:S(2)}) copy-start(bf16[8,32,3584]{2,1,0:T(8,128)(2,1)} %get-tuple-element.319) | copy-start | bytes 5505028 | tf_op jit(solution)/shard_map/while
  481.8 25.4 %all-to-all-start = ((bf16[32,2,4096]{2,1,0:T(2,128)(2,1)}), bf16[32,2,4096]{2,1,0:T(2,128)(2,1)S(1)}, u32[]{:S(2)}, u32[]{:S(2)}) async-start(bf16[32,2,4096]{2,1,0:T(2,128)(2,1)} %reshape.52), calls=%async_computation | async-start | bytes 1048576 | tf_op jit(solution)/shard_map/all_to_all | solution.py:78
Sparse Core Ops, SparseCore 0:
  10.2 96.9 all-gather.1
where the time goes:
time: 534 us; the launch traced here: 533 us
  waiting for transfers between devices  288 us (54%)
  matrix products  78.7 us (15%)
  starting transfers between devices  74 us (14%)
  local copies, waits for them, and re-layouts  60.3 us (11%)
  other arithmetic  18.1 us (3%)
  between operations  14.2 us (3%)
    ppermute x17, waiting for transfers between devices, from_behind(): return lax.ppermute(value, axis, pairs)  146 us
    all_gather x1, waiting for transfers between devices, shards(): rows_in = lax.all_gather(head_weight, 'resp', axis=0, tiled=True)  99.3 us
    ppermute x17, starting transfers between devices, from_behind(): return lax.ppermute(value, axis, pairs)  56.1 us
    dot_general x17, matrix products, pair_scores(): jnp.einsum('prd,pqd->prq', embeddings, block, preferred_element_type=jnp....  47 us
    all_to_all x1, waiting for transfers between devices, from_everyone(): return lax.all_to_all(copies, axis, split_axis=0, concat_axis=0, tiled=True)  35.5 us
    while x32, local copies, waits for them, and re-layouts  33.5 us
    dot_general x1, matrix products, shards(): direct = jnp.dot(flat_rows, rows_in, preferred_element_type=jnp.float32)  17.1 us
    dot_general x1, matrix products, shards(): lax.dot_general(flat_rows, rows_in, (((1,), (1,)), ((), ())), preferred_e...  14.7 us
  transfers between devices with their start and end apart: 20, of which 16 were waited for; matrix products, arithmetic and copies ran while one was open for 7% of the time, Pallas kernels for 0%

commit v1 on v0

v1 whole, which is shorter than its diff:
```python
import jax
import jax.numpy as jnp
from jax import lax
from jax.sharding import Mesh, PartitionSpec as P

RESP_AXES = ("y", "z", "c")
FILL = 256.0
FILL_TEST = 128.0
HIDDEN = -1e30
HIDDEN_TEST = -1e29


def ring(axis_size, step):
    return [(i, (i + step) % axis_size) for i in range(axis_size)]


def swap_cores(value):
    return lax.ppermute(value, "c", [(0, 1), (1, 0)])


def slab_pairs(first_core):
    pairs = []
    for y in range(4):
        for c in range(2):
            target = y if c == first_core else y ^ 2
            pairs.append((y * 2 + c, target * 2 + y // 2))
    return pairs


def shards(embeddings, head_weight, valid_mask):
    prompts, block_rows, features = embeddings.shape
    quarter = features // 4
    x = lax.axis_index("x")
    y = lax.axis_index("y")
    c = lax.axis_index("c")
    h = y % 2

    slab = lax.dynamic_slice_in_dim(head_weight, (y ^ x) * quarter, quarter, 1)
    part_a = lax.ppermute(slab, ("y", "c"), slab_pairs(0))
    part_b = lax.ppermute(slab, ("y", "c"), slab_pairs(1))
    at_home = c == y // 2
    both = jnp.stack([jnp.where(at_home, part_a, part_b), jnp.where(at_home, part_b, part_a)])
    copies = jnp.broadcast_to(both, (4, *both.shape))
    own = lax.all_to_all(copies, "z", 0, 0, tiled=True).reshape(quarter, quarter)
    half = quarter // 2
    below = lax.ppermute(own, "x", ring(4, 1))
    above = lax.ppermute(own, "x", ring(4, -1))
    across_top = lax.ppermute(below[:half], "x", ring(4, 1))
    across_bottom = lax.ppermute(above[half:], "x", ring(4, -1))
    across = jnp.concatenate([across_top, across_bottom])
    weights = jnp.zeros((4, quarter, quarter), head_weight.dtype)
    for step, piece in ((0, own), (3, below), (1, above), (2, across)):
        weights = lax.dynamic_update_slice_in_dim(weights, piece[None], (x + step) % 4, 0)

    filled = jnp.where(valid_mask[:, :, None] > 0, embeddings, jnp.asarray(FILL, embeddings.dtype))
    grouped = filled.reshape(2, 4, block_rows, 2, 2, quarter)
    grouped = jnp.transpose(grouped, (0, 1, 3, 2, 4, 5))
    outgoing = jnp.stack([grouped, grouped[..., ::-1, :]], axis=1)
    outgoing = outgoing.reshape(32, block_rows, 2 * quarter)
    near = lax.all_to_all(outgoing, RESP_AXES, 0, 0, tiled=True).reshape(32 * block_rows, 2 * quarter)
    far = swap_cores(near)

    def product(index, rows):
        return lax.dot_general(
            weights[index], rows, (((1,), (1,)), ((), ())), preferred_element_type=jnp.float32
        )

    mixed = product(0, near[:, :quarter]) + product(1, near[:, quarter:])
    mixed = mixed + product(2, far[:, :quarter]) + product(3, far[:, quarter:])
    table = jnp.dot(near[:, :quarter], mixed.astype(jnp.bfloat16), preferred_element_type=jnp.float32)
    skew = table - table.T
    slots = 32 * block_rows
    skew = skew.reshape(32, 2, block_rows // 2, slots)
    kept = lax.dynamic_slice_in_dim(skew, c, 1, 1)[:, 0]
    given = lax.dynamic_slice_in_dim(skew, 1 - c, 1, 1)[:, 0].astype(jnp.bfloat16)
    half_scores = kept + swap_cores(given).astype(jnp.float32)
    filled_columns = near[:, 0] < FILL_TEST
    half_scores = jnp.where(filled_columns[None, None, :], half_scores, HIDDEN).astype(jnp.bfloat16)
    returned = lax.all_to_all(half_scores, RESP_AXES, 0, 0, tiled=True)
    returned = returned.astype(jnp.float32).reshape(2, 2, 4, 2, block_rows // 2, slots)
    scores = (returned[:, 0] + returned[:, 1]).reshape(prompts, block_rows, slots)

    valid_rows = valid_mask.astype(jnp.float32)
    counts = jnp.sum((scores > HIDDEN_TEST).astype(jnp.float32), axis=2)
    preferences = jax.nn.sigmoid(scores) * valid_rows[:, :, None]
    totals = jnp.sum(preferences, axis=2) - 0.5 * valid_rows
    win_rates = valid_rows * totals / jnp.maximum(counts - 1.0, 1.0)
    return preferences, win_rates


def solution(mesh):
    mesh = Mesh(mesh.devices.reshape(4, 4, 4, 2), ("x", "y", "z", "c"))
    spec = P("x", RESP_AXES)
    return jax.shard_map(
        shards,
        mesh=mesh,
        in_specs=(P("x", RESP_AXES, None), P(RESP_AXES, None), spec),
        out_specs=(P("x", RESP_AXES, None), spec),
        check_vma=False,
    )
```

time: 534 us -> 258 us (0.48)
  waiting for transfers between devices: 288 us -> 130 us
  matrix products: 78.7 us -> 29.7 us
  starting transfers between devices: 74 us -> 32.1 us
  local copies, waits for them, and re-layouts: 60.3 us -> 41.5 us
  between operations: 14.2 us -> 0.9 us
    all_gather x1 -> x0, waiting for transfers between devices: 99.3 us -> none  [shards(): rows_in = lax.all_gather(head_weight, 'resp', axis=0, tiled=True)]
    ppermute x17 -> x8, waiting for transfers between devices: 146 us -> 94.3 us  [the longest x1 42.3 us: shards(): part_a = lax.ppermute(slab, ('y', 'c'), slab_pairs(0))]
    dot_general x19 -> x4, matrix products: 78.7 us -> 29.7 us  [the longest x3 17.6 us: product(): lax.dot_general(weights[index], rows, (((1,), (1,)), ((), ())), preferred...]
    ppermute x17 -> x8, starting transfers between devices: 56.1 us -> 12.6 us  [the longest x1 5.05 us: shards(): part_a = lax.ppermute(slab, ('y', 'c'), slab_pairs(0))]
    while x33 -> x0, local copies, waits for them, and re-layouts: 39.1 us -> none
    reshape x0 -> x3, local copies, waits for them, and re-layouts: none -> 13.8 us  [the longest x1 9.08 us: shards(): outgoing = outgoing.reshape(32, block_rows, 2 * quarter)]
    rev x0 -> x1, local copies, waits for them, and re-layouts: none -> 13.3 us  [shards(): outgoing = jnp.stack([grouped, grouped[..., ::-1, :]], axis=1)]
    div x2 -> x0, local copies, waits for them, and re-layouts: 10.1 us -> none  [shards(): jax.nn.sigmoid(combined) * valid_rows[:, :, None] * valid_cols[:, None, :]]
  transfers between devices with their start and end apart: 20 -> 11, of which waited for: 16 -> 8; matrix products, arithmetic and copies ran while one was open for 7% -> 5% of each run, Pallas kernels for 0% -> 0%
where the time goes in v1:
time: 258 us; the launch traced here: 257 us
  waiting for transfers between devices  130 us (50%)
  local copies, waits for them, and re-layouts  41.5 us (16%)
  starting transfers between devices  32.1 us (12%)
  matrix products  29.7 us (12%)
  other arithmetic  22.6 us (9%)
    ppermute x1, waiting for transfers between devices, shards(): part_a = lax.ppermute(slab, ('y', 'c'), slab_pairs(0))  42.3 us
    ppermute x1, waiting for transfers between devices, shards(): below = lax.ppermute(own, 'x', ring(4, 1))  34.2 us
    all_to_all x1, waiting for transfers between devices, shards(): lax.all_to_all(copies, 'z', 0, 0, tiled=True).reshape(quarter, quarter)  18.9 us
    dot_general x3, matrix products, product(): lax.dot_general(weights[index], rows, (((1,), (1,)), ((), ())), preferred...  17.6 us
    all_to_all x1, waiting for transfers between devices, shards(): returned = lax.all_to_all(half_scores, RESP_AXES, 0, 0, tiled=True)  16.8 us
    ppermute x1, waiting for transfers between devices, shards(): across_top = lax.ppermute(below[:half], 'x', ring(4, 1))  14.6 us
    rev x1, local copies, waits for them, and re-layouts, shards(): outgoing = jnp.stack([grouped, grouped[..., ::-1, :]], axis=1)  13.3 us
    dot_general x1, matrix products, shards(): jnp.dot(near[:, :quarter], mixed.astype(jnp.bfloat16), preferred_element_...  12.1 us
  transfers between devices with their start and end apart: 11, of which 8 were waited for; matrix products, arithmetic and copies ran while one was open for 5% of the time, Pallas kernels for 0%

profile of v1, /device:TPU:1, one launch (start us, length us, event | category | flops | bytes accessed | tf_op | source)
XLA Modules:
  0.0 256.8 jit_solution(1000089322742838224)
XLA Ops:
  1.4 1.7 broadcast_select_fusion
  3.1 1.5 reshape.57
  4.6 3.2 %copy.19 = bf16[2,4,32,2,2,896]{5,4,2,3,1,0:T(2,128)(2,1)S(1)} copy(bf16[2,4,32,2,2,896]{5,4,3,2,1,0:T(2,128)(2,1)} %reshape.57) | data formatting | bytes 3670016 | tf_op jit(solution)/shard_map/reshape | solution.py:56
  7.8 13.3 %rev.3 = bf16[2,4,2,32,2,896]{5,4,3,2,1,0:T(2,128)(2,1)} reverse(bf16[2,4,2,32,2,896]{5,4,3,2,1,0:T(2,128)(2,1)S(1)} %bitcast.73), dimensions={4} | reverse | bytes 3670016 | tf_op jit(solution)/shard_map/rev | solution.py:58
  21.1 8.7 %pad_maximum_fusion = bf16[2,2,4,2,32,2,896]{6,5,4,3,2,1,0:T(2,128)(2,1)} fusion(bf16[2,1,4,2,32,2,896]{6,5,4,3,2,1,0:T(2,128)(2,1)} %bitcast.77, bf16[2,1,4,2,32,2,896]{6,5,4,3,2,1,0:T(2,128)(2,1)S(1)} %bitcast.74), kind=kLoop, calls=%fused_computation.1 | loop fusion | flops 1835008 | bytes 7340032 | tf_op jit(solution)/shard_map/stack | solution.py:58
  29.8 9.1 %reshape.58 = bf16[32,32,1792]{2,1,0:T(8,128)(2,1)} reshape(bf16[2,2,4,2,32,2,896]{6,5,4,3,2,1,0:T(2,128)(2,1)} %pad_maximum_fusion) | data formatting | bytes 7340032 | tf_op jit(solution)/shard_map/reshape | solution.py:59
  38.9 9.6 %all-to-all-start = ((bf16[32,32,1792]{2,1,0:T(8,128)(2,1)}), bf16[32,32,1792]{2,1,0:T(8,128)(2,1)}, u32[]{:S(2)}, u32[]{:S(2)}) async-start(bf16[32,32,1792]{2,1,0:T(8,128)(2,1)} %reshape.58), calls=%async_computation | async-start | bytes 7340032 | tf_op jit(solution)/shard_map/all_to_all | solution.py:60
  48.6 5.1 %collective-permute-start = (bf16[112,896]{1,0:T(8,128)(2,1)S(1)}, bf16[112,896]{1,0:T(8,128)(2,1)S(1)}, u32[]{:S(2)}, u32[]{:S(2)}) collective-permute-start(bf16[112,896]{1,0:T(8,128)(2,1)S(1)} %constant_dynamic-slice_fusion), channel_id=1, source_target_pairs={{0,0},{1,16},{8,8},{9,24},{16,17},{17,1},{24,25},{25,9},{2,2},{3,1... | collective-permute-start | bytes 602120 | tf_op jit(solution)/shard_map/ppermute | solution.py:39
  53.6 1.9 collective-permute-start.1
  55.6 42.3 %collective-permute-done = bf16[112,896]{1,0:T(8,128)(2,1)S(1)} collective-permute-done((bf16[112,896]{1,0:T(8,128)(2,1)S(1)}, bf16[112,896]{1,0:T(8,128)(2,1)S(1)}, u32[]{:S(2)}, u32[]{:S(2)}) %collective-permute-start) | collective-permute-done | bytes 200736 | tf_op jit(solution)/shard_map/ppermute | solution.py:39
  98.6 1.3 broadcast_in_dim.46
  99.9 3.6 %all-to-all-start.1 = ((bf16[4,2,112,896]{3,2,1,0:T(8,128)(2,1)}), bf16[4,2,112,896]{3,2,1,0:T(8,128)(2,1)S(1)}, u32[]{:S(2)}, u32[]{:S(2)}) async-start(bf16[4,2,112,896]{3,2,1,0:T(8,128)(2,1)} %broadcast_in_dim.46), calls=%async_computation.1 | async-start | bytes 3211264 | tf_op jit(solution)/shard_map/all_to_all | solution.py:44
  103.6 18.9 %all-to-all-done.1 = bf16[4,2,112,896]{3,2,1,0:T(8,128)(2,1)S(1)} async-done(((bf16[4,2,112,896]{3,2,1,0:T(8,128)(2,1)}), bf16[4,2,112,896]{3,2,1,0:T(8,128)(2,1)S(1)}, u32[]{:S(2)}, u32[]{:S(2)}) %all-to-all-start.1) | async-done | bytes 1605664 | tf_op jit(solution)/shard_map/all_to_all | solution.py:44
  122.4 1.2 collective-permute-start.2
  123.7 1.5 collective-permute-start.3
  125.1 34.2 %collective-permute-done.2 = bf16[896,896]{1,0:T(8,128)(2,1)S(1)} collective-permute-done((bf16[896,896]{1,0:T(8,128)(2,1)S(1)}, bf16[896,896]{1,0:T(8,128)(2,1)S(1)}, u32[]{:S(2)}, u32[]{:S(2)}) %collective-permute-start.2) | collective-permute-done | bytes 1605664 | tf_op jit(solution)/shard_map/ppermute | solution.py:46
  161.9 1.8 collective-permute-start.5
  166.0 14.6 %collective-permute-done.4 = bf16[448,896]{1,0:T(8,128)(2,1)S(1)} collective-permute-done((bf16[448,896]{1,0:T(8,128)(2,1)S(1)}, bf16[448,896]{1,0:T(8,128)(2,1)S(1)}, u32[]{:S(2)}, u32[]{:S(2)}) %collective-permute-start.4) | collective-permute-done | bytes 802848 | tf_op jit(solution)/shard_map/ppermute | solution.py:48
  180.7 1.4 collective-permute-done.5
  182.1 1.4 fusion.12
  183.5 6.8 %fusion.10 = f32[896,1024]{1,0:T(8,128)} fusion(bf16[1024,1792]{1,0:T(8,128)(2,1)} %bitcast.4, bf16[4,896,896]{2,1,0:T(8,128)(2,1)S(1)} %fusion.12), kind=kOutput, calls=%fused_computation.16 | convolution fusion | flops 1644167168 | bytes 7110656 | tf_op jit(solution)/shard_map/dot_general | solution.py:64
  190.3 5.4 %fusion.5 = f32[896,1024]{1,0:T(8,128)} fusion(bf16[1024,1792]{1,0:T(8,128)(2,1)} %collective-permute-done.6, bf16[4,896,896]{2,1,0:T(8,128)(2,1)S(1)} %fusion.12), kind=kOutput, calls=%fused_computation.10 | convolution fusion | flops 1644167168 | bytes 7110656 | tf_op jit(solution)/shard_map/dot_general | solution.py:64
  195.7 5.4 %fusion.3 = f32[896,1024]{1,0:T(8,128)} fusion(bf16[1024,1792]{1,0:T(8,128)(2,1)} %collective-permute-done.6, bf16[4,896,896]{2,1,0:T(8,128)(2,1)S(1)} %fusion.12), kind=kOutput, calls=%fused_computation.8 | convolution fusion | flops 1644167168 | bytes 7110656 | tf_op jit(solution)/shard_map/dot_general | solution.py:64
  201.1 12.1 %fusion.2 = f32[1024,1024]{1,0:T(8,128)} fusion(f32[896,1024]{1,0:T(8,128)} %fusion.3, f32[896,1024]{1,0:T(8,128)} %fusion.5, f32[896,1024]{1,0:T(8,128)} %fusion.10, bf16[1024,1792]{1,0:T(8,128)(2,1)} %bitcast.4, bf16[4,896,896]{2,1,0:T(8,128)(2,1)} %copy-done.3), kind=kOutput, calls=%fused_computation.7 | convolution fusion | flops 3526885376 | bytes 20480000 | tf_op jit(solution)/shard_map/dot_general | solution.py:70
  213.2 5.4 %copy.11 = f32[1024,1024]{0,1:T(8,128)} copy(f32[1024,1024]{1,0:T(8,128)} %fusion.2) | data formatting | bytes 8388608 | tf_op jit(solution)/shard_map/dot_general | solution.py:70
  218.6 4.4 %bitcast_subtract_fusion = f32[1024,1024]{1,0:T(8,128)S(1)} fusion(f32[1024,1024]{1,0:T(8,128)} %fusion.2, f32[1024,1024]{0,1:T(8,128)} %copy.11), kind=kLoop, calls=%fused_computation | loop fusion | flops 1048576 | bytes 12582912 | tf_op jit(solution)/shard_map/sub | solution.py:71
  223.0 2.0 copy-done.2
  226.8 1.1 collective-permute-done.7
  227.9 2.9 %fusion.1 = bf16[32,16,1024]{2,1,0:T(8,128)(2,1)} fusion(bf16[32,16,1024]{2,1,0:T(8,128)(2,1)S(1)} %collective-permute-done.7, f32[32,2,16,1024]{3,2,1,0:T(8,128)} %bitcast.76, s32[]{:T(128)S(6)} %select_n.78, pred[1024]{0:T(1024)(128)(4,1)S(1)} %compare_reduce_fusion), kind=kLoop, calls=%fused_computation.5 | loop fusion | flops 2097152 | bytes 4195332 | tf_op jit(solution)/shard_map/convert_element_type | solution.py:78
  230.9 6.3 %all-to-all-start.2 = ((bf16[32,16,1024]{2,1,0:T(8,128)(2,1)}), bf16[32,16,1024]{2,1,0:T(8,128)(2,1)S(1)}, u32[]{:S(2)}, u32[]{:S(2)}) async-start(bf16[32,16,1024]{2,1,0:T(8,128)(2,1)} %fusion.1), calls=%async_computation.2 | async-start | bytes 2097152 | tf_op jit(solution)/shard_map/all_to_all | solution.py:79
  237.3 16.8 %all-to-all-done.2 = bf16[32,16,1024]{2,1,0:T(8,128)(2,1)S(1)} async-done(((bf16[32,16,1024]{2,1,0:T(8,128)(2,1)}), bf16[32,16,1024]{2,1,0:T(8,128)(2,1)S(1)}, u32[]{:S(2)}, u32[]{:S(2)}) %all-to-all-start.2) | async-done | bytes 1048608 | tf_op jit(solution)/shard_map/all_to_all | solution.py:79
  255.0 1.1 broadcast_multiply_fusion
  (46 shorter events, 9.9 us)
Async XLA Ops:
  0.6 47.9 %copy-start = (bf16[112,3584]{1,0:T(8,128)(2,1)S(1)}, bf16[112,3584]{1,0:T(8,128)(2,1)}, u32[]{:S(2)}) copy-start(bf16[112,3584]{1,0:T(8,128)(2,1)} %param.4) | copy-start | bytes 2408452
  38.9 59.7 %all-to-all-start = ((bf16[32,32,1792]{2,1,0:T(8,128)(2,1)}), bf16[32,32,1792]{2,1,0:T(8,128)(2,1)}, u32[]{:S(2)}, u32[]{:S(2)}) async-start(bf16[32,32,1792]{2,1,0:T(8,128)(2,1)} %reshape.58), calls=%async_computation | async-start | bytes 7340032 | tf_op jit(solution)/shard_map/all_to_all | solution.py:60
  48.6 49.3 %collective-permute-start = (bf16[112,896]{1,0:T(8,128)(2,1)S(1)}, bf16[112,896]{1,0:T(8,128)(2,1)S(1)}, u32[]{:S(2)}, u32[]{:S(2)}) collective-permute-start(bf16[112,896]{1,0:T(8,128)(2,1)S(1)} %constant_dynamic-slice_fusion), channel_id=1, source_target_pairs={{0,0},{1,16},{8,8},{9,24},{16,17},{17,1},{24,25},{25,9},{2,2},{3,1... | collective-permute-start | bytes 602120 | tf_op jit(solution)/shard_map/ppermute | solution.py:39
  53.6 44.8 %collective-permute-start.1 = (bf16[112,896]{1,0:T(8,128)(2,1)S(1)}, bf16[112,896]{1,0:T(8,128)(2,1)S(1)}, u32[]{:S(2)}, u32[]{:S(2)}) collective-permute-start(bf16[112,896]{1,0:T(8,128)(2,1)S(1)} %constant_dynamic-slice_fusion), channel_id=1, source_target_pairs={{0,16},{1,0},{8,24},{9,8},{16,1},{17,17},{24,9},{25,25},{2,18},{3,... | collective-permute-start | bytes 602120 | tf_op jit(solution)/shard_map/ppermute | solution.py:40
  99.9 22.5 %all-to-all-start.1 = ((bf16[4,2,112,896]{3,2,1,0:T(8,128)(2,1)}), bf16[4,2,112,896]{3,2,1,0:T(8,128)(2,1)S(1)}, u32[]{:S(2)}, u32[]{:S(2)}) async-start(bf16[4,2,112,896]{3,2,1,0:T(8,128)(2,1)} %broadcast_in_dim.46), calls=%async_computation.1 | async-start | bytes 3211264 | tf_op jit(solution)/shard_map/all_to_all | solution.py:44
  103.5 86.8 %collective-permute-start.6 = (bf16[1024,1792]{1,0:T(8,128)(2,1)}, bf16[1024,1792]{1,0:T(8,128)(2,1)}, u32[]{:S(2)}, u32[]{:S(2)}) collective-permute-start(bf16[1024,1792]{1,0:T(8,128)(2,1)} %bitcast.4), channel_id=1, source_target_pairs={{0,1},{1,0},{2,3},{3,2},{4,5},{5,4},{6,7},{7,6},{8,9},{9,8},{10,11... | collective-permute-start | bytes 11010056 | tf_op jit(solution)/shard_map/ppermute | solution.py:18
  122.4 36.9 %collective-permute-start.2 = (bf16[896,896]{1,0:T(8,128)(2,1)S(1)}, bf16[896,896]{1,0:T(8,128)(2,1)S(1)}, u32[]{:S(2)}, u32[]{:S(2)}) collective-permute-start(bf16[896,896]{1,0:T(8,128)(2,1)S(1)} %bitcast.78), channel_id=1, source_target_pairs={{0,32},{32,64},{64,96},{96,0},{1,33},{33,65},{65,97},{97,1},{2,34}... | collective-permute-start | bytes 4816904 | tf_op jit(solution)/shard_map/ppermute | solution.py:46
  123.7 36.3 %collective-permute-start.3 = (bf16[896,896]{1,0:T(8,128)(2,1)S(1)}, bf16[896,896]{1,0:T(8,128)(2,1)S(1)}, u32[]{:S(2)}, u32[]{:S(2)}) collective-permute-start(bf16[896,896]{1,0:T(8,128)(2,1)S(1)} %bitcast.79), channel_id=1, source_target_pairs={{0,96},{32,0},{64,32},{96,64},{1,97},{33,1},{65,33},{97,65},{2,98}... | collective-permute-start | bytes 4816904 | tf_op jit(solution)/shard_map/ppermute | solution.py:47
  159.3 1.2 copy-start.4
  159.4 21.3 %collective-permute-start.4 = (bf16[448,896]{1,0:T(8,128)(2,1)S(1)}, bf16[448,896]{1,0:T(8,128)(2,1)S(1)}, u32[]{:S(2)}, u32[]{:S(2)}) collective-permute-start(bf16[448,896]{1,0:T(8,128)(2,1)S(1)} %slice.55), channel_id=1, source_target_pairs={{0,32},{32,64},{64,96},{96,0},{1,33},{33,65},{65,97},{97,1},{2,34}... | collective-permute-start | bytes 2408456 | tf_op jit(solution)/shard_map/ppermute | solution.py:48
  160.5 1.4 copy-start.6
  161.9 20.2 %collective-permute-start.5 = (bf16[448,896]{1,0:T(8,128)(2,1)}, bf16[448,896]{1,0:T(8,128)(2,1)}, u32[]{:S(2)}, u32[]{:S(2)}) collective-permute-start(bf16[448,896]{1,0:T(8,128)(2,1)} %slice.56), channel_id=1, source_target_pairs={{0,96},{32,0},{64,32},{96,64},{1,97},{33,1},{65,33},{97,65},{2,98}... | collective-permute-start | bytes 2408456 | tf_op jit(solution)/shard_map/ppermute | solution.py:49
  163.7 1.4 copy-start.5
  164.2 1.5 copy-start.7
  183.5 12.2 %copy-start.3 = (bf16[4,896,896]{2,1,0:T(8,128)(2,1)}, bf16[4,896,896]{2,1,0:T(8,128)(2,1)S(1)}, u32[]{:S(2)}) copy-start(bf16[4,896,896]{2,1,0:T(8,128)(2,1)S(1)} %fusion.12) | copy-start | bytes 19267588
  223.0 2.0 copy-start.2
  225.2 12.0 %copy-start.8 = (s32[8,32]{1,0:T(8,128)S(1)}, s32[8,32]{1,0:T(8,128)}, u32[]{:S(2)}) copy-start(s32[8,32]{1,0:T(8,128)} %param.5) | copy-start | bytes 3076
  225.2 2.8 %collective-permute-start.7 = (bf16[32,16,1024]{2,1,0:T(8,128)(2,1)S(1)}, bf16[32,16,1024]{2,1,0:T(8,128)(2,1)S(1)}, u32[]{:S(2)}, u32[]{:S(2)}) collective-permute-start(bf16[32,16,1024]{2,1,0:T(8,128)(2,1)S(1)} %fusion.17), channel_id=1, source_target_pairs={{0,1},{1,0},{2,3},{3,2},{4,5},{5,4},{6,7},{7,6},{8,9},{9,8},{10,11... | collective-permute-start | bytes 3145736 | tf_op jit(solution)/shard_map/ppermute | solution.py:18
  230.9 23.2 %all-to-all-start.2 = ((bf16[32,16,1024]{2,1,0:T(8,128)(2,1)}), bf16[32,16,1024]{2,1,0:T(8,128)(2,1)S(1)}, u32[]{:S(2)}, u32[]{:S(2)}) async-start(bf16[32,16,1024]{2,1,0:T(8,128)(2,1)} %fusion.1), calls=%async_computation.2 | async-start | bytes 2097152 | tf_op jit(solution)/shard_map/all_to_all | solution.py:79
  237.2 19.6 %copy-start.1 = (bf16[112,3584]{1,0:T(8,128)(2,1)S(1)}, bf16[112,3584]{1,0:T(8,128)(2,1)}, u32[]{:S(2)}) copy-start(bf16[112,3584]{1,0:T(8,128)(2,1)} %param.4) | copy-start | bytes 2408452

commit v2 on v1

v2 whole, which is shorter than its diff:
```python
import jax
import jax.numpy as jnp
from jax import lax
from jax.experimental import pallas as pl
from jax.experimental.pallas import tpu as pltpu
from jax.sharding import Mesh, PartitionSpec as P


RESP_AXES = ("y", "z", "c")
FILL = 256.0
FILL_TEST = 128.0
HIDDEN = 1e30
HIDDEN_TEST = -1e29


def ring(value, axis, step):
    return lax.ppermute(value, axis, [(i, (i + step) % 4) for i in range(4)])


def swap_cores(value):
    return lax.ppermute(value, "c", [(0, 1), (1, 0)])


def slab_pairs(first_core):
    pairs = []
    for y in range(4):
        for c in range(2):
            target = y if c == first_core else y ^ 2
            pairs.append((y * 2 + c, target * 2 + y // 2))
    return pairs


def pack_kernel(rows_ref, valid_ref, out_ref):
    rows = rows_ref[0]
    filled = jnp.where(valid_ref[0] > 0, rows, jnp.asarray(FILL, rows.dtype))
    half = filled.shape[1] // 2
    quarter = half // 2
    for c in range(2):
        lanes = filled[:, c * half : (c + 1) * half]
        out_ref[0, 0, 0, c] = lanes
        out_ref[0, 1, 0, c, :, :quarter] = lanes[:, quarter:]
        out_ref[0, 1, 0, c, :, quarter:] = lanes[:, :quarter]


def pack(embeddings, valid_mask):
    prompts, block_rows, features = embeddings.shape
    half = features // 2
    out = pl.pallas_call(
        pack_kernel,
        grid=(prompts,),
        in_specs=[
            pl.BlockSpec((1, block_rows, features), lambda p: (p, 0, 0)),
            pl.BlockSpec((1, block_rows, 1), lambda p: (p, 0, 0)),
        ],
        out_specs=pl.BlockSpec((1, 2, 1, 2, block_rows, half), lambda p: (p // 4, 0, p % 4, 0, 0, 0)),
        out_shape=jax.ShapeDtypeStruct((2, 2, 4, 2, block_rows, half), embeddings.dtype),
    )(embeddings, valid_mask[:, :, None])
    return out.reshape(32, block_rows, half)


def load_weights(place_ref, pieces, w_ref, sems, first):
    quarter = w_ref.shape[0]
    rows = quarter // 4
    for s in range(4):
        position = lax.rem(place_ref[0] + s, 4)

        @pl.when(jnp.logical_and(position >= first, position < first + 2))
        def _():
            for r in range(4):
                at = pl.multiple_of(lax.rem(place_ref[1] + r, 4) * rows, rows)
                lanes = pl.multiple_of((position - first) * quarter, quarter)
                pltpu.make_async_copy(
                    pieces[s * 4 + r], w_ref.at[pl.ds(at, rows), pl.ds(lanes, quarter)], sems.at[s * 4 + r]
                ).start()


def wait_weights(place_ref, pieces, w_ref, sems, first):
    quarter = w_ref.shape[0]
    rows = quarter // 4
    for s in range(4):
        position = lax.rem(place_ref[0] + s, 4)

        @pl.when(jnp.logical_and(position >= first, position < first + 2))
        def _():
            for r in range(4):
                at = pl.multiple_of(lax.rem(place_ref[1] + r, 4) * rows, rows)
                lanes = pl.multiple_of((position - first) * quarter, quarter)
                pltpu.make_async_copy(
                    pieces[s * 4 + r], w_ref.at[pl.ds(at, rows), pl.ds(lanes, quarter)], sems.at[s * 4 + r]
                ).wait()


def times_rows(w_ref, rows_ref):
    return lax.dot_general(
        w_ref[...], rows_ref[...], (((1,), (1,)), ((), ())), preferred_element_type=jnp.float32
    )


def near_kernel(place_ref, near_ref, *refs):
    pieces, mixed_ref, w_ref, sems = refs[:16], refs[16], refs[17], refs[18]
    load_weights(place_ref, pieces, w_ref, sems, 0)
    wait_weights(place_ref, pieces, w_ref, sems, 0)
    mixed_ref[...] = times_rows(w_ref, near_ref)


def far_kernel(place_ref, near_ref, far_ref, mixed_ref, *refs):
    pieces, kept_ref, given_ref, w_ref, total_ref, table_ref, sems = refs[:16], *refs[16:]
    load_weights(place_ref, pieces, w_ref, sems, 2)
    wait_weights(place_ref, pieces, w_ref, sems, 2)
    total_ref[...] = (mixed_ref[...] + times_rows(w_ref, far_ref)).astype(total_ref.dtype)
    quarter = w_ref.shape[0]
    slots = table_ref.shape[0]
    hidden = jnp.where(near_ref[:, :1].astype(jnp.float32) < FILL_TEST, 0.0, HIDDEN)
    table_ref[...] = (
        jnp.dot(near_ref[:, :quarter], total_ref[...], preferred_element_type=jnp.float32) + hidden
    )
    c = place_ref[2]
    block = 128
    part = kept_ref.shape[1]
    for i in range(slots // block):
        rows = slice(i * block, (i + 1) * block)
        skew = table_ref[rows, :] - table_ref[:, rows].T
        groups = block // (2 * part)
        skew = skew.reshape(groups, 2, part, slots)
        first, second = skew[:, 0], skew[:, 1]
        at = slice(i * groups, (i + 1) * groups)
        kept_ref[at] = jnp.where(c == 0, first, second)
        given_ref[at] = jnp.where(c == 0, second, first).astype(given_ref.dtype)


def in_hbm():
    return pl.BlockSpec(memory_space=pl.ANY)


def whole():
    return pl.BlockSpec(memory_space=pltpu.VMEM)


def score_parts(place, near, far, pieces):
    slots, half = near.shape
    quarter = half // 2
    scalars = pl.BlockSpec(memory_space=pltpu.SMEM)
    limit = pltpu.CompilerParams(vmem_limit_bytes=56 * 2**20)
    mixed = pl.pallas_call(
        near_kernel,
        in_specs=[scalars, whole()] + [in_hbm()] * 16,
        out_specs=whole(),
        out_shape=jax.ShapeDtypeStruct((quarter, slots), jnp.float32),
        scratch_shapes=[pltpu.VMEM((quarter, half), near.dtype), pltpu.SemaphoreType.DMA((16,))],
        compiler_params=limit,
        cost_estimate=pl.CostEstimate(
            flops=2 * quarter * half * slots, bytes_accessed=12 * 2**20, transcendentals=0
        ),
    )(place, near, *pieces)
    part = slots // 64
    return pl.pallas_call(
        far_kernel,
        in_specs=[scalars, whole(), whole(), whole()] + [in_hbm()] * 16,
        out_specs=[whole(), whole()],
        out_shape=[
            jax.ShapeDtypeStruct((32, part, slots), jnp.float32),
            jax.ShapeDtypeStruct((32, part, slots), jnp.bfloat16),
        ],
        scratch_shapes=[
            pltpu.VMEM((quarter, half), near.dtype),
            pltpu.VMEM((quarter, slots), near.dtype),
            pltpu.VMEM((slots, slots), jnp.float32),
            pltpu.SemaphoreType.DMA((16,)),
        ],
        compiler_params=limit,
        cost_estimate=pl.CostEstimate(
            flops=2 * quarter * (half + slots) * slots, bytes_accessed=16 * 2**20, transcendentals=0
        ),
    )(place, near, far, mixed, *pieces)


def scored(embeddings, head_weight, valid_mask):
    prompts, block_rows, features = embeddings.shape
    quarter = features // 4
    slots = 32 * block_rows
    x = lax.axis_index("x")
    y = lax.axis_index("y")
    z = lax.axis_index("z")
    c = lax.axis_index("c")

    slab = lax.dynamic_slice_in_dim(head_weight, (y ^ x) * quarter, quarter, 1)
    part_a = lax.ppermute(slab, ("y", "c"), slab_pairs(0))
    part_b = lax.ppermute(slab, ("y", "c"), slab_pairs(1))
    outgoing = pack(embeddings, valid_mask)
    at_home = c == y // 2
    own = jnp.concatenate([jnp.where(at_home, part_a, part_b), jnp.where(at_home, part_b, part_a)])
    chain = [own, ring(own, "z", -1), ring(own, "z", 2), ring(own, "z", 1)]
    near = lax.all_to_all(outgoing, RESP_AXES, 0, 0, tiled=True).reshape(slots, 2 * quarter)
    below, above = [], []
    for piece in chain:
        below.append(ring(piece, "x", 1))
        above.append(ring(piece, "x", -1))
    across = [
        ring(below[0], "x", 1),
        ring(above[1], "x", -1),
        ring(above[2], "x", -1),
        ring(below[3], "x", 1),
    ]
    far = swap_cores(near)

    place = jnp.stack([x, z, c]).astype(jnp.int32)
    kept, given = score_parts(place, near, far, [*chain, *above, *across, *below])
    half_scores = (kept + swap_cores(given).astype(jnp.float32)).astype(jnp.bfloat16)
    returned = lax.all_to_all(half_scores, RESP_AXES, 0, 0, tiled=True)
    returned = returned.astype(jnp.float32).reshape(2, 2, 4, 2, block_rows // 2, slots)
    scores = (returned[:, 0] + returned[:, 1]).reshape(prompts, block_rows, slots)

    valid_rows = valid_mask.astype(jnp.float32)
    counts = jnp.sum((scores > HIDDEN_TEST).astype(jnp.float32), axis=2)
    preferences = jax.nn.sigmoid(scores) * valid_rows[:, :, None]
    totals = jnp.sum(preferences, axis=2) - 0.5 * valid_rows
    win_rates = valid_rows * totals / jnp.maximum(counts - 1.0, 1.0)
    return preferences, win_rates


def solution(mesh):
    mesh = Mesh(mesh.devices.reshape(4, 4, 4, 2), ("x", "y", "z", "c"))
    spec = P("x", RESP_AXES)
    return jax.shard_map(
        scored,
        mesh=mesh,
        in_specs=(P("x", RESP_AXES, None), P(RESP_AXES, None), spec),
        out_specs=(P("x", RESP_AXES, None), spec),
        check_vma=False,
    )
```

time: 258 us -> 203 us (0.79)
  blocking collectives: 0 us -> 55 us
  waiting for transfers between devices: 130 us -> 80.9 us
  local copies, waits for them, and re-layouts: 41.5 us -> 2.61 us
  Pallas kernels: 0 us -> 29.8 us
  matrix products: 29.7 us -> 0 us
  other arithmetic: 22.6 us -> 6.18 us
  starting transfers between devices: 32.1 us -> 27.2 us
    all_to_all x0 -> x1, blocking collectives: none -> 55 us  [scored(): lax.all_to_all(outgoing, RESP_AXES, 0, 0, tiled=True)]
    ppermute x6 -> x17, waiting for transfers between devices: 93.1 us -> 61.5 us  [the longest x15 54.9 us: ring(): return lax.ppermute(value, axis, [(i, (i + step) % 4) for i in range(4)])]
    pallas_call x0 -> x3, Pallas kernels: none -> 29.8 us  [the longest x1 14 us: score_parts(): pl.pallas_call(far_kernel, in_specs=[scalars, whole(), whole(), whole()]...]
    dot_general x4 -> x0, matrix products: 29.7 us -> none  [the longest x3 17.6 us: product(): lax.dot_general(weights[index], rows, (((1,), (1,)), ((), ())), preferred...]
    all_to_all x3 -> x1, waiting for transfers between devices: 35.7 us -> 16.9 us  [scored(): returned = lax.all_to_all(half_scores, RESP_AXES, 0, 0, tiled=True)]
    all_to_all x3 -> x1, starting transfers between devices: 19.5 us -> 4.09 us  [scored(): returned = lax.all_to_all(half_scores, RESP_AXES, 0, 0, tiled=True)]
    reshape x3 -> x0, local copies, waits for them, and re-layouts: 13.8 us -> none  [the longest x1 9.08 us: shards(): outgoing = outgoing.reshape(32, block_rows, 2 * quarter)]
    rev x1 -> x0, local copies, waits for them, and re-layouts: 13.3 us -> none  [shards(): outgoing = jnp.stack([grouped, grouped[..., ::-1, :]], axis=1)]
  transfers between devices with their start and end apart: 11 -> 20, of which waited for: 8 -> 14; matrix products, arithmetic and copies ran while one was open for 5% -> 0% of each run, Pallas kernels for 0% -> 5%
where the time goes in v2:
time: 203 us; the launch traced here: 202 us
  waiting for transfers between devices  80.9 us (40%)
  blocking collectives  55 us (27%)
  Pallas kernels  29.8 us (15%)
  starting transfers between devices  27.2 us (13%)
  other arithmetic  6.18 us (3%)
  local copies, waits for them, and re-layouts  2.61 us (1%)
    all_to_all x1, blocking collectives, scored(): lax.all_to_all(outgoing, RESP_AXES, 0, 0, tiled=True)  55 us
    ppermute x15, waiting for transfers between devices, ring(): return lax.ppermute(value, axis, [(i, (i + step) % 4) for i in range(4)])  54.9 us
    all_to_all x1, waiting for transfers between devices, scored(): returned = lax.all_to_all(half_scores, RESP_AXES, 0, 0, tiled=True)  16.9 us
    ppermute x15, starting transfers between devices, ring(): return lax.ppermute(value, axis, [(i, (i + step) % 4) for i in range(4)])  15.5 us
    pallas_call x1, Pallas kernels, score_parts(): pl.pallas_call(far_kernel, in_specs=[scalars, whole(), whole(), whole()]...  14 us
    pallas_call x1, Pallas kernels, score_parts(): pl.pallas_call(near_kernel, in_specs=[scalars, whole()] + [in_hbm()] * 16...  9.49 us
    pallas_call x1, Pallas kernels, pack(): pl.pallas_call(pack_kernel, grid=(prompts,), in_specs=[pl.BlockSpec((1, b...  6.3 us
    all_to_all x1, starting transfers between devices, scored(): returned = lax.all_to_all(half_scores, RESP_AXES, 0, 0, tiled=True)  4.09 us
  transfers between devices with their start and end apart: 20, of which 14 were waited for; matrix products, arithmetic and copies ran while one was open for 0% of the time, Pallas kernels for 5%

profile of v2, /device:TPU:1, one launch (start us, length us, event | category | flops | bytes accessed | tf_op | source)
XLA Modules:
  0.0 202.4 jit_solution(489166259322419761)
XLA Ops:
  0.6 1.5 copy.5.valid_ref
  2.2 6.3 %shard_map.50 = bf16[2,2,4,2,32,1792]{5,4,3,2,1,0:T(8,128)(2,1)} custom-call(bf16[8,32,3584]{2,1,0:T(8,128)(2,1)} %rows_ref.1, s32[8,32,1]{2,1,0:T(8,128)} %copy.5.valid_ref), custom_call_target="tpu_custom_call" | custom-call | tf_op jit(solution)/shard_map/pallas_call | solution.py:48
  8.5 55.0 %all_to_all.10 = bf16[32,32,1792]{2,1,0:T(8,128)(2,1)} all-to-all(bf16[32,32,1792]{2,1,0:T(8,128)(2,1)} %bitcast.10), channel_id=1, replica_groups=mesh['x'=4,'y'=4,'z'=4,'c'=2] {'y','z','c'}, dimensions={0} | all-to-all | bytes 7340032 | tf_op jit(solution)/shard_map/all_to_all | solution.py:193
  63.5 3.4 %collective-permute-start.1 = (bf16[112,896]{1,0:T(8,128)(2,1)S(1)}, bf16[112,896]{1,0:T(8,128)(2,1)S(1)}, u32[]{:S(2)}, u32[]{:S(2)}) collective-permute-start(bf16[112,896]{1,0:T(8,128)(2,1)S(1)} %constant_dynamic-slice_fusion), channel_id=1, source_target_pairs={{0,0},{1,16},{8,8},{9,24},{16,17},{17,1},{24,25},{25,9},{2,2},{3,1... | collective-permute-start | bytes 602120 | tf_op jit(solution)/shard_map/ppermute | solution.py:187
  66.9 1.9 collective-permute-start.2
  68.9 2.6 %collective-permute-done.1 = bf16[112,896]{1,0:T(8,128)(2,1)S(1)} collective-permute-done((bf16[112,896]{1,0:T(8,128)(2,1)S(1)}, bf16[112,896]{1,0:T(8,128)(2,1)S(1)}, u32[]{:S(2)}, u32[]{:S(2)}) %collective-permute-start.1) | collective-permute-done | bytes 200736 | tf_op jit(solution)/shard_map/ppermute | solution.py:187
  71.5 4.0 %collective-permute-done.2 = bf16[112,896]{1,0:T(8,128)(2,1)S(1)} collective-permute-done((bf16[112,896]{1,0:T(8,128)(2,1)S(1)}, bf16[112,896]{1,0:T(8,128)(2,1)S(1)}, u32[]{:S(2)}, u32[]{:S(2)}) %collective-permute-start.2) | collective-permute-done | bytes 200736 | tf_op jit(solution)/shard_map/ppermute | solution.py:188
  76.1 1.7 collective-permute-start.4
  77.7 1.2 collective-permute-start.10
  78.9 8.0 %collective-permute-done.3.refs_1_ = bf16[224,896]{1,0:T(8,128)(2,1)S(1)} collective-permute-done((bf16[224,896]{1,0:T(8,128)(2,1)S(1)}, bf16[224,896]{1,0:T(8,128)(2,1)S(1)}, u32[]{:S(2)}, u32[]{:S(2)}) %collective-permute-start.3) | collective-permute-done | bytes 401440 | tf_op jit(solution)/shard_map/ppermute | solution.py:17
  87.0 2.5 %collective-permute-start.6 = (bf16[224,896]{1,0:T(8,128)(2,1)S(1)}, bf16[224,896]{1,0:T(8,128)(2,1)S(1)}, u32[]{:S(2)}, u32[]{:S(2)}) collective-permute-start(bf16[224,896]{1,0:T(8,128)(2,1)S(1)} %pad_maximum_fusion.refs_0_), channel_id=1, source_target_pairs={{0,96},{32,0},{64,32},{96,64},{1,97},{33,1},{65,33},{97,65},{2,98}... | collective-permute-start | bytes 1204232 | tf_op jit(solution)/shard_map/ppermute | solution.py:17
  89.4 1.7 collective-permute-start.7
  91.1 4.4 %collective-permute-done.5.refs_3_ = bf16[224,896]{1,0:T(8,128)(2,1)S(1)} collective-permute-done((bf16[224,896]{1,0:T(8,128)(2,1)S(1)}, bf16[224,896]{1,0:T(8,128)(2,1)S(1)}, u32[]{:S(2)}, u32[]{:S(2)}) %collective-permute-start.5) | collective-permute-done | bytes 401440 | tf_op jit(solution)/shard_map/ppermute | solution.py:17
  95.5 2.7 %collective-permute-start.8 = (bf16[224,896]{1,0:T(8,128)(2,1)S(1)}, bf16[224,896]{1,0:T(8,128)(2,1)}, u32[]{:S(2)}, u32[]{:S(2)}) collective-permute-start(bf16[224,896]{1,0:T(8,128)(2,1)S(1)} %collective-permute-done.4.refs_2_), channel_id=1, source_target_pairs={{0,96},{32,0},{64,32},{96,64},{1,97},{33,1},{65,33},{97,65},{2,98}... | collective-permute-start | bytes 1204232 | tf_op jit(solution)/shard_map/ppermute | solution.py:17
  98.5 1.0 collective-permute-start.11
  99.6 7.3 %collective-permute-done.7.refs_5_ = bf16[224,896]{1,0:T(8,128)(2,1)} collective-permute-done((bf16[224,896]{1,0:T(8,128)(2,1)S(1)}, bf16[224,896]{1,0:T(8,128)(2,1)}, u32[]{:S(2)}, u32[]{:S(2)}) %collective-permute-start.7) | collective-permute-done | bytes 401440 | tf_op jit(solution)/shard_map/ppermute | solution.py:17
  106.9 1.0 collective-permute-start.16
  107.9 3.8 %collective-permute-done.8.refs_6_ = bf16[224,896]{1,0:T(8,128)(2,1)} collective-permute-done((bf16[224,896]{1,0:T(8,128)(2,1)S(1)}, bf16[224,896]{1,0:T(8,128)(2,1)}, u32[]{:S(2)}, u32[]{:S(2)}) %collective-permute-start.8) | collective-permute-done | bytes 401440 | tf_op jit(solution)/shard_map/ppermute | solution.py:17
  112.6 2.3 %collective-permute-start.9 = (bf16[224,896]{1,0:T(8,128)(2,1)S(1)}, bf16[224,896]{1,0:T(8,128)(2,1)}, u32[]{:S(2)}, u32[]{:S(2)}) collective-permute-start(bf16[224,896]{1,0:T(8,128)(2,1)S(1)} %collective-permute-done.5.refs_3_), channel_id=1, source_target_pairs={{0,96},{32,0},{64,32},{96,64},{1,97},{33,1},{65,33},{97,65},{2,98}... | collective-permute-start | bytes 1204232 | tf_op jit(solution)/shard_map/ppermute | solution.py:17
  114.9 3.4 %collective-permute-done.11.refs_8_ = bf16[224,896]{1,0:T(8,128)(2,1)S(1)} collective-permute-done((bf16[224,896]{1,0:T(8,128)(2,1)S(1)}, bf16[224,896]{1,0:T(8,128)(2,1)S(1)}, u32[]{:S(2)}, u32[]{:S(2)}) %collective-permute-start.11) | collective-permute-done | bytes 401440 | tf_op jit(solution)/shard_map/ppermute | solution.py:17
  118.4 8.6 %collective-permute-done.16.refs_13_ = bf16[224,896]{1,0:T(8,128)(2,1)S(1)} collective-permute-done((bf16[224,896]{1,0:T(8,128)(2,1)S(1)}, bf16[224,896]{1,0:T(8,128)(2,1)S(1)}, u32[]{:S(2)}, u32[]{:S(2)}) %collective-permute-start.16) | collective-permute-done | bytes 401440 | tf_op jit(solution)/shard_map/ppermute | solution.py:17
  127.0 8.6 %collective-permute-done.17.refs_14_ = bf16[224,896]{1,0:T(8,128)(2,1)S(1)} collective-permute-done((bf16[224,896]{1,0:T(8,128)(2,1)S(1)}, bf16[224,896]{1,0:T(8,128)(2,1)S(1)}, u32[]{:S(2)}, u32[]{:S(2)}) %collective-permute-start.17) | collective-permute-done | bytes 401440 | tf_op jit(solution)/shard_map/ppermute | solution.py:17
  137.0 4.1 %collective-permute-done.13.refs_10_ = bf16[224,896]{1,0:T(8,128)(2,1)} collective-permute-done((bf16[224,896]{1,0:T(8,128)(2,1)}, bf16[224,896]{1,0:T(8,128)(2,1)}, u32[]{:S(2)}, u32[]{:S(2)}) %collective-permute-start.13) | collective-permute-done | bytes 401440 | tf_op jit(solution)/shard_map/ppermute | solution.py:17
  141.1 6.3 %collective-permute-done.15.refs_11_ = bf16[224,896]{1,0:T(8,128)(2,1)} collective-permute-done((bf16[224,896]{1,0:T(8,128)(2,1)}, bf16[224,896]{1,0:T(8,128)(2,1)}, u32[]{:S(2)}, u32[]{:S(2)}) %collective-permute-start.15) | collective-permute-done | bytes 401440 | tf_op jit(solution)/shard_map/ppermute | solution.py:17
  147.4 9.5 %shard_map.51.mixed_ref = f32[896,1024]{1,0:T(8,128)} custom-call(s32[3]{0:T(128)} %pad_add_fusion.place_ref, bf16[1024,1792]{1,0:T(8,128)(2,1)} %bitcast.5.near_ref, bf16[224,896]{1,0:T(8,128)(2,1)} %copy-done.1, bf16[224,896]{1,0:T(8,128)(2,1)} %copy-done.2, bf16[224,896]{1,0:T(8,128)(2,1)} %copy-done.3, bf16[224,896]{1,0:T(8,128)(2,1)} %copy-done.4, ...), custom_call_target="tpu_custom_call" | custom-call | flops 3288334336 | bytes 12582912 | tf_op jit(solution)/shard_map/pallas_call | solution.py:144
  157.0 14.0 %shard_map.52 = (f32[32,16,1024]{2,1,0:T(8,128)}, bf16[32,16,1024]{2,1,0:T(8,128)(2,1)}) custom-call(s32[3]{0:T(128)} %pad_add_fusion.place_ref, bf16[1024,1792]{1,0:T(8,128)(2,1)} %bitcast.5.near_ref, bf16[1024,1792]{1,0:T(8,128)(2,1)} %collective-permute-done.far_ref, f32[896,1024]{1,0:T(8,128)} %shard_map.51.mixed_ref, bf16[224,896]{1,0:T(8,128)(2,1)} %copy-done.1, ...), custom_call_target="tpu_custom_call" | custom-call | flops 5167382528 | bytes 16777216 | tf_op jit(solution)/shard_map/pallas_call | solution.py:156
  171.0 2.3 %collective-permute-start.18 = (bf16[32,16,1024]{2,1,0:T(8,128)(2,1)}, bf16[32,16,1024]{2,1,0:T(8,128)(2,1)S(1)}, u32[]{:S(2)}, u32[]{:S(2)}) collective-permute-start(bf16[32,16,1024]{2,1,0:T(8,128)(2,1)} %get-tuple-element.5), channel_id=1, source_target_pairs={{0,1},{1,0},{2,3},{3,2},{4,5},{5,4},{6,7},{7,6},{8,9},{9,8},{10,11... | collective-permute-start | bytes 3145736 | tf_op jit(solution)/shard_map/ppermute | solution.py:21
  173.2 2.5 %collective-permute-done.18 = bf16[32,16,1024]{2,1,0:T(8,128)(2,1)S(1)} collective-permute-done((bf16[32,16,1024]{2,1,0:T(8,128)(2,1)}, bf16[32,16,1024]{2,1,0:T(8,128)(2,1)S(1)}, u32[]{:S(2)}, u32[]{:S(2)}) %collective-permute-start.18) | collective-permute-done | bytes 1048608 | tf_op jit(solution)/shard_map/ppermute | solution.py:21
  175.7 2.9 %add_convert_fusion = bf16[32,16,1024]{2,1,0:T(8,128)(2,1)} fusion(f32[32,16,1024]{2,1,0:T(8,128)} %get-tuple-element.4, bf16[32,16,1024]{2,1,0:T(8,128)(2,1)S(1)} %collective-permute-done.18), kind=kLoop, calls=%fused_computation | loop fusion | flops 1572864 | bytes 4194304 | tf_op jit(solution)/shard_map/convert_element_type | solution.py:208
  178.7 4.1 %all-to-all-start.1 = ((bf16[32,16,1024]{2,1,0:T(8,128)(2,1)}), bf16[32,16,1024]{2,1,0:T(8,128)(2,1)S(1)}, u32[]{:S(2)}, u32[]{:S(2)}) async-start(bf16[32,16,1024]{2,1,0:T(8,128)(2,1)} %add_convert_fusion), calls=%async_computation.1 | async-start | bytes 2097152 | tf_op jit(solution)/shard_map/all_to_all | solution.py:209
  182.9 16.9 %all-to-all-done.1 = bf16[32,16,1024]{2,1,0:T(8,128)(2,1)S(1)} async-done(((bf16[32,16,1024]{2,1,0:T(8,128)(2,1)}), bf16[32,16,1024]{2,1,0:T(8,128)(2,1)S(1)}, u32[]{:S(2)}, u32[]{:S(2)}) %all-to-all-start.1) | async-done | bytes 1048608 | tf_op jit(solution)/shard_map/all_to_all | solution.py:209
  200.7 1.1 broadcast_multiply_fusion
  (49 shorter events, 5.0 us)
Async XLA Ops:
  0.6 62.9 %copy-start = (bf16[112,3584]{1,0:T(8,128)(2,1)S(1)}, bf16[112,3584]{1,0:T(8,128)(2,1)}, u32[]{:S(2)}) copy-start(bf16[112,3584]{1,0:T(8,128)(2,1)} %param.4) | copy-start | bytes 2408452
  63.5 93.5 %collective-permute-start = (bf16[1024,1792]{1,0:T(8,128)(2,1)}, bf16[1024,1792]{1,0:T(8,128)(2,1)}, u32[]{:S(2)}, u32[]{:S(2)}) collective-permute-start(bf16[1024,1792]{1,0:T(8,128)(2,1)} %bitcast.5.near_ref), channel_id=1, source_target_pairs={{0,1},{1,0},{2,3},{3,2},{4,5},{5,4},{6,7},{7,6},{8,9},{9,8},{10,11... | collective-permute-start | bytes 11010056 | tf_op jit(solution)/shard_map/ppermute | solution.py:21
  63.5 8.0 %collective-permute-start.1 = (bf16[112,896]{1,0:T(8,128)(2,1)S(1)}, bf16[112,896]{1,0:T(8,128)(2,1)S(1)}, u32[]{:S(2)}, u32[]{:S(2)}) collective-permute-start(bf16[112,896]{1,0:T(8,128)(2,1)S(1)} %constant_dynamic-slice_fusion), channel_id=1, source_target_pairs={{0,0},{1,16},{8,8},{9,24},{16,17},{17,1},{24,25},{25,9},{2,2},{3,1... | collective-permute-start | bytes 602120 | tf_op jit(solution)/shard_map/ppermute | solution.py:187
  66.9 8.5 %collective-permute-start.2 = (bf16[112,896]{1,0:T(8,128)(2,1)S(1)}, bf16[112,896]{1,0:T(8,128)(2,1)S(1)}, u32[]{:S(2)}, u32[]{:S(2)}) collective-permute-start(bf16[112,896]{1,0:T(8,128)(2,1)S(1)} %constant_dynamic-slice_fusion), channel_id=1, source_target_pairs={{0,16},{1,0},{8,24},{9,8},{16,1},{17,17},{24,9},{25,25},{2,18},{3,... | collective-permute-start | bytes 602120 | tf_op jit(solution)/shard_map/ppermute | solution.py:188
  75.6 71.8 %copy-start.1 = (bf16[224,896]{1,0:T(8,128)(2,1)}, bf16[224,896]{1,0:T(8,128)(2,1)S(1)}, u32[]{:S(2)}) copy-start(bf16[224,896]{1,0:T(8,128)(2,1)S(1)} %pad_maximum_fusion.refs_0_) | copy-start | bytes 1204228
  75.6 11.4 %collective-permute-start.3 = (bf16[224,896]{1,0:T(8,128)(2,1)S(1)}, bf16[224,896]{1,0:T(8,128)(2,1)S(1)}, u32[]{:S(2)}, u32[]{:S(2)}) collective-permute-start(bf16[224,896]{1,0:T(8,128)(2,1)S(1)} %pad_maximum_fusion.refs_0_), channel_id=1, source_target_pairs={{0,6},{2,0},{4,2},{6,4},{1,7},{3,1},{5,3},{7,5},{8,14},{10,8},{12,... | collective-permute-start | bytes 1204232 | tf_op jit(solution)/shard_map/ppermute | solution.py:17
  76.1 13.4 %collective-permute-start.4 = (bf16[224,896]{1,0:T(8,128)(2,1)S(1)}, bf16[224,896]{1,0:T(8,128)(2,1)S(1)}, u32[]{:S(2)}, u32[]{:S(2)}) collective-permute-start(bf16[224,896]{1,0:T(8,128)(2,1)S(1)} %pad_maximum_fusion.refs_0_), channel_id=1, source_target_pairs={{0,4},{2,6},{4,0},{6,2},{1,5},{3,7},{5,1},{7,3},{8,12},{10,14},{12... | collective-permute-start | bytes 1204232 | tf_op jit(solution)/shard_map/ppermute | solution.py:17
  77.7 17.8 %collective-permute-start.5 = (bf16[224,896]{1,0:T(8,128)(2,1)S(1)}, bf16[224,896]{1,0:T(8,128)(2,1)S(1)}, u32[]{:S(2)}, u32[]{:S(2)}) collective-permute-start(bf16[224,896]{1,0:T(8,128)(2,1)S(1)} %pad_maximum_fusion.refs_0_), channel_id=1, source_target_pairs={{0,2},{2,4},{4,6},{6,0},{1,3},{3,5},{5,7},{7,1},{8,10},{10,12},{12... | collective-permute-start | bytes 1204232 | tf_op jit(solution)/shard_map/ppermute | solution.py:17
  77.7 20.4 %collective-permute-start.10 = (bf16[224,896]{1,0:T(8,128)(2,1)S(1)}, bf16[224,896]{1,0:T(8,128)(2,1)S(1)}, u32[]{:S(2)}, u32[]{:S(2)}) collective-permute-start(bf16[224,896]{1,0:T(8,128)(2,1)S(1)} %pad_maximum_fusion.refs_0_), channel_id=1, source_target_pairs={{0,32},{32,64},{64,96},{96,0},{1,33},{33,65},{65,97},{97,1},{2,34}... | collective-permute-start | bytes 1204232 | tf_op jit(solution)/shard_map/ppermute | solution.py:17
  87.0 60.4 %copy-start.2 = (bf16[224,896]{1,0:T(8,128)(2,1)}, bf16[224,896]{1,0:T(8,128)(2,1)S(1)}, u32[]{:S(2)}) copy-start(bf16[224,896]{1,0:T(8,128)(2,1)S(1)} %collective-permute-done.3.refs_1_) | copy-start | bytes 1204228
  87.0 11.6 %collective-permute-start.6 = (bf16[224,896]{1,0:T(8,128)(2,1)S(1)}, bf16[224,896]{1,0:T(8,128)(2,1)S(1)}, u32[]{:S(2)}, u32[]{:S(2)}) collective-permute-start(bf16[224,896]{1,0:T(8,128)(2,1)S(1)} %pad_maximum_fusion.refs_0_), channel_id=1, source_target_pairs={{0,96},{32,0},{64,32},{96,64},{1,97},{33,1},{65,33},{97,65},{2,98}... | collective-permute-start | bytes 1204232 | tf_op jit(solution)/shard_map/ppermute | solution.py:17
  89.4 58.0 %copy-start.3 = (bf16[224,896]{1,0:T(8,128)(2,1)}, bf16[224,896]{1,0:T(8,128)(2,1)S(1)}, u32[]{:S(2)}) copy-start(bf16[224,896]{1,0:T(8,128)(2,1)S(1)} %collective-permute-done.4.refs_2_) | copy-start | bytes 1204228
  89.4 17.4 %collective-permute-start.7 = (bf16[224,896]{1,0:T(8,128)(2,1)S(1)}, bf16[224,896]{1,0:T(8,128)(2,1)}, u32[]{:S(2)}, u32[]{:S(2)}) collective-permute-start(bf16[224,896]{1,0:T(8,128)(2,1)S(1)} %collective-permute-done.3.refs_1_), channel_id=1, source_target_pairs={{0,96},{32,0},{64,32},{96,64},{1,97},{33,1},{65,33},{97,65},{2,98}... | collective-permute-start | bytes 1204232 | tf_op jit(solution)/shard_map/ppermute | solution.py:17
  95.5 51.9 %copy-start.4 = (bf16[224,896]{1,0:T(8,128)(2,1)}, bf16[224,896]{1,0:T(8,128)(2,1)S(1)}, u32[]{:S(2)}) copy-start(bf16[224,896]{1,0:T(8,128)(2,1)S(1)} %collective-permute-done.5.refs_3_) | copy-start | bytes 1204228
  95.5 16.2 %collective-permute-start.8 = (bf16[224,896]{1,0:T(8,128)(2,1)S(1)}, bf16[224,896]{1,0:T(8,128)(2,1)}, u32[]{:S(2)}, u32[]{:S(2)}) collective-permute-start(bf16[224,896]{1,0:T(8,128)(2,1)S(1)} %collective-permute-done.4.refs_2_), channel_id=1, source_target_pairs={{0,96},{32,0},{64,32},{96,64},{1,97},{33,1},{65,33},{97,65},{2,98}... | collective-permute-start | bytes 1204232 | tf_op jit(solution)/shard_map/ppermute | solution.py:17
  98.2 49.2 %copy-start.5 = (bf16[224,896]{1,0:T(8,128)(2,1)}, bf16[224,896]{1,0:T(8,128)(2,1)S(1)}, u32[]{:S(2)}) copy-start(bf16[224,896]{1,0:T(8,128)(2,1)S(1)} %collective-permute-done.10.refs_12_) | copy-start | bytes 1204228
  98.2 14.5 %collective-permute-start.14 = (bf16[224,896]{1,0:T(8,128)(2,1)S(1)}, bf16[224,896]{1,0:T(8,128)(2,1)}, u32[]{:S(2)}, u32[]{:S(2)}) collective-permute-start(bf16[224,896]{1,0:T(8,128)(2,1)S(1)} %collective-permute-done.5.refs_3_), channel_id=1, source_target_pairs={{0,32},{32,64},{64,96},{96,0},{1,33},{33,65},{65,97},{97,1},{2,34}... | collective-permute-start | bytes 1204232 | tf_op jit(solution)/shard_map/ppermute | solution.py:17
  98.5 48.9 %copy-start.6 = (bf16[224,896]{1,0:T(8,128)(2,1)}, bf16[224,896]{1,0:T(8,128)(2,1)S(1)}, u32[]{:S(2)}) copy-start(bf16[224,896]{1,0:T(8,128)(2,1)S(1)} %collective-permute-done.6.refs_4_) | copy-start | bytes 1204228
  98.5 19.8 %collective-permute-start.11 = (bf16[224,896]{1,0:T(8,128)(2,1)S(1)}, bf16[224,896]{1,0:T(8,128)(2,1)S(1)}, u32[]{:S(2)}, u32[]{:S(2)}) collective-permute-start(bf16[224,896]{1,0:T(8,128)(2,1)S(1)} %collective-permute-done.10.refs_12_), channel_id=1, source_target_pairs={{0,32},{32,64},{64,96},{96,0},{1,33},{33,65},{65,97},{97,1},{2,34}... | collective-permute-start | bytes 1204232 | tf_op jit(solution)/shard_map/ppermute | solution.py:17
  106.9 20.1 %collective-permute-start.16 = (bf16[224,896]{1,0:T(8,128)(2,1)S(1)}, bf16[224,896]{1,0:T(8,128)(2,1)S(1)}, u32[]{:S(2)}, u32[]{:S(2)}) collective-permute-start(bf16[224,896]{1,0:T(8,128)(2,1)S(1)} %collective-permute-done.3.refs_1_), channel_id=1, source_target_pairs={{0,32},{32,64},{64,96},{96,0},{1,33},{33,65},{65,97},{97,1},{2,34}... | collective-permute-start | bytes 1204232 | tf_op jit(solution)/shard_map/ppermute | solution.py:17
  111.7 23.9 %collective-permute-start.17 = (bf16[224,896]{1,0:T(8,128)(2,1)S(1)}, bf16[224,896]{1,0:T(8,128)(2,1)S(1)}, u32[]{:S(2)}, u32[]{:S(2)}) collective-permute-start(bf16[224,896]{1,0:T(8,128)(2,1)S(1)} %collective-permute-done.4.refs_2_), channel_id=1, source_target_pairs={{0,32},{32,64},{64,96},{96,0},{1,33},{33,65},{65,97},{97,1},{2,34}... | collective-permute-start | bytes 1204232 | tf_op jit(solution)/shard_map/ppermute | solution.py:17
  112.6 24.4 %collective-permute-start.9 = (bf16[224,896]{1,0:T(8,128)(2,1)S(1)}, bf16[224,896]{1,0:T(8,128)(2,1)}, u32[]{:S(2)}, u32[]{:S(2)}) collective-permute-start(bf16[224,896]{1,0:T(8,128)(2,1)S(1)} %collective-permute-done.5.refs_3_), channel_id=1, source_target_pairs={{0,96},{32,0},{64,32},{96,64},{1,97},{33,1},{65,33},{97,65},{2,98}... | collective-permute-start | bytes 1204232 | tf_op jit(solution)/shard_map/ppermute | solution.py:17
  118.4 17.2 %copy-start.7 = (bf16[224,896]{1,0:T(8,128)(2,1)}, bf16[224,896]{1,0:T(8,128)(2,1)S(1)}, u32[]{:S(2)}) copy-start(bf16[224,896]{1,0:T(8,128)(2,1)S(1)} %collective-permute-done.11.refs_8_) | copy-start | bytes 1204228
  118.4 18.6 %collective-permute-start.12 = (bf16[224,896]{1,0:T(8,128)(2,1)}, bf16[224,896]{1,0:T(8,128)(2,1)}, u32[]{:S(2)}, u32[]{:S(2)}) collective-permute-start(bf16[224,896]{1,0:T(8,128)(2,1)} %collective-permute-done.7.refs_5_), channel_id=1, source_target_pairs={{0,96},{32,0},{64,32},{96,64},{1,97},{33,1},{65,33},{97,65},{2,98}... | collective-permute-start | bytes 1204232 | tf_op jit(solution)/shard_map/ppermute | solution.py:17
  127.0 8.6 %copy-start.8 = (bf16[224,896]{1,0:T(8,128)(2,1)}, bf16[224,896]{1,0:T(8,128)(2,1)S(1)}, u32[]{:S(2)}) copy-start(bf16[224,896]{1,0:T(8,128)(2,1)S(1)} %collective-permute-done.16.refs_13_) | copy-start | bytes 1204228
  127.0 14.1 %collective-permute-start.13 = (bf16[224,896]{1,0:T(8,128)(2,1)}, bf16[224,896]{1,0:T(8,128)(2,1)}, u32[]{:S(2)}, u32[]{:S(2)}) collective-permute-start(bf16[224,896]{1,0:T(8,128)(2,1)} %collective-permute-done.8.refs_6_), channel_id=1, source_target_pairs={{0,96},{32,0},{64,32},{96,64},{1,97},{33,1},{65,33},{97,65},{2,98}... | collective-permute-start | bytes 1204232 | tf_op jit(solution)/shard_map/ppermute | solution.py:17
  135.6 0.8 copy-start.9
  136.3 11.0 %collective-permute-start.15 = (bf16[224,896]{1,0:T(8,128)(2,1)}, bf16[224,896]{1,0:T(8,128)(2,1)}, u32[]{:S(2)}, u32[]{:S(2)}) collective-permute-start(bf16[224,896]{1,0:T(8,128)(2,1)} %collective-permute-done.14.refs_15_), channel_id=1, source_target_pairs={{0,32},{32,64},{64,96},{96,0},{1,33},{33,65},{65,97},{97,1},{2,34}... | collective-permute-start | bytes 1204232 | tf_op jit(solution)/shard_map/ppermute | solution.py:17
  171.0 4.8 %collective-permute-start.18 = (bf16[32,16,1024]{2,1,0:T(8,128)(2,1)}, bf16[32,16,1024]{2,1,0:T(8,128)(2,1)S(1)}, u32[]{:S(2)}, u32[]{:S(2)}) collective-permute-start(bf16[32,16,1024]{2,1,0:T(8,128)(2,1)} %get-tuple-element.5), channel_id=1, source_target_pairs={{0,1},{1,0},{2,3},{3,2},{4,5},{5,4},{6,7},{7,6},{8,9},{9,8},{10,11... | collective-permute-start | bytes 3145736 | tf_op jit(solution)/shard_map/ppermute | solution.py:21
  178.7 4.1 %copy-start.10 = (s32[8,32]{1,0:T(8,128)S(1)}, s32[8,32]{1,0:T(8,128)}, u32[]{:S(2)}) copy-start(s32[8,32]{1,0:T(8,128)} %param.5) | copy-start | bytes 3076
  178.7 21.1 %all-to-all-start.1 = ((bf16[32,16,1024]{2,1,0:T(8,128)(2,1)}), bf16[32,16,1024]{2,1,0:T(8,128)(2,1)S(1)}, u32[]{:S(2)}, u32[]{:S(2)}) async-start(bf16[32,16,1024]{2,1,0:T(8,128)(2,1)} %add_convert_fusion), calls=%async_computation.1 | async-start | bytes 2097152 | tf_op jit(solution)/shard_map/all_to_all | solution.py:209

commit v3 on v2

--- a/solution.py
+++ b/solution.py
@@ -195,12 +195,9 @@
     for piece in chain:
         below.append(ring(piece, "x", 1))
         above.append(ring(piece, "x", -1))
-    across = [
-        ring(below[0], "x", 1),
-        ring(above[1], "x", -1),
-        ring(above[2], "x", -1),
-        ring(below[3], "x", 1),
-    ]
+    across = []
+    for index, step in enumerate((1, -1, -1, 1)):
+        across.append(ring((below if step == 1 else above)[index], "x", step))
     far = swap_cores(near)
 
     place = jnp.stack([x, z, c]).astype(jnp.int32)

time: 203 us -> 203 us (level)
  no operation moved by 1% of the time
where the time goes in v3:
time: 203 us; the launch traced here: 202 us
  waiting for transfers between devices  80.9 us (40%)
  blocking collectives  55 us (27%)
  Pallas kernels  29.8 us (15%)
  starting transfers between devices  27.2 us (13%)
  other arithmetic  6.18 us (3%)
  local copies, waits for them, and re-layouts  2.61 us (1%)
    all_to_all x1, blocking collectives, scored(): lax.all_to_all(outgoing, RESP_AXES, 0, 0, tiled=True)  55 us
    ppermute x15, waiting for transfers between devices, ring(): return lax.ppermute(value, axis, [(i, (i + step) % 4) for i in range(4)])  54.9 us
    all_to_all x1, waiting for transfers between devices, scored(): returned = lax.all_to_all(half_scores, RESP_AXES, 0, 0, tiled=True)  16.9 us
    ppermute x15, starting transfers between devices, ring(): return lax.ppermute(value, axis, [(i, (i + step) % 4) for i in range(4)])  15.5 us
    pallas_call x1, Pallas kernels, score_parts(): pl.pallas_call(far_kernel, in_specs=[scalars, whole(), whole(), whole()]...  14 us
    pallas_call x1, Pallas kernels, score_parts(): pl.pallas_call(near_kernel, in_specs=[scalars, whole()] + [in_hbm()] * 16...  9.49 us
    pallas_call x1, Pallas kernels, pack(): pl.pallas_call(pack_kernel, grid=(prompts,), in_specs=[pl.BlockSpec((1, b...  6.3 us
    all_to_all x1, starting transfers between devices, scored(): returned = lax.all_to_all(half_scores, RESP_AXES, 0, 0, tiled=True)  4.09 us
  transfers between devices with their start and end apart: 20, of which 14 were waited for; matrix products, arithmetic and copies ran while one was open for 0% of the time, Pallas kernels for 5%

profile of v3, /device:TPU:1, one launch (start us, length us, event | category | flops | bytes accessed | tf_op | source)
XLA Modules:
  0.0 202.4 jit_solution(489166259322419761)
XLA Ops:
  0.6 1.5 copy.5.valid_ref
  2.2 6.3 %shard_map.50 = bf16[2,2,4,2,32,1792]{5,4,3,2,1,0:T(8,128)(2,1)} custom-call(bf16[8,32,3584]{2,1,0:T(8,128)(2,1)} %rows_ref.1, s32[8,32,1]{2,1,0:T(8,128)} %copy.5.valid_ref), custom_call_target="tpu_custom_call" | custom-call | tf_op jit(solution)/shard_map/pallas_call | solution.py:48
  8.5 55.0 %all_to_all.10 = bf16[32,32,1792]{2,1,0:T(8,128)(2,1)} all-to-all(bf16[32,32,1792]{2,1,0:T(8,128)(2,1)} %bitcast.10), channel_id=1, replica_groups=mesh['x'=4,'y'=4,'z'=4,'c'=2] {'y','z','c'}, dimensions={0} | all-to-all | bytes 7340032 | tf_op jit(solution)/shard_map/all_to_all | solution.py:193
  63.5 3.4 %collective-permute-start.1 = (bf16[112,896]{1,0:T(8,128)(2,1)S(1)}, bf16[112,896]{1,0:T(8,128)(2,1)S(1)}, u32[]{:S(2)}, u32[]{:S(2)}) collective-permute-start(bf16[112,896]{1,0:T(8,128)(2,1)S(1)} %constant_dynamic-slice_fusion), channel_id=1, source_target_pairs={{0,0},{1,16},{8,8},{9,24},{16,17},{17,1},{24,25},{25,9},{2,2},{3,1... | collective-permute-start | bytes 602120 | tf_op jit(solution)/shard_map/ppermute | solution.py:187
  66.9 1.9 collective-permute-start.2
  68.9 2.6 %collective-permute-done.1 = bf16[112,896]{1,0:T(8,128)(2,1)S(1)} collective-permute-done((bf16[112,896]{1,0:T(8,128)(2,1)S(1)}, bf16[112,896]{1,0:T(8,128)(2,1)S(1)}, u32[]{:S(2)}, u32[]{:S(2)}) %collective-permute-start.1) | collective-permute-done | bytes 200736 | tf_op jit(solution)/shard_map/ppermute | solution.py:187
  71.5 4.0 %collective-permute-done.2 = bf16[112,896]{1,0:T(8,128)(2,1)S(1)} collective-permute-done((bf16[112,896]{1,0:T(8,128)(2,1)S(1)}, bf16[112,896]{1,0:T(8,128)(2,1)S(1)}, u32[]{:S(2)}, u32[]{:S(2)}) %collective-permute-start.2) | collective-permute-done | bytes 200736 | tf_op jit(solution)/shard_map/ppermute | solution.py:188
  76.1 1.7 collective-permute-start.4
  77.7 1.2 collective-permute-start.10
  78.9 8.0 %collective-permute-done.3.refs_1_ = bf16[224,896]{1,0:T(8,128)(2,1)S(1)} collective-permute-done((bf16[224,896]{1,0:T(8,128)(2,1)S(1)}, bf16[224,896]{1,0:T(8,128)(2,1)S(1)}, u32[]{:S(2)}, u32[]{:S(2)}) %collective-permute-start.3) | collective-permute-done | bytes 401440 | tf_op jit(solution)/shard_map/ppermute | solution.py:17
  87.0 2.5 %collective-permute-start.6 = (bf16[224,896]{1,0:T(8,128)(2,1)S(1)}, bf16[224,896]{1,0:T(8,128)(2,1)S(1)}, u32[]{:S(2)}, u32[]{:S(2)}) collective-permute-start(bf16[224,896]{1,0:T(8,128)(2,1)S(1)} %pad_maximum_fusion.refs_0_), channel_id=1, source_target_pairs={{0,96},{32,0},{64,32},{96,64},{1,97},{33,1},{65,33},{97,65},{2,98}... | collective-permute-start | bytes 1204232 | tf_op jit(solution)/shard_map/ppermute | solution.py:17
  89.4 1.7 collective-permute-start.7
  91.1 4.4 %collective-permute-done.5.refs_3_ = bf16[224,896]{1,0:T(8,128)(2,1)S(1)} collective-permute-done((bf16[224,896]{1,0:T(8,128)(2,1)S(1)}, bf16[224,896]{1,0:T(8,128)(2,1)S(1)}, u32[]{:S(2)}, u32[]{:S(2)}) %collective-permute-start.5) | collective-permute-done | bytes 401440 | tf_op jit(solution)/shard_map/ppermute | solution.py:17
  95.5 2.7 %collective-permute-start.8 = (bf16[224,896]{1,0:T(8,128)(2,1)S(1)}, bf16[224,896]{1,0:T(8,128)(2,1)}, u32[]{:S(2)}, u32[]{:S(2)}) collective-permute-start(bf16[224,896]{1,0:T(8,128)(2,1)S(1)} %collective-permute-done.4.refs_2_), channel_id=1, source_target_pairs={{0,96},{32,0},{64,32},{96,64},{1,97},{33,1},{65,33},{97,65},{2,98}... | collective-permute-start | bytes 1204232 | tf_op jit(solution)/shard_map/ppermute | solution.py:17
  98.5 1.0 collective-permute-start.11
  99.6 7.3 %collective-permute-done.7.refs_5_ = bf16[224,896]{1,0:T(8,128)(2,1)} collective-permute-done((bf16[224,896]{1,0:T(8,128)(2,1)S(1)}, bf16[224,896]{1,0:T(8,128)(2,1)}, u32[]{:S(2)}, u32[]{:S(2)}) %collective-permute-start.7) | collective-permute-done | bytes 401440 | tf_op jit(solution)/shard_map/ppermute | solution.py:17
  106.9 1.0 collective-permute-start.16
  107.9 3.8 %collective-permute-done.8.refs_6_ = bf16[224,896]{1,0:T(8,128)(2,1)} collective-permute-done((bf16[224,896]{1,0:T(8,128)(2,1)S(1)}, bf16[224,896]{1,0:T(8,128)(2,1)}, u32[]{:S(2)}, u32[]{:S(2)}) %collective-permute-start.8) | collective-permute-done | bytes 401440 | tf_op jit(solution)/shard_map/ppermute | solution.py:17
  112.6 2.3 %collective-permute-start.9 = (bf16[224,896]{1,0:T(8,128)(2,1)S(1)}, bf16[224,896]{1,0:T(8,128)(2,1)}, u32[]{:S(2)}, u32[]{:S(2)}) collective-permute-start(bf16[224,896]{1,0:T(8,128)(2,1)S(1)} %collective-permute-done.5.refs_3_), channel_id=1, source_target_pairs={{0,96},{32,0},{64,32},{96,64},{1,97},{33,1},{65,33},{97,65},{2,98}... | collective-permute-start | bytes 1204232 | tf_op jit(solution)/shard_map/ppermute | solution.py:17
  114.9 3.4 %collective-permute-done.11.refs_8_ = bf16[224,896]{1,0:T(8,128)(2,1)S(1)} collective-permute-done((bf16[224,896]{1,0:T(8,128)(2,1)S(1)}, bf16[224,896]{1,0:T(8,128)(2,1)S(1)}, u32[]{:S(2)}, u32[]{:S(2)}) %collective-permute-start.11) | collective-permute-done | bytes 401440 | tf_op jit(solution)/shard_map/ppermute | solution.py:17
  118.4 8.6 %collective-permute-done.16.refs_13_ = bf16[224,896]{1,0:T(8,128)(2,1)S(1)} collective-permute-done((bf16[224,896]{1,0:T(8,128)(2,1)S(1)}, bf16[224,896]{1,0:T(8,128)(2,1)S(1)}, u32[]{:S(2)}, u32[]{:S(2)}) %collective-permute-start.16) | collective-permute-done | bytes 401440 | tf_op jit(solution)/shard_map/ppermute | solution.py:17
  127.0 8.6 %collective-permute-done.17.refs_14_ = bf16[224,896]{1,0:T(8,128)(2,1)S(1)} collective-permute-done((bf16[224,896]{1,0:T(8,128)(2,1)S(1)}, bf16[224,896]{1,0:T(8,128)(2,1)S(1)}, u32[]{:S(2)}, u32[]{:S(2)}) %collective-permute-start.17) | collective-permute-done | bytes 401440 | tf_op jit(solution)/shard_map/ppermute | solution.py:17
  137.0 4.1 %collective-permute-done.13.refs_10_ = bf16[224,896]{1,0:T(8,128)(2,1)} collective-permute-done((bf16[224,896]{1,0:T(8,128)(2,1)}, bf16[224,896]{1,0:T(8,128)(2,1)}, u32[]{:S(2)}, u32[]{:S(2)}) %collective-permute-start.13) | collective-permute-done | bytes 401440 | tf_op jit(solution)/shard_map/ppermute | solution.py:17
  141.1 6.3 %collective-permute-done.15.refs_11_ = bf16[224,896]{1,0:T(8,128)(2,1)} collective-permute-done((bf16[224,896]{1,0:T(8,128)(2,1)}, bf16[224,896]{1,0:T(8,128)(2,1)}, u32[]{:S(2)}, u32[]{:S(2)}) %collective-permute-start.15) | collective-permute-done | bytes 401440 | tf_op jit(solution)/shard_map/ppermute | solution.py:17
  147.4 9.5 %shard_map.51.mixed_ref = f32[896,1024]{1,0:T(8,128)} custom-call(s32[3]{0:T(128)} %pad_add_fusion.place_ref, bf16[1024,1792]{1,0:T(8,128)(2,1)} %bitcast.5.near_ref, bf16[224,896]{1,0:T(8,128)(2,1)} %copy-done.1, bf16[224,896]{1,0:T(8,128)(2,1)} %copy-done.2, bf16[224,896]{1,0:T(8,128)(2,1)} %copy-done.3, bf16[224,896]{1,0:T(8,128)(2,1)} %copy-done.4, ...), custom_call_target="tpu_custom_call" | custom-call | flops 3288334336 | bytes 12582912 | tf_op jit(solution)/shard_map/pallas_call | solution.py:144
  157.0 14.0 %shard_map.52 = (f32[32,16,1024]{2,1,0:T(8,128)}, bf16[32,16,1024]{2,1,0:T(8,128)(2,1)}) custom-call(s32[3]{0:T(128)} %pad_add_fusion.place_ref, bf16[1024,1792]{1,0:T(8,128)(2,1)} %bitcast.5.near_ref, bf16[1024,1792]{1,0:T(8,128)(2,1)} %collective-permute-done.far_ref, f32[896,1024]{1,0:T(8,128)} %shard_map.51.mixed_ref, bf16[224,896]{1,0:T(8,128)(2,1)} %copy-done.1, ...), custom_call_target="tpu_custom_call" | custom-call | flops 5167382528 | bytes 16777216 | tf_op jit(solution)/shard_map/pallas_call | solution.py:156
  171.0 2.3 %collective-permute-start.18 = (bf16[32,16,1024]{2,1,0:T(8,128)(2,1)}, bf16[32,16,1024]{2,1,0:T(8,128)(2,1)S(1)}, u32[]{:S(2)}, u32[]{:S(2)}) collective-permute-start(bf16[32,16,1024]{2,1,0:T(8,128)(2,1)} %get-tuple-element.5), channel_id=1, source_target_pairs={{0,1},{1,0},{2,3},{3,2},{4,5},{5,4},{6,7},{7,6},{8,9},{9,8},{10,11... | collective-permute-start | bytes 3145736 | tf_op jit(solution)/shard_map/ppermute | solution.py:21
  173.2 2.5 %collective-permute-done.18 = bf16[32,16,1024]{2,1,0:T(8,128)(2,1)S(1)} collective-permute-done((bf16[32,16,1024]{2,1,0:T(8,128)(2,1)}, bf16[32,16,1024]{2,1,0:T(8,128)(2,1)S(1)}, u32[]{:S(2)}, u32[]{:S(2)}) %collective-permute-start.18) | collective-permute-done | bytes 1048608 | tf_op jit(solution)/shard_map/ppermute | solution.py:21
  175.7 2.9 %add_convert_fusion = bf16[32,16,1024]{2,1,0:T(8,128)(2,1)} fusion(f32[32,16,1024]{2,1,0:T(8,128)} %get-tuple-element.4, bf16[32,16,1024]{2,1,0:T(8,128)(2,1)S(1)} %collective-permute-done.18), kind=kLoop, calls=%fused_computation | loop fusion | flops 1572864 | bytes 4194304 | tf_op jit(solution)/shard_map/convert_element_type | solution.py:205
  178.7 4.1 %all-to-all-start.1 = ((bf16[32,16,1024]{2,1,0:T(8,128)(2,1)}), bf16[32,16,1024]{2,1,0:T(8,128)(2,1)S(1)}, u32[]{:S(2)}, u32[]{:S(2)}) async-start(bf16[32,16,1024]{2,1,0:T(8,128)(2,1)} %add_convert_fusion), calls=%async_computation.1 | async-start | bytes 2097152 | tf_op jit(solution)/shard_map/all_to_all | solution.py:206
  182.9 16.9 %all-to-all-done.1 = bf16[32,16,1024]{2,1,0:T(8,128)(2,1)S(1)} async-done(((bf16[32,16,1024]{2,1,0:T(8,128)(2,1)}), bf16[32,16,1024]{2,1,0:T(8,128)(2,1)S(1)}, u32[]{:S(2)}, u32[]{:S(2)}) %all-to-all-start.1) | async-done | bytes 1048608 | tf_op jit(solution)/shard_map/all_to_all | solution.py:206
  200.7 1.1 broadcast_multiply_fusion
  (49 shorter events, 5.0 us)
Async XLA Ops:
  0.6 62.9 %copy-start = (bf16[112,3584]{1,0:T(8,128)(2,1)S(1)}, bf16[112,3584]{1,0:T(8,128)(2,1)}, u32[]{:S(2)}) copy-start(bf16[112,3584]{1,0:T(8,128)(2,1)} %param.4) | copy-start | bytes 2408452
  63.5 93.5 %collective-permute-start = (bf16[1024,1792]{1,0:T(8,128)(2,1)}, bf16[1024,1792]{1,0:T(8,128)(2,1)}, u32[]{:S(2)}, u32[]{:S(2)}) collective-permute-start(bf16[1024,1792]{1,0:T(8,128)(2,1)} %bitcast.5.near_ref), channel_id=1, source_target_pairs={{0,1},{1,0},{2,3},{3,2},{4,5},{5,4},{6,7},{7,6},{8,9},{9,8},{10,11... | collective-permute-start | bytes 11010056 | tf_op jit(solution)/shard_map/ppermute | solution.py:21
  63.5 8.0 %collective-permute-start.1 = (bf16[112,896]{1,0:T(8,128)(2,1)S(1)}, bf16[112,896]{1,0:T(8,128)(2,1)S(1)}, u32[]{:S(2)}, u32[]{:S(2)}) collective-permute-start(bf16[112,896]{1,0:T(8,128)(2,1)S(1)} %constant_dynamic-slice_fusion), channel_id=1, source_target_pairs={{0,0},{1,16},{8,8},{9,24},{16,17},{17,1},{24,25},{25,9},{2,2},{3,1... | collective-permute-start | bytes 602120 | tf_op jit(solution)/shard_map/ppermute | solution.py:187
  66.9 8.5 %collective-permute-start.2 = (bf16[112,896]{1,0:T(8,128)(2,1)S(1)}, bf16[112,896]{1,0:T(8,128)(2,1)S(1)}, u32[]{:S(2)}, u32[]{:S(2)}) collective-permute-start(bf16[112,896]{1,0:T(8,128)(2,1)S(1)} %constant_dynamic-slice_fusion), channel_id=1, source_target_pairs={{0,16},{1,0},{8,24},{9,8},{16,1},{17,17},{24,9},{25,25},{2,18},{3,... | collective-permute-start | bytes 602120 | tf_op jit(solution)/shard_map/ppermute | solution.py:188
  75.6 71.8 %copy-start.1 = (bf16[224,896]{1,0:T(8,128)(2,1)}, bf16[224,896]{1,0:T(8,128)(2,1)S(1)}, u32[]{:S(2)}) copy-start(bf16[224,896]{1,0:T(8,128)(2,1)S(1)} %pad_maximum_fusion.refs_0_) | copy-start | bytes 1204228
  75.6 11.4 %collective-permute-start.3 = (bf16[224,896]{1,0:T(8,128)(2,1)S(1)}, bf16[224,896]{1,0:T(8,128)(2,1)S(1)}, u32[]{:S(2)}, u32[]{:S(2)}) collective-permute-start(bf16[224,896]{1,0:T(8,128)(2,1)S(1)} %pad_maximum_fusion.refs_0_), channel_id=1, source_target_pairs={{0,6},{2,0},{4,2},{6,4},{1,7},{3,1},{5,3},{7,5},{8,14},{10,8},{12,... | collective-permute-start | bytes 1204232 | tf_op jit(solution)/shard_map/ppermute | solution.py:17
  76.1 13.4 %collective-permute-start.4 = (bf16[224,896]{1,0:T(8,128)(2,1)S(1)}, bf16[224,896]{1,0:T(8,128)(2,1)S(1)}, u32[]{:S(2)}, u32[]{:S(2)}) collective-permute-start(bf16[224,896]{1,0:T(8,128)(2,1)S(1)} %pad_maximum_fusion.refs_0_), channel_id=1, source_target_pairs={{0,4},{2,6},{4,0},{6,2},{1,5},{3,7},{5,1},{7,3},{8,12},{10,14},{12... | collective-permute-start | bytes 1204232 | tf_op jit(solution)/shard_map/ppermute | solution.py:17
  77.7 17.8 %collective-permute-start.5 = (bf16[224,896]{1,0:T(8,128)(2,1)S(1)}, bf16[224,896]{1,0:T(8,128)(2,1)S(1)}, u32[]{:S(2)}, u32[]{:S(2)}) collective-permute-start(bf16[224,896]{1,0:T(8,128)(2,1)S(1)} %pad_maximum_fusion.refs_0_), channel_id=1, source_target_pairs={{0,2},{2,4},{4,6},{6,0},{1,3},{3,5},{5,7},{7,1},{8,10},{10,12},{12... | collective-permute-start | bytes 1204232 | tf_op jit(solution)/shard_map/ppermute | solution.py:17
  77.7 20.4 %collective-permute-start.10 = (bf16[224,896]{1,0:T(8,128)(2,1)S(1)}, bf16[224,896]{1,0:T(8,128)(2,1)S(1)}, u32[]{:S(2)}, u32[]{:S(2)}) collective-permute-start(bf16[224,896]{1,0:T(8,128)(2,1)S(1)} %pad_maximum_fusion.refs_0_), channel_id=1, source_target_pairs={{0,32},{32,64},{64,96},{96,0},{1,33},{33,65},{65,97},{97,1},{2,34}... | collective-permute-start | bytes 1204232 | tf_op jit(solution)/shard_map/ppermute | solution.py:17
  87.0 60.4 %copy-start.2 = (bf16[224,896]{1,0:T(8,128)(2,1)}, bf16[224,896]{1,0:T(8,128)(2,1)S(1)}, u32[]{:S(2)}) copy-start(bf16[224,896]{1,0:T(8,128)(2,1)S(1)} %collective-permute-done.3.refs_1_) | copy-start | bytes 1204228
  87.0 11.6 %collective-permute-start.6 = (bf16[224,896]{1,0:T(8,128)(2,1)S(1)}, bf16[224,896]{1,0:T(8,128)(2,1)S(1)}, u32[]{:S(2)}, u32[]{:S(2)}) collective-permute-start(bf16[224,896]{1,0:T(8,128)(2,1)S(1)} %pad_maximum_fusion.refs_0_), channel_id=1, source_target_pairs={{0,96},{32,0},{64,32},{96,64},{1,97},{33,1},{65,33},{97,65},{2,98}... | collective-permute-start | bytes 1204232 | tf_op jit(solution)/shard_map/ppermute | solution.py:17
  89.4 58.0 %copy-start.3 = (bf16[224,896]{1,0:T(8,128)(2,1)}, bf16[224,896]{1,0:T(8,128)(2,1)S(1)}, u32[]{:S(2)}) copy-start(bf16[224,896]{1,0:T(8,128)(2,1)S(1)} %collective-permute-done.4.refs_2_) | copy-start | bytes 1204228
  89.4 17.4 %collective-permute-start.7 = (bf16[224,896]{1,0:T(8,128)(2,1)S(1)}, bf16[224,896]{1,0:T(8,128)(2,1)}, u32[]{:S(2)}, u32[]{:S(2)}) collective-permute-start(bf16[224,896]{1,0:T(8,128)(2,1)S(1)} %collective-permute-done.3.refs_1_), channel_id=1, source_target_pairs={{0,96},{32,0},{64,32},{96,64},{1,97},{33,1},{65,33},{97,65},{2,98}... | collective-permute-start | bytes 1204232 | tf_op jit(solution)/shard_map/ppermute | solution.py:17
  95.5 51.9 %copy-start.4 = (bf16[224,896]{1,0:T(8,128)(2,1)}, bf16[224,896]{1,0:T(8,128)(2,1)S(1)}, u32[]{:S(2)}) copy-start(bf16[224,896]{1,0:T(8,128)(2,1)S(1)} %collective-permute-done.5.refs_3_) | copy-start | bytes 1204228
  95.5 16.2 %collective-permute-start.8 = (bf16[224,896]{1,0:T(8,128)(2,1)S(1)}, bf16[224,896]{1,0:T(8,128)(2,1)}, u32[]{:S(2)}, u32[]{:S(2)}) collective-permute-start(bf16[224,896]{1,0:T(8,128)(2,1)S(1)} %collective-permute-done.4.refs_2_), channel_id=1, source_target_pairs={{0,96},{32,0},{64,32},{96,64},{1,97},{33,1},{65,33},{97,65},{2,98}... | collective-permute-start | bytes 1204232 | tf_op jit(solution)/shard_map/ppermute | solution.py:17
  98.2 49.2 %copy-start.5 = (bf16[224,896]{1,0:T(8,128)(2,1)}, bf16[224,896]{1,0:T(8,128)(2,1)S(1)}, u32[]{:S(2)}) copy-start(bf16[224,896]{1,0:T(8,128)(2,1)S(1)} %collective-permute-done.10.refs_12_) | copy-start | bytes 1204228
  98.2 14.5 %collective-permute-start.14 = (bf16[224,896]{1,0:T(8,128)(2,1)S(1)}, bf16[224,896]{1,0:T(8,128)(2,1)}, u32[]{:S(2)}, u32[]{:S(2)}) collective-permute-start(bf16[224,896]{1,0:T(8,128)(2,1)S(1)} %collective-permute-done.5.refs_3_), channel_id=1, source_target_pairs={{0,32},{32,64},{64,96},{96,0},{1,33},{33,65},{65,97},{97,1},{2,34}... | collective-permute-start | bytes 1204232 | tf_op jit(solution)/shard_map/ppermute | solution.py:17
  98.5 48.9 %copy-start.6 = (bf16[224,896]{1,0:T(8,128)(2,1)}, bf16[224,896]{1,0:T(8,128)(2,1)S(1)}, u32[]{:S(2)}) copy-start(bf16[224,896]{1,0:T(8,128)(2,1)S(1)} %collective-permute-done.6.refs_4_) | copy-start | bytes 1204228
  98.5 19.8 %collective-permute-start.11 = (bf16[224,896]{1,0:T(8,128)(2,1)S(1)}, bf16[224,896]{1,0:T(8,128)(2,1)S(1)}, u32[]{:S(2)}, u32[]{:S(2)}) collective-permute-start(bf16[224,896]{1,0:T(8,128)(2,1)S(1)} %collective-permute-done.10.refs_12_), channel_id=1, source_target_pairs={{0,32},{32,64},{64,96},{96,0},{1,33},{33,65},{65,97},{97,1},{2,34}... | collective-permute-start | bytes 1204232 | tf_op jit(solution)/shard_map/ppermute | solution.py:17
  106.9 20.1 %collective-permute-start.16 = (bf16[224,896]{1,0:T(8,128)(2,1)S(1)}, bf16[224,896]{1,0:T(8,128)(2,1)S(1)}, u32[]{:S(2)}, u32[]{:S(2)}) collective-permute-start(bf16[224,896]{1,0:T(8,128)(2,1)S(1)} %collective-permute-done.3.refs_1_), channel_id=1, source_target_pairs={{0,32},{32,64},{64,96},{96,0},{1,33},{33,65},{65,97},{97,1},{2,34}... | collective-permute-start | bytes 1204232 | tf_op jit(solution)/shard_map/ppermute | solution.py:17
  111.7 23.9 %collective-permute-start.17 = (bf16[224,896]{1,0:T(8,128)(2,1)S(1)}, bf16[224,896]{1,0:T(8,128)(2,1)S(1)}, u32[]{:S(2)}, u32[]{:S(2)}) collective-permute-start(bf16[224,896]{1,0:T(8,128)(2,1)S(1)} %collective-permute-done.4.refs_2_), channel_id=1, source_target_pairs={{0,32},{32,64},{64,96},{96,0},{1,33},{33,65},{65,97},{97,1},{2,34}... | collective-permute-start | bytes 1204232 | tf_op jit(solution)/shard_map/ppermute | solution.py:17
  112.6 24.4 %collective-permute-start.9 = (bf16[224,896]{1,0:T(8,128)(2,1)S(1)}, bf16[224,896]{1,0:T(8,128)(2,1)}, u32[]{:S(2)}, u32[]{:S(2)}) collective-permute-start(bf16[224,896]{1,0:T(8,128)(2,1)S(1)} %collective-permute-done.5.refs_3_), channel_id=1, source_target_pairs={{0,96},{32,0},{64,32},{96,64},{1,97},{33,1},{65,33},{97,65},{2,98}... | collective-permute-start | bytes 1204232 | tf_op jit(solution)/shard_map/ppermute | solution.py:17
  118.4 17.2 %copy-start.7 = (bf16[224,896]{1,0:T(8,128)(2,1)}, bf16[224,896]{1,0:T(8,128)(2,1)S(1)}, u32[]{:S(2)}) copy-start(bf16[224,896]{1,0:T(8,128)(2,1)S(1)} %collective-permute-done.11.refs_8_) | copy-start | bytes 1204228
  118.4 18.6 %collective-permute-start.12 = (bf16[224,896]{1,0:T(8,128)(2,1)}, bf16[224,896]{1,0:T(8,128)(2,1)}, u32[]{:S(2)}, u32[]{:S(2)}) collective-permute-start(bf16[224,896]{1,0:T(8,128)(2,1)} %collective-permute-done.7.refs_5_), channel_id=1, source_target_pairs={{0,96},{32,0},{64,32},{96,64},{1,97},{33,1},{65,33},{97,65},{2,98}... | collective-permute-start | bytes 1204232 | tf_op jit(solution)/shard_map/ppermute | solution.py:17
  127.0 8.6 %copy-start.8 = (bf16[224,896]{1,0:T(8,128)(2,1)}, bf16[224,896]{1,0:T(8,128)(2,1)S(1)}, u32[]{:S(2)}) copy-start(bf16[224,896]{1,0:T(8,128)(2,1)S(1)} %collective-permute-done.16.refs_13_) | copy-start | bytes 1204228
  127.0 14.1 %collective-permute-start.13 = (bf16[224,896]{1,0:T(8,128)(2,1)}, bf16[224,896]{1,0:T(8,128)(2,1)}, u32[]{:S(2)}, u32[]{:S(2)}) collective-permute-start(bf16[224,896]{1,0:T(8,128)(2,1)} %collective-permute-done.8.refs_6_), channel_id=1, source_target_pairs={{0,96},{32,0},{64,32},{96,64},{1,97},{33,1},{65,33},{97,65},{2,98}... | collective-permute-start | bytes 1204232 | tf_op jit(solution)/shard_map/ppermute | solution.py:17
  135.6 0.8 copy-start.9
  136.3 11.0 %collective-permute-start.15 = (bf16[224,896]{1,0:T(8,128)(2,1)}, bf16[224,896]{1,0:T(8,128)(2,1)}, u32[]{:S(2)}, u32[]{:S(2)}) collective-permute-start(bf16[224,896]{1,0:T(8,128)(2,1)} %collective-permute-done.14.refs_15_), channel_id=1, source_target_pairs={{0,32},{32,64},{64,96},{96,0},{1,33},{33,65},{65,97},{97,1},{2,34}... | collective-permute-start | bytes 1204232 | tf_op jit(solution)/shard_map/ppermute | solution.py:17
  171.0 4.8 %collective-permute-start.18 = (bf16[32,16,1024]{2,1,0:T(8,128)(2,1)}, bf16[32,16,1024]{2,1,0:T(8,128)(2,1)S(1)}, u32[]{:S(2)}, u32[]{:S(2)}) collective-permute-start(bf16[32,16,1024]{2,1,0:T(8,128)(2,1)} %get-tuple-element.5), channel_id=1, source_target_pairs={{0,1},{1,0},{2,3},{3,2},{4,5},{5,4},{6,7},{7,6},{8,9},{9,8},{10,11... | collective-permute-start | bytes 3145736 | tf_op jit(solution)/shard_map/ppermute | solution.py:21
  178.7 4.1 %copy-start.10 = (s32[8,32]{1,0:T(8,128)S(1)}, s32[8,32]{1,0:T(8,128)}, u32[]{:S(2)}) copy-start(s32[8,32]{1,0:T(8,128)} %param.5) | copy-start | bytes 3076
  178.7 21.1 %all-to-all-start.1 = ((bf16[32,16,1024]{2,1,0:T(8,128)(2,1)}), bf16[32,16,1024]{2,1,0:T(8,128)(2,1)S(1)}, u32[]{:S(2)}, u32[]{:S(2)}) async-start(bf16[32,16,1024]{2,1,0:T(8,128)(2,1)} %add_convert_fusion), calls=%async_computation.1 | async-start | bytes 2097152 | tf_op jit(solution)/shard_map/all_to_all | solution.py:206

commit v4 on v3

v4 whole, which is shorter than its diff:
```python
import jax
import jax.numpy as jnp
from jax import lax
from jax.experimental import pallas as pl
from jax.experimental.pallas import tpu as pltpu
from jax.sharding import Mesh, PartitionSpec as P


RESP_AXES = ("y", "z", "c")
FILL = 256.0
FILL_TEST = 128.0
HIDDEN = 1e30
HIDDEN_TEST = -1e29
CHUNKS = 2
PIECES = tuple((s, r, 0) for s in (0, 1, 3) for r in range(4)) + ((2, 0, 0), (2, 1, 0), (2, 2, 0), (2, 2, 1), (2, 3, 0))
COUNT = len(PIECES)


def ring(value, axis, step):
    return lax.ppermute(value, axis, [(i, (i + step) % 4) for i in range(4)])


def swap_cores(value):
    return lax.ppermute(value, "c", [(0, 1), (1, 0)])


def slab_pairs(first_core):
    pairs = []
    for y in range(4):
        for c in range(2):
            target = y if c == first_core else y ^ 1
            pairs.append((y * 2 + c, target * 2 + y % 2))
    return pairs


def pack_kernel(rows_ref, valid_ref, out_ref, in_ref, send_ref, in_sems, out_sems):
    prompts, _, features = in_ref.shape
    half = features // 2
    quarter = half // 2
    loads = [
        pltpu.make_async_copy(rows_ref.at[p], in_ref.at[p], in_sems.at[p]) for p in range(prompts)
    ]
    stores = [
        pltpu.make_async_copy(send_ref.at[p], out_ref.at[:, p // 4, p % 4], out_sems.at[p])
        for p in range(prompts)
    ]
    for load in loads:
        load.start()
    valid = valid_ref[...].astype(jnp.float32).T
    for p in range(prompts):
        loads[p].wait()
        rows = in_ref[p]
        filled = jnp.where(valid[:, p : p + 1] > 0, rows.astype(jnp.float32), FILL).astype(rows.dtype)
        for h in range(2):
            for c in range(2):
                for place, index in enumerate((2 * h + c, 2 * (1 - h) + c)):
                    send_ref[p, h, c, :, place * quarter : (place + 1) * quarter] = filled[
                        :, index * quarter : (index + 1) * quarter
                    ]
        stores[p].start()
    for store in stores:
        store.wait()


def pack(embeddings, valid_mask):
    prompts, block_rows, features = embeddings.shape
    half = features // 2
    out = pl.pallas_call(
        pack_kernel,
        in_specs=[in_hbm(), whole()],
        out_specs=in_hbm(),
        out_shape=jax.ShapeDtypeStruct((2, 2, 4, 2, block_rows, half), embeddings.dtype),
        scratch_shapes=[
            pltpu.VMEM(embeddings.shape, embeddings.dtype),
            pltpu.VMEM((prompts, 2, 2, block_rows, half), embeddings.dtype),
            pltpu.SemaphoreType.DMA((prompts,)),
            pltpu.SemaphoreType.DMA((prompts,)),
        ],
    )(embeddings, valid_mask)
    return out.reshape(32, block_rows, half)


def weight_copies(place_ref, pieces, w_ref, sems, first, s):
    quarter = w_ref.shape[0]
    rows = quarter // 4
    position = lax.rem(place_ref[0] + s, 4)
    lanes = pl.multiple_of((position - first) * quarter, quarter)
    copies = []
    for index, (from_plane, from_row, half) in enumerate(PIECES):
        if from_plane == s:
            count = pieces[index].shape[0]
            at = pl.multiple_of(lax.rem(place_ref[1] + from_row, 4) * rows + half * count, count)
            target = w_ref.at[pl.ds(at, count), pl.ds(lanes, quarter)]
            copies.append(pltpu.make_async_copy(pieces[index], target, sems.at[index]))
    return jnp.logical_and(position >= first, position < first + 2), copies


def load_weights(place_ref, pieces, w_ref, sems, first):
    for s in range(4):
        here, copies = weight_copies(place_ref, pieces, w_ref, sems, first, s)

        @pl.when(here)
        def _():
            for copy in copies:
                copy.start()


def wait_weights(place_ref, pieces, w_ref, sems, first):
    for s in range(4):
        here, copies = weight_copies(place_ref, pieces, w_ref, sems, first, s)

        @pl.when(here)
        def _():
            for copy in copies:
                copy.wait()


def times_rows(w_ref, rows):
    return lax.dot_general(w_ref[...], rows, (((1,), (1,)), ((), ())), preferred_element_type=jnp.float32)


def row_loads(source, target, sems):
    rows = target.shape[0] // CHUNKS
    at = [pl.ds(n * rows, rows) for n in range(CHUNKS)]
    return [pltpu.make_async_copy(source.at[at[n]], target.at[at[n]], sems.at[n]) for n in range(CHUNKS)]


def near_kernel(place_ref, near_hbm, *refs):
    pieces, (mixed_hbm, w_ref, near_ref, mixed_ref, sems, near_sems, out_sems) = refs[:COUNT], refs[COUNT:]
    load_weights(place_ref, pieces, w_ref, sems, 0)
    loads = row_loads(near_hbm, near_ref, near_sems)
    for load in loads:
        load.start()
    wait_weights(place_ref, pieces, w_ref, sems, 0)
    rows = near_ref.shape[0] // CHUNKS
    stores = []
    for n in range(CHUNKS):
        loads[n].wait()
        mixed_ref[n] = times_rows(w_ref, near_ref[n * rows : (n + 1) * rows, :])
        stores.append(pltpu.make_async_copy(mixed_ref.at[n], mixed_hbm.at[n], out_sems.at[n]))
        stores[n].start()
    for store in stores:
        store.wait()


def far_kernel(place_ref, near_hbm, far_hbm, mixed_hbm, *refs):
    pieces, outs, scratch = refs[:COUNT], refs[COUNT : COUNT + 2], refs[COUNT + 2 :]
    kept_ref, given_ref = outs
    w_ref, far_ref, first_ref, mixed_ref, total_ref, table_ref, sems, far_sems, mixed_sems, first_sem = scratch
    load_weights(place_ref, pieces, w_ref, sems, 2)
    quarter = w_ref.shape[0]
    slots = table_ref.shape[0]
    rows = slots // CHUNKS
    loads = row_loads(far_hbm, far_ref, far_sems)
    partials = [pltpu.make_async_copy(mixed_hbm.at[n], mixed_ref.at[n], mixed_sems.at[n]) for n in range(CHUNKS)]
    first = pltpu.make_async_copy(near_hbm.at[:, pl.ds(0, quarter)], first_ref, first_sem.at[0])
    for n in range(CHUNKS):
        loads[n].start()
        partials[n].start()
    first.start()
    wait_weights(place_ref, pieces, w_ref, sems, 2)
    for n in range(CHUNKS):
        at = slice(n * rows, (n + 1) * rows)
        loads[n].wait()
        partials[n].wait()
        total_ref[:, at] = (mixed_ref[n] + times_rows(w_ref, far_ref[at, :])).astype(total_ref.dtype)
    first.wait()
    hidden = jnp.where(first_ref[:, :1].astype(jnp.float32) < FILL_TEST, 0.0, HIDDEN)
    table_ref[...] = jnp.dot(first_ref[...], total_ref[...], preferred_element_type=jnp.float32) + hidden
    c = place_ref[2]
    block = 128
    part = kept_ref.shape[1]
    for i in range(slots // block):
        at = slice(i * block, (i + 1) * block)
        skew = table_ref[at, :] - table_ref[:, at].T
        groups = block // (2 * part)
        skew = skew.reshape(groups, 2, part, slots)
        low, high = skew[:, 0], skew[:, 1]
        at = slice(i * groups, (i + 1) * groups)
        kept_ref[at] = jnp.where(c == 0, low, high).astype(kept_ref.dtype)
        given_ref[at] = jnp.where(c == 0, high, low).astype(given_ref.dtype)


def in_hbm():
    return pl.BlockSpec(memory_space=pl.ANY)


def whole():
    return pl.BlockSpec(memory_space=pltpu.VMEM)


def score_parts(place, near, far, pieces):
    slots, half = near.shape
    quarter = half // 2
    rows = slots // CHUNKS
    scalars = pl.BlockSpec(memory_space=pltpu.SMEM)
    limit = pltpu.CompilerParams(vmem_limit_bytes=56 * 2**20)
    four = pltpu.SemaphoreType.DMA((CHUNKS,))
    each = pltpu.SemaphoreType.DMA((COUNT,))
    mixed = pl.pallas_call(
        near_kernel,
        in_specs=[scalars] + [in_hbm()] * (COUNT + 1),
        out_specs=in_hbm(),
        out_shape=jax.ShapeDtypeStruct((CHUNKS, quarter, rows), jnp.float32),
        scratch_shapes=[
            pltpu.VMEM((quarter, half), near.dtype),
            pltpu.VMEM((slots, half), near.dtype),
            pltpu.VMEM((CHUNKS, quarter, rows), jnp.float32),
            each,
            four,
            four,
        ],
        compiler_params=limit,
        cost_estimate=pl.CostEstimate(
            flops=2 * quarter * half * slots, bytes_accessed=12 * 2**20, transcendentals=0
        ),
    )(place, near, *pieces)
    part = slots // 64
    return pl.pallas_call(
        far_kernel,
        in_specs=[scalars] + [in_hbm()] * (COUNT + 3),
        out_specs=[whole(), whole()],
        out_shape=[
            jax.ShapeDtypeStruct((32, part, slots), jnp.bfloat16),
            jax.ShapeDtypeStruct((32, part, slots), jnp.bfloat16),
        ],
        scratch_shapes=[
            pltpu.VMEM((quarter, half), near.dtype),
            pltpu.VMEM((slots, half), near.dtype),
            pltpu.VMEM((slots, quarter), near.dtype),
            pltpu.VMEM((CHUNKS, quarter, rows), jnp.float32),
            pltpu.VMEM((quarter, slots), near.dtype),
            pltpu.VMEM((slots, slots), jnp.float32),
            each,
            four,
            four,
            pltpu.SemaphoreType.DMA((1,)),
        ],
        compiler_params=limit,
        cost_estimate=pl.CostEstimate(
            flops=2 * quarter * (half + slots) * slots, bytes_accessed=16 * 2**20, transcendentals=0
        ),
    )(place, near, far, mixed, *pieces)


def scored(embeddings, head_weight, valid_mask):
    prompts, block_rows, features = embeddings.shape
    quarter = features // 4
    slots = 32 * block_rows
    x = lax.axis_index("x")
    y = lax.axis_index("y")
    z = lax.axis_index("z")
    c = lax.axis_index("c")

    slab = lax.dynamic_slice_in_dim(head_weight, (y ^ ((x % 2) * 2 + x // 2)) * quarter, quarter, 1)
    part_a = lax.ppermute(slab, ("y", "c"), slab_pairs(0))
    part_b = lax.ppermute(slab, ("y", "c"), slab_pairs(1))
    outgoing = pack(embeddings, valid_mask)
    at_home = c == y % 2
    own = jnp.concatenate([jnp.where(at_home, part_a, part_b), jnp.where(at_home, part_b, part_a)])
    chain = [own]
    for step in (-1, 2, 1):
        chain.append(ring(own, "z", step))
    near = lax.all_to_all(outgoing, RESP_AXES, 0, 0, tiled=True).reshape(slots, 2 * quarter)
    below, above = [], []
    for piece in chain:
        below.append(ring(piece, "x", 1))
        above.append(ring(piece, "x", -1))
    across = []
    for index, steps in enumerate(((1,), (-1,), (1, -1), (1,))):
        for half, step in enumerate(steps):
            piece = (below if step == 1 else above)[index]
            rows = piece.shape[0] // len(steps)
            across.append(ring(piece[half * rows : (half + 1) * rows], "x", step))
    far = swap_cores(near)

    place = jnp.stack([x, z, c]).astype(jnp.int32)
    kept, given = score_parts(place, near, far, [*chain, *above, *below, *across])
    half_scores = (kept.astype(jnp.float32) + swap_cores(given).astype(jnp.float32)).astype(jnp.bfloat16)
    returned = lax.all_to_all(half_scores, RESP_AXES, 0, 0, tiled=True)
    returned = returned.astype(jnp.float32).reshape(2, 2, 4, 2, block_rows // 2, slots)
    scores = (returned[0] + returned[1]).reshape(prompts, block_rows, slots)

    valid_rows = valid_mask.astype(jnp.float32)
    counts = jnp.sum((scores > HIDDEN_TEST).astype(jnp.float32), axis=2)
    preferences = jax.nn.sigmoid(scores) * valid_rows[:, :, None]
    totals = jnp.sum(preferences, axis=2) - 0.5 * valid_rows
    win_rates = valid_rows * totals / jnp.maximum(counts - 1.0, 1.0)
    return preferences, win_rates


def solution(mesh):
    mesh = Mesh(mesh.devices.reshape(4, 4, 4, 2), ("x", "y", "z", "c"))
    spec = P("x", RESP_AXES)
    return jax.shard_map(
        scored,
        mesh=mesh,
        in_specs=(P("x", RESP_AXES, None), P(RESP_AXES, None), spec),
        out_specs=(P("x", RESP_AXES, None), spec),
        check_vma=False,
    )
```

time: 203 us -> 194 us (0.956)
  waiting for transfers between devices: 80.9 us -> 74.2 us
  Pallas kernels: 29.8 us -> 24.6 us
  starting transfers between devices: 27.2 us -> 29.9 us
    pallas_call x3, Pallas kernels: 29.8 us -> 24.6 us  [the longest x1 12.6 us: score_parts(): pl.pallas_call(far_kernel, in_specs=[scalars] + [in_hbm()] * (COUNT + 3),...]
    ppermute x15 -> x16, waiting for transfers between devices: 54.9 us -> 49.8 us  [ring(): return lax.ppermute(value, axis, [(i, (i + step) % 4) for i in range(4)])]
    ppermute x15 -> x16, starting transfers between devices: 15.5 us -> 19 us  [ring(): return lax.ppermute(value, axis, [(i, (i + step) % 4) for i in range(4)])]
  transfers between devices with their start and end apart: 20 -> 21, of which waited for: 14 -> 13; matrix products, arithmetic and copies ran while one was open for 0% -> 1% of each run, Pallas kernels for 5% -> 4%
where the time goes in v4:
time: 194 us
  waiting for transfers between devices  74.2 us (38%)
  blocking collectives  55 us (28%)
  starting transfers between devices  29.9 us (15%)
  Pallas kernels  24.6 us (13%)
  other arithmetic  5.74 us (3%)
  local copies, waits for them, and re-layouts  3.21 us (2%)
    all_to_all x1, blocking collectives, scored(): lax.all_to_all(outgoing, RESP_AXES, 0, 0, tiled=True)  55 us
    ppermute x16, waiting for transfers between devices, ring(): return lax.ppermute(value, axis, [(i, (i + step) % 4) for i in range(4)])  49.8 us
    ppermute x16, starting transfers between devices, ring(): return lax.ppermute(value, axis, [(i, (i + step) % 4) for i in range(4)])  19 us
    all_to_all x1, waiting for transfers between devices, scored(): returned = lax.all_to_all(half_scores, RESP_AXES, 0, 0, tiled=True)  16.8 us
    pallas_call x1, Pallas kernels, score_parts(): pl.pallas_call(far_kernel, in_specs=[scalars] + [in_hbm()] * (COUNT + 3),...  12.6 us
    pallas_call x1, Pallas kernels, score_parts(): pl.pallas_call(near_kernel, in_specs=[scalars] + [in_hbm()] * (COUNT + 1)...  8.21 us
    all_to_all x1, starting transfers between devices, scored(): returned = lax.all_to_all(half_scores, RESP_AXES, 0, 0, tiled=True)  5.18 us
  transfers between devices with their start and end apart: 21, of which 13 were waited for; matrix products, arithmetic and copies ran while one was open for 1% of the time, Pallas kernels for 4%

profile of v4, /device:TPU:1, one launch (start us, length us, event | category | flops | bytes accessed | tf_op | source)
XLA Modules:
  0.0 193.5 jit_solution(13639510353224194888)
XLA Ops:
  0.6 3.8 %shard_map.50 = bf16[2,2,4,2,32,1792]{5,4,3,2,1,0:T(8,128)(2,1)} custom-call(bf16[8,32,3584]{2,1,0:T(8,128)(2,1)} %rows_ref.1, s32[8,32]{1,0:T(8,128)} %valid_ref.1), custom_call_target="tpu_custom_call" | custom-call | tf_op jit(solution)/shard_map/pallas_call | solution.py:68
  4.4 55.0 %all_to_all.10 = bf16[32,32,1792]{2,1,0:T(8,128)(2,1)} all-to-all(bf16[32,32,1792]{2,1,0:T(8,128)(2,1)} %bitcast.8), channel_id=1, replica_groups=mesh['x'=4,'y'=4,'z'=4,'c'=2] {'y','z','c'}, dimensions={0} | all-to-all | bytes 7340032 | tf_op jit(solution)/shard_map/all_to_all | solution.py:264
  59.4 2.5 %collective-permute-start.1 = (bf16[112,896]{1,0:T(8,128)(2,1)S(1)}, bf16[112,896]{1,0:T(8,128)(2,1)S(1)}, u32[]{:S(2)}, u32[]{:S(2)}) collective-permute-start(bf16[112,896]{1,0:T(8,128)(2,1)S(1)} %constant_dynamic-slice_fusion), channel_id=1, source_target_pairs={{0,0},{1,8},{8,9},{9,1},{16,16},{17,24},{24,25},{25,17},{2,2},{3,1... | collective-permute-start | bytes 602120 | tf_op jit(solution)/shard_map/ppermute | solution.py:256
  61.9 1.9 collective-permute-start.2
  63.9 2.0 %collective-permute-done.1 = bf16[112,896]{1,0:T(8,128)(2,1)S(1)} collective-permute-done((bf16[112,896]{1,0:T(8,128)(2,1)S(1)}, bf16[112,896]{1,0:T(8,128)(2,1)S(1)}, u32[]{:S(2)}, u32[]{:S(2)}) %collective-permute-start.1) | collective-permute-done | bytes 200736 | tf_op jit(solution)/shard_map/ppermute | solution.py:256
  65.9 3.0 %collective-permute-done.2 = bf16[112,896]{1,0:T(8,128)(2,1)S(1)} collective-permute-done((bf16[112,896]{1,0:T(8,128)(2,1)S(1)}, bf16[112,896]{1,0:T(8,128)(2,1)S(1)}, u32[]{:S(2)}, u32[]{:S(2)}) %collective-permute-start.2) | collective-permute-done | bytes 200736 | tf_op jit(solution)/shard_map/ppermute | solution.py:257
  69.0 1.3 collective-permute-start.3
  70.3 1.0 collective-permute-start.4
  71.4 1.2 collective-permute-start.10
  72.6 7.8 %collective-permute-done.3.refs_1_ = bf16[224,896]{1,0:T(8,128)(2,1)S(1)} collective-permute-done((bf16[224,896]{1,0:T(8,128)(2,1)S(1)}, bf16[224,896]{1,0:T(8,128)(2,1)S(1)}, u32[]{:S(2)}, u32[]{:S(2)}) %collective-permute-start.3) | collective-permute-done | bytes 401440 | tf_op jit(solution)/shard_map/ppermute | solution.py:20
  80.4 2.5 %collective-permute-start.6 = (bf16[224,896]{1,0:T(8,128)(2,1)S(1)}, bf16[224,896]{1,0:T(8,128)(2,1)S(1)}, u32[]{:S(2)}, u32[]{:S(2)}) collective-permute-start(bf16[224,896]{1,0:T(8,128)(2,1)S(1)} %pad_maximum_fusion.refs_0_), channel_id=1, source_target_pairs={{0,96},{32,0},{64,32},{96,64},{1,97},{33,1},{65,33},{97,65},{2,98}... | collective-permute-start | bytes 1204232 | tf_op jit(solution)/shard_map/ppermute | solution.py:20
  82.9 2.5 %collective-permute-start.7 = (bf16[224,896]{1,0:T(8,128)(2,1)S(1)}, bf16[224,896]{1,0:T(8,128)(2,1)}, u32[]{:S(2)}, u32[]{:S(2)}) collective-permute-start(bf16[224,896]{1,0:T(8,128)(2,1)S(1)} %collective-permute-done.3.refs_1_), channel_id=1, source_target_pairs={{0,96},{32,0},{64,32},{96,64},{1,97},{33,1},{65,33},{97,65},{2,98}... | collective-permute-start | bytes 1204232 | tf_op jit(solution)/shard_map/ppermute | solution.py:20
  85.4 5.6 %collective-permute-done.5.refs_3_ = bf16[224,896]{1,0:T(8,128)(2,1)S(1)} collective-permute-done((bf16[224,896]{1,0:T(8,128)(2,1)S(1)}, bf16[224,896]{1,0:T(8,128)(2,1)S(1)}, u32[]{:S(2)}, u32[]{:S(2)}) %collective-permute-start.5) | collective-permute-done | bytes 401440 | tf_op jit(solution)/shard_map/ppermute | solution.py:20
  91.0 1.2 collective-permute-start.12
  92.2 1.5 collective-permute-start.8
  93.7 6.9 %collective-permute-done.7.refs_5_ = bf16[224,896]{1,0:T(8,128)(2,1)} collective-permute-done((bf16[224,896]{1,0:T(8,128)(2,1)S(1)}, bf16[224,896]{1,0:T(8,128)(2,1)}, u32[]{:S(2)}, u32[]{:S(2)}) %collective-permute-start.7) | collective-permute-done | bytes 401440 | tf_op jit(solution)/shard_map/ppermute | solution.py:20
  101.5 1.1 collective-permute-done.12.refs_10_
  102.8 5.2 %collective-permute-done.8.refs_6_ = bf16[224,896]{1,0:T(8,128)(2,1)S(1)} collective-permute-done((bf16[224,896]{1,0:T(8,128)(2,1)S(1)}, bf16[224,896]{1,0:T(8,128)(2,1)S(1)}, u32[]{:S(2)}, u32[]{:S(2)}) %collective-permute-start.8) | collective-permute-done | bytes 401440 | tf_op jit(solution)/shard_map/ppermute | solution.py:20
  108.0 3.1 %collective-permute-start.9 = (bf16[224,896]{1,0:T(8,128)(2,1)S(1)}, bf16[224,896]{1,0:T(8,128)(2,1)S(1)}, u32[]{:S(2)}, u32[]{:S(2)}) collective-permute-start(bf16[224,896]{1,0:T(8,128)(2,1)S(1)} %collective-permute-done.5.refs_3_), channel_id=1, source_target_pairs={{0,96},{32,0},{64,32},{96,64},{1,97},{33,1},{65,33},{97,65},{2,98}... | collective-permute-start | bytes 1204232 | tf_op jit(solution)/shard_map/ppermute | solution.py:20
  111.3 1.6 collective-permute-start.15
  112.9 6.9 %collective-permute-done.11.refs_9_ = bf16[224,896]{1,0:T(8,128)(2,1)S(1)} collective-permute-done((bf16[224,896]{1,0:T(8,128)(2,1)S(1)}, bf16[224,896]{1,0:T(8,128)(2,1)S(1)}, u32[]{:S(2)}, u32[]{:S(2)}) %collective-permute-start.11) | collective-permute-done | bytes 401440 | tf_op jit(solution)/shard_map/ppermute | solution.py:20
  121.4 7.0 %collective-permute-done.14.refs_12_ = bf16[224,896]{1,0:T(8,128)(2,1)S(1)} collective-permute-done((bf16[224,896]{1,0:T(8,128)(2,1)S(1)}, bf16[224,896]{1,0:T(8,128)(2,1)S(1)}, u32[]{:S(2)}, u32[]{:S(2)}) %collective-permute-start.14) | collective-permute-done | bytes 401440 | tf_op jit(solution)/shard_map/ppermute | solution.py:20
  129.9 1.9 %collective-permute-start.17 = (bf16[112,896]{1,0:T(8,128)(2,1)S(1)}, bf16[112,896]{1,0:T(8,128)(2,1)}, u32[]{:S(2)}, u32[]{:S(2)}) collective-permute-start(bf16[112,896]{1,0:T(8,128)(2,1)S(1)} %slice.19), channel_id=1, source_target_pairs={{0,96},{32,0},{64,32},{96,64},{1,97},{33,1},{65,33},{97,65},{2,98}... | collective-permute-start | bytes 602120 | tf_op jit(solution)/shard_map/ppermute | solution.py:20
  132.5 9.0 %collective-permute-done.16.refs_14_ = bf16[112,896]{1,0:T(8,128)(2,1)} collective-permute-done((bf16[112,896]{1,0:T(8,128)(2,1)}, bf16[112,896]{1,0:T(8,128)(2,1)}, u32[]{:S(2)}, u32[]{:S(2)}) %collective-permute-start.16) | collective-permute-done | bytes 200736 | tf_op jit(solution)/shard_map/ppermute | solution.py:20
  141.5 8.2 %shard_map.51.mixed_hbm = f32[2,896,512]{2,1,0:T(8,128)} custom-call(s32[3]{0:T(128)} %pad_add_fusion.place_ref, bf16[1024,1792]{1,0:T(8,128)(2,1)} %bitcast.4.near_hbm, bf16[224,896]{1,0:T(8,128)(2,1)} %copy-done.1, bf16[224,896]{1,0:T(8,128)(2,1)} %copy-done.4, bf16[224,896]{1,0:T(8,128)(2,1)} %copy-done.5, bf16[224,896]{1,0:T(8,128)(2,1)} %copy-done.6, ...), custom_call_target="tpu_custom_call" | custom-call | flops 3288334336 | bytes 12582912 | tf_op jit(solution)/shard_map/pallas_call | solution.py:200
  149.7 12.6 %shard_map.52 = (bf16[32,16,1024]{2,1,0:T(8,128)(2,1)}, bf16[32,16,1024]{2,1,0:T(8,128)(2,1)}) custom-call(s32[3]{0:T(128)} %pad_add_fusion.place_ref, bf16[1024,1792]{1,0:T(8,128)(2,1)} %bitcast.4.near_hbm, bf16[1024,1792]{1,0:T(8,128)(2,1)} %collective-permute-done.far_hbm, f32[2,896,512]{2,1,0:T(8,128)} %shard_map.51.mixed_hbm, ...), custom_call_target="tpu_custom_call" | custom-call | flops 5167382528 | bytes 16777216 | tf_op jit(solution)/shard_map/pallas_call | solution.py:219
  162.3 1.3 collective-permute-start.19
  163.7 2.5 %collective-permute-done.19 = bf16[32,16,1024]{2,1,0:T(8,128)(2,1)S(1)} collective-permute-done((bf16[32,16,1024]{2,1,0:T(8,128)(2,1)}, bf16[32,16,1024]{2,1,0:T(8,128)(2,1)S(1)}, u32[]{:S(2)}, u32[]{:S(2)}) %collective-permute-start.19) | collective-permute-done | bytes 1048608 | tf_op jit(solution)/shard_map/ppermute | solution.py:24
  166.2 2.6 %add_convert_fusion = bf16[32,16,1024]{2,1,0:T(8,128)(2,1)} fusion(bf16[32,16,1024]{2,1,0:T(8,128)(2,1)S(1)} %collective-permute-done.19, bf16[32,16,1024]{2,1,0:T(8,128)(2,1)} %get-tuple-element.4), kind=kLoop, calls=%fused_computation | loop fusion | flops 2097152 | bytes 3145728 | tf_op jit(solution)/shard_map/convert_element_type | solution.py:279
  168.8 5.2 %all-to-all-start.1 = ((bf16[32,16,1024]{2,1,0:T(8,128)(2,1)}), bf16[32,16,1024]{2,1,0:T(8,128)(2,1)S(1)}, u32[]{:S(2)}, u32[]{:S(2)}) async-start(bf16[32,16,1024]{2,1,0:T(8,128)(2,1)} %add_convert_fusion), calls=%async_computation.1 | async-start | bytes 2097152 | tf_op jit(solution)/shard_map/all_to_all | solution.py:280
  174.1 16.8 %all-to-all-done.1 = bf16[32,16,1024]{2,1,0:T(8,128)(2,1)S(1)} async-done(((bf16[32,16,1024]{2,1,0:T(8,128)(2,1)}), bf16[32,16,1024]{2,1,0:T(8,128)(2,1)S(1)}, u32[]{:S(2)}, u32[]{:S(2)}) %all-to-all-start.1) | async-done | bytes 1048608 | tf_op jit(solution)/shard_map/all_to_all | solution.py:280
  191.8 1.1 bitcast_multiply_fusion
  (56 shorter events, 6.7 us)
Async XLA Ops:
  0.6 58.8 %copy-start = (bf16[112,3584]{1,0:T(8,128)(2,1)S(1)}, bf16[112,3584]{1,0:T(8,128)(2,1)}, u32[]{:S(2)}) copy-start(bf16[112,3584]{1,0:T(8,128)(2,1)} %param.4) | copy-start | bytes 2408452
  59.4 90.3 %collective-permute-start = (bf16[1024,1792]{1,0:T(8,128)(2,1)}, bf16[1024,1792]{1,0:T(8,128)(2,1)}, u32[]{:S(2)}, u32[]{:S(2)}) collective-permute-start(bf16[1024,1792]{1,0:T(8,128)(2,1)} %bitcast.4.near_hbm), channel_id=1, source_target_pairs={{0,1},{1,0},{2,3},{3,2},{4,5},{5,4},{6,7},{7,6},{8,9},{9,8},{10,11... | collective-permute-start | bytes 11010056 | tf_op jit(solution)/shard_map/ppermute | solution.py:24
  59.4 6.5 %collective-permute-start.1 = (bf16[112,896]{1,0:T(8,128)(2,1)S(1)}, bf16[112,896]{1,0:T(8,128)(2,1)S(1)}, u32[]{:S(2)}, u32[]{:S(2)}) collective-permute-start(bf16[112,896]{1,0:T(8,128)(2,1)S(1)} %constant_dynamic-slice_fusion), channel_id=1, source_target_pairs={{0,0},{1,8},{8,9},{9,1},{16,16},{17,24},{24,25},{25,17},{2,2},{3,1... | collective-permute-start | bytes 602120 | tf_op jit(solution)/shard_map/ppermute | solution.py:256
  61.9 7.0 %collective-permute-start.2 = (bf16[112,896]{1,0:T(8,128)(2,1)S(1)}, bf16[112,896]{1,0:T(8,128)(2,1)S(1)}, u32[]{:S(2)}, u32[]{:S(2)}) collective-permute-start(bf16[112,896]{1,0:T(8,128)(2,1)S(1)} %constant_dynamic-slice_fusion), channel_id=1, source_target_pairs={{0,8},{1,0},{8,1},{9,9},{16,24},{17,16},{24,17},{25,25},{2,10},{3,... | collective-permute-start | bytes 602120 | tf_op jit(solution)/shard_map/ppermute | solution.py:257
  69.0 72.4 %copy-start.1 = (bf16[224,896]{1,0:T(8,128)(2,1)}, bf16[224,896]{1,0:T(8,128)(2,1)S(1)}, u32[]{:S(2)}) copy-start(bf16[224,896]{1,0:T(8,128)(2,1)S(1)} %pad_maximum_fusion.refs_0_) | copy-start | bytes 1204228
  69.0 11.4 %collective-permute-start.3 = (bf16[224,896]{1,0:T(8,128)(2,1)S(1)}, bf16[224,896]{1,0:T(8,128)(2,1)S(1)}, u32[]{:S(2)}, u32[]{:S(2)}) collective-permute-start(bf16[224,896]{1,0:T(8,128)(2,1)S(1)} %pad_maximum_fusion.refs_0_), channel_id=1, source_target_pairs={{0,6},{2,0},{4,2},{6,4},{1,7},{3,1},{5,3},{7,5},{8,14},{10,8},{12,... | collective-permute-start | bytes 1204232 | tf_op jit(solution)/shard_map/ppermute | solution.py:20
  70.3 12.6 %collective-permute-start.4 = (bf16[224,896]{1,0:T(8,128)(2,1)S(1)}, bf16[224,896]{1,0:T(8,128)(2,1)S(1)}, u32[]{:S(2)}, u32[]{:S(2)}) collective-permute-start(bf16[224,896]{1,0:T(8,128)(2,1)S(1)} %pad_maximum_fusion.refs_0_), channel_id=1, source_target_pairs={{0,4},{2,6},{4,0},{6,2},{1,5},{3,7},{5,1},{7,3},{8,12},{10,14},{12... | collective-permute-start | bytes 1204232 | tf_op jit(solution)/shard_map/ppermute | solution.py:20
  71.4 19.6 %collective-permute-start.5 = (bf16[224,896]{1,0:T(8,128)(2,1)S(1)}, bf16[224,896]{1,0:T(8,128)(2,1)S(1)}, u32[]{:S(2)}, u32[]{:S(2)}) collective-permute-start(bf16[224,896]{1,0:T(8,128)(2,1)S(1)} %pad_maximum_fusion.refs_0_), channel_id=1, source_target_pairs={{0,2},{2,4},{4,6},{6,0},{1,3},{3,5},{5,7},{7,1},{8,10},{10,12},{12... | collective-permute-start | bytes 1204232 | tf_op jit(solution)/shard_map/ppermute | solution.py:20
  71.4 20.8 %collective-permute-start.10 = (bf16[224,896]{1,0:T(8,128)(2,1)S(1)}, bf16[224,896]{1,0:T(8,128)(2,1)S(1)}, u32[]{:S(2)}, u32[]{:S(2)}) collective-permute-start(bf16[224,896]{1,0:T(8,128)(2,1)S(1)} %pad_maximum_fusion.refs_0_), channel_id=1, source_target_pairs={{0,32},{32,64},{64,96},{96,0},{1,33},{33,65},{65,97},{97,1},{2,34}... | collective-permute-start | bytes 1204232 | tf_op jit(solution)/shard_map/ppermute | solution.py:20
  80.4 61.0 %copy-start.4 = (bf16[224,896]{1,0:T(8,128)(2,1)}, bf16[224,896]{1,0:T(8,128)(2,1)S(1)}, u32[]{:S(2)}) copy-start(bf16[224,896]{1,0:T(8,128)(2,1)S(1)} %collective-permute-done.3.refs_1_) | copy-start | bytes 1204228
  80.4 13.2 %collective-permute-start.6 = (bf16[224,896]{1,0:T(8,128)(2,1)S(1)}, bf16[224,896]{1,0:T(8,128)(2,1)S(1)}, u32[]{:S(2)}, u32[]{:S(2)}) collective-permute-start(bf16[224,896]{1,0:T(8,128)(2,1)S(1)} %pad_maximum_fusion.refs_0_), channel_id=1, source_target_pairs={{0,96},{32,0},{64,32},{96,64},{1,97},{33,1},{65,33},{97,65},{2,98}... | collective-permute-start | bytes 1204232 | tf_op jit(solution)/shard_map/ppermute | solution.py:20
  82.9 58.6 %copy-start.5 = (bf16[224,896]{1,0:T(8,128)(2,1)}, bf16[224,896]{1,0:T(8,128)(2,1)S(1)}, u32[]{:S(2)}) copy-start(bf16[224,896]{1,0:T(8,128)(2,1)S(1)} %collective-permute-done.4.refs_2_) | copy-start | bytes 1204228
  82.9 17.7 %collective-permute-start.7 = (bf16[224,896]{1,0:T(8,128)(2,1)S(1)}, bf16[224,896]{1,0:T(8,128)(2,1)}, u32[]{:S(2)}, u32[]{:S(2)}) collective-permute-start(bf16[224,896]{1,0:T(8,128)(2,1)S(1)} %collective-permute-done.3.refs_1_), channel_id=1, source_target_pairs={{0,96},{32,0},{64,32},{96,64},{1,97},{33,1},{65,33},{97,65},{2,98}... | collective-permute-start | bytes 1204232 | tf_op jit(solution)/shard_map/ppermute | solution.py:20
  91.0 50.5 %copy-start.6 = (bf16[224,896]{1,0:T(8,128)(2,1)}, bf16[224,896]{1,0:T(8,128)(2,1)S(1)}, u32[]{:S(2)}) copy-start(bf16[224,896]{1,0:T(8,128)(2,1)S(1)} %collective-permute-done.5.refs_3_) | copy-start | bytes 1204228
  91.0 11.7 %collective-permute-start.12 = (bf16[224,896]{1,0:T(8,128)(2,1)S(1)}, bf16[224,896]{1,0:T(8,128)(2,1)S(1)}, u32[]{:S(2)}, u32[]{:S(2)}) collective-permute-start(bf16[224,896]{1,0:T(8,128)(2,1)S(1)} %collective-permute-done.4.refs_2_), channel_id=1, source_target_pairs={{0,32},{32,64},{64,96},{96,0},{1,33},{33,65},{65,97},{97,1},{2,34}... | collective-permute-start | bytes 1204232 | tf_op jit(solution)/shard_map/ppermute | solution.py:20
  92.2 36.3 %copy-start.7 = (bf16[224,896]{1,0:T(8,128)(2,1)}, bf16[224,896]{1,0:T(8,128)(2,1)S(1)}, u32[]{:S(2)}) copy-start(bf16[224,896]{1,0:T(8,128)(2,1)S(1)} %collective-permute-done.10.refs_8_) | copy-start | bytes 1204228
  92.2 15.8 %collective-permute-start.8 = (bf16[224,896]{1,0:T(8,128)(2,1)S(1)}, bf16[224,896]{1,0:T(8,128)(2,1)S(1)}, u32[]{:S(2)}, u32[]{:S(2)}) collective-permute-start(bf16[224,896]{1,0:T(8,128)(2,1)S(1)} %collective-permute-done.4.refs_2_), channel_id=1, source_target_pairs={{0,96},{32,0},{64,32},{96,64},{1,97},{33,1},{65,33},{97,65},{2,98}... | collective-permute-start | bytes 1204232 | tf_op jit(solution)/shard_map/ppermute | solution.py:20
  93.7 26.2 %copy-start.8 = (bf16[224,896]{1,0:T(8,128)(2,1)}, bf16[224,896]{1,0:T(8,128)(2,1)S(1)}, u32[]{:S(2)}) copy-start(bf16[224,896]{1,0:T(8,128)(2,1)S(1)} %collective-permute-done.6.refs_4_) | copy-start | bytes 1204228
  93.7 17.7 %collective-permute-start.13 = (bf16[224,896]{1,0:T(8,128)(2,1)S(1)}, bf16[224,896]{1,0:T(8,128)(2,1)}, u32[]{:S(2)}, u32[]{:S(2)}) collective-permute-start(bf16[224,896]{1,0:T(8,128)(2,1)S(1)} %collective-permute-done.5.refs_3_), channel_id=1, source_target_pairs={{0,32},{32,64},{64,96},{96,0},{1,33},{33,65},{65,97},{97,1},{2,34}... | collective-permute-start | bytes 1204232 | tf_op jit(solution)/shard_map/ppermute | solution.py:20
  100.6 19.2 %collective-permute-start.11 = (bf16[224,896]{1,0:T(8,128)(2,1)S(1)}, bf16[224,896]{1,0:T(8,128)(2,1)S(1)}, u32[]{:S(2)}, u32[]{:S(2)}) collective-permute-start(bf16[224,896]{1,0:T(8,128)(2,1)S(1)} %collective-permute-done.3.refs_1_), channel_id=1, source_target_pairs={{0,32},{32,64},{64,96},{96,0},{1,33},{33,65},{65,97},{97,1},{2,34}... | collective-permute-start | bytes 1204232 | tf_op jit(solution)/shard_map/ppermute | solution.py:20
  102.6 38.9 %copy-start.2 = (bf16[224,896]{1,0:T(8,128)(2,1)}, bf16[224,896]{1,0:T(8,128)(2,1)S(1)}, u32[]{:S(2)}) copy-start(bf16[224,896]{1,0:T(8,128)(2,1)S(1)} %collective-permute-done.12.refs_10_) | copy-start | bytes 1204228
  102.6 25.8 %collective-permute-start.14 = (bf16[224,896]{1,0:T(8,128)(2,1)S(1)}, bf16[224,896]{1,0:T(8,128)(2,1)S(1)}, u32[]{:S(2)}, u32[]{:S(2)}) collective-permute-start(bf16[224,896]{1,0:T(8,128)(2,1)S(1)} %collective-permute-done.10.refs_8_), channel_id=1, source_target_pairs={{0,32},{32,64},{64,96},{96,0},{1,33},{33,65},{65,97},{97,1},{2,34}... | collective-permute-start | bytes 1204232 | tf_op jit(solution)/shard_map/ppermute | solution.py:20
  108.0 33.5 %copy-start.3 = (bf16[224,896]{1,0:T(8,128)(2,1)}, bf16[224,896]{1,0:T(8,128)(2,1)S(1)}, u32[]{:S(2)}) copy-start(bf16[224,896]{1,0:T(8,128)(2,1)S(1)} %collective-permute-done.8.refs_6_) | copy-start | bytes 1204228
  108.0 20.4 %collective-permute-start.9 = (bf16[224,896]{1,0:T(8,128)(2,1)S(1)}, bf16[224,896]{1,0:T(8,128)(2,1)S(1)}, u32[]{:S(2)}, u32[]{:S(2)}) collective-permute-start(bf16[224,896]{1,0:T(8,128)(2,1)S(1)} %collective-permute-done.5.refs_3_), channel_id=1, source_target_pairs={{0,96},{32,0},{64,32},{96,64},{1,97},{33,1},{65,33},{97,65},{2,98}... | collective-permute-start | bytes 1204232 | tf_op jit(solution)/shard_map/ppermute | solution.py:20
  111.3 30.1 %collective-permute-start.15 = (bf16[224,896]{1,0:T(8,128)(2,1)}, bf16[224,896]{1,0:T(8,128)(2,1)}, u32[]{:S(2)}, u32[]{:S(2)}) collective-permute-start(bf16[224,896]{1,0:T(8,128)(2,1)} %collective-permute-done.7.refs_5_), channel_id=1, source_target_pairs={{0,96},{32,0},{64,32},{96,64},{1,97},{33,1},{65,33},{97,65},{2,98}... | collective-permute-start | bytes 1204232 | tf_op jit(solution)/shard_map/ppermute | solution.py:20
  119.8 0.8 copy-start.9
  120.6 20.9 %collective-permute-start.18 = (bf16[224,896]{1,0:T(8,128)(2,1)}, bf16[224,896]{1,0:T(8,128)(2,1)}, u32[]{:S(2)}, u32[]{:S(2)}) collective-permute-start(bf16[224,896]{1,0:T(8,128)(2,1)} %collective-permute-done.13.refs_11_), channel_id=1, source_target_pairs={{0,32},{32,64},{64,96},{96,0},{1,33},{33,65},{65,97},{97,1},{2,34}... | collective-permute-start | bytes 1204232 | tf_op jit(solution)/shard_map/ppermute | solution.py:20
  128.4 13.0 %collective-permute-start.16 = (bf16[112,896]{1,0:T(8,128)(2,1)}, bf16[112,896]{1,0:T(8,128)(2,1)}, u32[]{:S(2)}, u32[]{:S(2)}) collective-permute-start(bf16[112,896]{1,0:T(8,128)(2,1)} %slice.18), channel_id=1, source_target_pairs={{0,32},{32,64},{64,96},{96,0},{1,33},{33,65},{65,97},{97,1},{2,34}... | collective-permute-start | bytes 602120 | tf_op jit(solution)/shard_map/ppermute | solution.py:20
  129.9 11.5 %collective-permute-start.17 = (bf16[112,896]{1,0:T(8,128)(2,1)S(1)}, bf16[112,896]{1,0:T(8,128)(2,1)}, u32[]{:S(2)}, u32[]{:S(2)}) collective-permute-start(bf16[112,896]{1,0:T(8,128)(2,1)S(1)} %slice.19), channel_id=1, source_target_pairs={{0,96},{32,0},{64,32},{96,64},{1,97},{33,1},{65,33},{97,65},{2,98}... | collective-permute-start | bytes 602120 | tf_op jit(solution)/shard_map/ppermute | solution.py:20
  162.3 3.8 %collective-permute-start.19 = (bf16[32,16,1024]{2,1,0:T(8,128)(2,1)}, bf16[32,16,1024]{2,1,0:T(8,128)(2,1)S(1)}, u32[]{:S(2)}, u32[]{:S(2)}) collective-permute-start(bf16[32,16,1024]{2,1,0:T(8,128)(2,1)} %get-tuple-element.5), channel_id=1, source_target_pairs={{0,1},{1,0},{2,3},{3,2},{4,5},{5,4},{6,7},{7,6},{8,9},{9,8},{10,11... | collective-permute-start | bytes 3145736 | tf_op jit(solution)/shard_map/ppermute | solution.py:24
  166.2 7.8 %copy-start.12 = (s32[8,32]{1,0:T(8,128)S(1)}, s32[8,32]{1,0:T(8,128)}, u32[]{:S(2)}) copy-start(s32[8,32]{1,0:T(8,128)} %valid_ref.1) | copy-start | bytes 3076
  168.8 22.1 %all-to-all-start.1 = ((bf16[32,16,1024]{2,1,0:T(8,128)(2,1)}), bf16[32,16,1024]{2,1,0:T(8,128)(2,1)S(1)}, u32[]{:S(2)}, u32[]{:S(2)}) async-start(bf16[32,16,1024]{2,1,0:T(8,128)(2,1)} %add_convert_fusion), calls=%async_computation.1 | async-start | bytes 2097152 | tf_op jit(solution)/shard_map/all_to_all | solution.py:280
  (2 other events, 1.5 us)

commit v5 on v4

--- a/solution.py
+++ b/solution.py
@@ -170,10 +170,10 @@
     c = place_ref[2]
     block = 128
     part = kept_ref.shape[1]
+    groups = block // (2 * part)
     for i in range(slots // block):
         at = slice(i * block, (i + 1) * block)
         skew = table_ref[at, :] - table_ref[:, at].T
-        groups = block // (2 * part)
         skew = skew.reshape(groups, 2, part, slots)
         low, high = skew[:, 0], skew[:, 1]
         at = slice(i * groups, (i + 1) * groups)
@@ -215,14 +215,14 @@
             flops=2 * quarter * half * slots, bytes_accessed=12 * 2**20, transcendentals=0
         ),
     )(place, near, *pieces)
-    part = slots // 64
+    part = slots // 32
     return pl.pallas_call(
         far_kernel,
         in_specs=[scalars] + [in_hbm()] * (COUNT + 3),
         out_specs=[whole(), whole()],
         out_shape=[
-            jax.ShapeDtypeStruct((32, part, slots), jnp.bfloat16),
-            jax.ShapeDtypeStruct((32, part, slots), jnp.bfloat16),
+            jax.ShapeDtypeStruct((16, part, slots), jnp.bfloat16),
+            jax.ShapeDtypeStruct((16, part, slots), jnp.bfloat16),
         ],
         scratch_shapes=[
             pltpu.VMEM((quarter, half), near.dtype),
@@ -277,9 +277,8 @@
     place = jnp.stack([x, z, c]).astype(jnp.int32)
     kept, given = score_parts(place, near, far, [*chain, *above, *below, *across])
     half_scores = (kept.astype(jnp.float32) + swap_cores(given).astype(jnp.float32)).astype(jnp.bfloat16)
-    returned = lax.all_to_all(half_scores, RESP_AXES, 0, 0, tiled=True)
-    returned = returned.astype(jnp.float32).reshape(2, 2, 4, 2, block_rows // 2, slots)
-    scores = (returned[0] + returned[1]).reshape(prompts, block_rows, slots)
+    returned = lax.all_to_all(half_scores, ("y", "z"), 0, 0, tiled=True).astype(jnp.float32)
+    scores = returned[:prompts] + returned[prompts:]
 
     valid_rows = valid_mask.astype(jnp.float32)
     counts = jnp.sum((scores > HIDDEN_TEST).astype(jnp.float32), axis=2)

time: 194 us -> 193 us (level)
  no operation moved by 1% of the time
where the time goes in v5:
time: 193 us; the launch traced here: 191 us
  waiting for transfers between devices  73 us (38%)
  blocking collectives  55 us (28%)
  starting transfers between devices  29.2 us (15%)
  Pallas kernels  24.6 us (13%)
  other arithmetic  5.49 us (3%)
  local copies, waits for them, and re-layouts  3 us (2%)
    all_to_all x1, blocking collectives, scored(): lax.all_to_all(outgoing, RESP_AXES, 0, 0, tiled=True)  55 us
    ppermute x16, waiting for transfers between devices, ring(): return lax.ppermute(value, axis, [(i, (i + step) % 4) for i in range(4)])  49.8 us
    ppermute x16, starting transfers between devices, ring(): return lax.ppermute(value, axis, [(i, (i + step) % 4) for i in range(4)])  19 us
    all_to_all x1, waiting for transfers between devices, scored(): lax.all_to_all(half_scores, ('y', 'z'), 0, 0, tiled=True)  15.6 us
    pallas_call x1, Pallas kernels, score_parts(): pl.pallas_call(far_kernel, in_specs=[scalars] + [in_hbm()] * (COUNT + 3),...  12.6 us
    pallas_call x1, Pallas kernels, score_parts(): pl.pallas_call(near_kernel, in_specs=[scalars] + [in_hbm()] * (COUNT + 1)...  8.21 us
    all_to_all x1, starting transfers between devices, scored(): lax.all_to_all(half_scores, ('y', 'z'), 0, 0, tiled=True)  4.48 us
  transfers between devices with their start and end apart: 21, of which 13 were waited for; matrix products, arithmetic and copies ran while one was open for 1% of the time, Pallas kernels for 4%

profile of v5, /device:TPU:1, one launch (start us, length us, event | category | flops | bytes accessed | tf_op | source)
XLA Modules:
  0.0 191.2 jit_solution(18185010952811888420)
XLA Ops:
  0.6 3.8 %shard_map.50 = bf16[2,2,4,2,32,1792]{5,4,3,2,1,0:T(8,128)(2,1)} custom-call(bf16[8,32,3584]{2,1,0:T(8,128)(2,1)} %rows_ref.1, s32[8,32]{1,0:T(8,128)} %valid_ref.1), custom_call_target="tpu_custom_call" | custom-call | tf_op jit(solution)/shard_map/pallas_call | solution.py:68
  4.4 55.0 %all_to_all.10 = bf16[32,32,1792]{2,1,0:T(8,128)(2,1)} all-to-all(bf16[32,32,1792]{2,1,0:T(8,128)(2,1)} %bitcast.5), channel_id=1, replica_groups=mesh['x'=4,'y'=4,'z'=4,'c'=2] {'y','z','c'}, dimensions={0} | all-to-all | bytes 7340032 | tf_op jit(solution)/shard_map/all_to_all | solution.py:264
  59.4 2.5 %collective-permute-start.1 = (bf16[112,896]{1,0:T(8,128)(2,1)S(1)}, bf16[112,896]{1,0:T(8,128)(2,1)S(1)}, u32[]{:S(2)}, u32[]{:S(2)}) collective-permute-start(bf16[112,896]{1,0:T(8,128)(2,1)S(1)} %constant_dynamic-slice_fusion), channel_id=1, source_target_pairs={{0,0},{1,8},{8,9},{9,1},{16,16},{17,24},{24,25},{25,17},{2,2},{3,1... | collective-permute-start | bytes 602120 | tf_op jit(solution)/shard_map/ppermute | solution.py:256
  61.9 1.9 %collective-permute-start.2 = (bf16[112,896]{1,0:T(8,128)(2,1)S(1)}, bf16[112,896]{1,0:T(8,128)(2,1)S(1)}, u32[]{:S(2)}, u32[]{:S(2)}) collective-permute-start(bf16[112,896]{1,0:T(8,128)(2,1)S(1)} %constant_dynamic-slice_fusion), channel_id=1, source_target_pairs={{0,8},{1,0},{8,1},{9,9},{16,24},{17,16},{24,17},{25,25},{2,10},{3,... | collective-permute-start | bytes 602120 | tf_op jit(solution)/shard_map/ppermute | solution.py:257
  63.9 2.0 %collective-permute-done.1 = bf16[112,896]{1,0:T(8,128)(2,1)S(1)} collective-permute-done((bf16[112,896]{1,0:T(8,128)(2,1)S(1)}, bf16[112,896]{1,0:T(8,128)(2,1)S(1)}, u32[]{:S(2)}, u32[]{:S(2)}) %collective-permute-start.1) | collective-permute-done | bytes 200736 | tf_op jit(solution)/shard_map/ppermute | solution.py:256
  65.9 3.0 %collective-permute-done.2 = bf16[112,896]{1,0:T(8,128)(2,1)S(1)} collective-permute-done((bf16[112,896]{1,0:T(8,128)(2,1)S(1)}, bf16[112,896]{1,0:T(8,128)(2,1)S(1)}, u32[]{:S(2)}, u32[]{:S(2)}) %collective-permute-start.2) | collective-permute-done | bytes 200736 | tf_op jit(solution)/shard_map/ppermute | solution.py:257
  69.0 1.3 collective-permute-start.3
  70.3 1.0 collective-permute-start.4
  71.4 1.2 collective-permute-start.10
  72.6 7.8 %collective-permute-done.3.refs_1_ = bf16[224,896]{1,0:T(8,128)(2,1)S(1)} collective-permute-done((bf16[224,896]{1,0:T(8,128)(2,1)S(1)}, bf16[224,896]{1,0:T(8,128)(2,1)S(1)}, u32[]{:S(2)}, u32[]{:S(2)}) %collective-permute-start.3) | collective-permute-done | bytes 401440 | tf_op jit(solution)/shard_map/ppermute | solution.py:20
  80.4 2.5 %collective-permute-start.6 = (bf16[224,896]{1,0:T(8,128)(2,1)S(1)}, bf16[224,896]{1,0:T(8,128)(2,1)S(1)}, u32[]{:S(2)}, u32[]{:S(2)}) collective-permute-start(bf16[224,896]{1,0:T(8,128)(2,1)S(1)} %pad_maximum_fusion.refs_0_), channel_id=1, source_target_pairs={{0,96},{32,0},{64,32},{96,64},{1,97},{33,1},{65,33},{97,65},{2,98}... | collective-permute-start | bytes 1204232 | tf_op jit(solution)/shard_map/ppermute | solution.py:20
  82.9 2.5 %collective-permute-start.7 = (bf16[224,896]{1,0:T(8,128)(2,1)S(1)}, bf16[224,896]{1,0:T(8,128)(2,1)}, u32[]{:S(2)}, u32[]{:S(2)}) collective-permute-start(bf16[224,896]{1,0:T(8,128)(2,1)S(1)} %collective-permute-done.3.refs_1_), channel_id=1, source_target_pairs={{0,96},{32,0},{64,32},{96,64},{1,97},{33,1},{65,33},{97,65},{2,98}... | collective-permute-start | bytes 1204232 | tf_op jit(solution)/shard_map/ppermute | solution.py:20
  85.4 5.6 %collective-permute-done.5.refs_3_ = bf16[224,896]{1,0:T(8,128)(2,1)S(1)} collective-permute-done((bf16[224,896]{1,0:T(8,128)(2,1)S(1)}, bf16[224,896]{1,0:T(8,128)(2,1)S(1)}, u32[]{:S(2)}, u32[]{:S(2)}) %collective-permute-start.5) | collective-permute-done | bytes 401440 | tf_op jit(solution)/shard_map/ppermute | solution.py:20
  91.0 1.2 collective-permute-start.12
  92.2 1.5 collective-permute-start.8
  93.7 6.9 %collective-permute-done.7.refs_5_ = bf16[224,896]{1,0:T(8,128)(2,1)} collective-permute-done((bf16[224,896]{1,0:T(8,128)(2,1)S(1)}, bf16[224,896]{1,0:T(8,128)(2,1)}, u32[]{:S(2)}, u32[]{:S(2)}) %collective-permute-start.7) | collective-permute-done | bytes 401440 | tf_op jit(solution)/shard_map/ppermute | solution.py:20
  101.5 1.1 collective-permute-done.12.refs_10_
  102.8 5.2 %collective-permute-done.8.refs_6_ = bf16[224,896]{1,0:T(8,128)(2,1)S(1)} collective-permute-done((bf16[224,896]{1,0:T(8,128)(2,1)S(1)}, bf16[224,896]{1,0:T(8,128)(2,1)S(1)}, u32[]{:S(2)}, u32[]{:S(2)}) %collective-permute-start.8) | collective-permute-done | bytes 401440 | tf_op jit(solution)/shard_map/ppermute | solution.py:20
  108.0 3.1 %collective-permute-start.9 = (bf16[224,896]{1,0:T(8,128)(2,1)S(1)}, bf16[224,896]{1,0:T(8,128)(2,1)S(1)}, u32[]{:S(2)}, u32[]{:S(2)}) collective-permute-start(bf16[224,896]{1,0:T(8,128)(2,1)S(1)} %collective-permute-done.5.refs_3_), channel_id=1, source_target_pairs={{0,96},{32,0},{64,32},{96,64},{1,97},{33,1},{65,33},{97,65},{2,98}... | collective-permute-start | bytes 1204232 | tf_op jit(solution)/shard_map/ppermute | solution.py:20
  111.3 1.6 collective-permute-start.15
  112.9 6.9 %collective-permute-done.11.refs_9_ = bf16[224,896]{1,0:T(8,128)(2,1)S(1)} collective-permute-done((bf16[224,896]{1,0:T(8,128)(2,1)S(1)}, bf16[224,896]{1,0:T(8,128)(2,1)S(1)}, u32[]{:S(2)}, u32[]{:S(2)}) %collective-permute-start.11) | collective-permute-done | bytes 401440 | tf_op jit(solution)/shard_map/ppermute | solution.py:20
  121.4 7.0 %collective-permute-done.14.refs_12_ = bf16[224,896]{1,0:T(8,128)(2,1)S(1)} collective-permute-done((bf16[224,896]{1,0:T(8,128)(2,1)S(1)}, bf16[224,896]{1,0:T(8,128)(2,1)S(1)}, u32[]{:S(2)}, u32[]{:S(2)}) %collective-permute-start.14) | collective-permute-done | bytes 401440 | tf_op jit(solution)/shard_map/ppermute | solution.py:20
  129.9 1.9 %collective-permute-start.17 = (bf16[112,896]{1,0:T(8,128)(2,1)S(1)}, bf16[112,896]{1,0:T(8,128)(2,1)}, u32[]{:S(2)}, u32[]{:S(2)}) collective-permute-start(bf16[112,896]{1,0:T(8,128)(2,1)S(1)} %slice.17), channel_id=1, source_target_pairs={{0,96},{32,0},{64,32},{96,64},{1,97},{33,1},{65,33},{97,65},{2,98}... | collective-permute-start | bytes 602120 | tf_op jit(solution)/shard_map/ppermute | solution.py:20
  132.5 9.0 %collective-permute-done.16.refs_14_ = bf16[112,896]{1,0:T(8,128)(2,1)} collective-permute-done((bf16[112,896]{1,0:T(8,128)(2,1)}, bf16[112,896]{1,0:T(8,128)(2,1)}, u32[]{:S(2)}, u32[]{:S(2)}) %collective-permute-start.16) | collective-permute-done | bytes 200736 | tf_op jit(solution)/shard_map/ppermute | solution.py:20
  141.5 8.2 %shard_map.51.mixed_hbm = f32[2,896,512]{2,1,0:T(8,128)} custom-call(s32[3]{0:T(128)} %pad_add_fusion.place_ref, bf16[1024,1792]{1,0:T(8,128)(2,1)} %bitcast.4.near_hbm, bf16[224,896]{1,0:T(8,128)(2,1)} %copy-done.1, bf16[224,896]{1,0:T(8,128)(2,1)} %copy-done.4, bf16[224,896]{1,0:T(8,128)(2,1)} %copy-done.5, bf16[224,896]{1,0:T(8,128)(2,1)} %copy-done.6, ...), custom_call_target="tpu_custom_call" | custom-call | flops 3288334336 | bytes 12582912 | tf_op jit(solution)/shard_map/pallas_call | solution.py:200
  149.7 12.6 %shard_map.52 = (bf16[16,32,1024]{2,1,0:T(8,128)(2,1)}, bf16[16,32,1024]{2,1,0:T(8,128)(2,1)}) custom-call(s32[3]{0:T(128)} %pad_add_fusion.place_ref, bf16[1024,1792]{1,0:T(8,128)(2,1)} %bitcast.4.near_hbm, bf16[1024,1792]{1,0:T(8,128)(2,1)} %collective-permute-done.far_hbm, f32[2,896,512]{2,1,0:T(8,128)} %shard_map.51.mixed_hbm, ...), custom_call_target="tpu_custom_call" | custom-call | flops 5167382528 | bytes 16777216 | tf_op jit(solution)/shard_map/pallas_call | solution.py:219
  162.4 1.3 collective-permute-start.19
  163.7 2.5 %collective-permute-done.19 = bf16[16,32,1024]{2,1,0:T(8,128)(2,1)S(1)} collective-permute-done((bf16[16,32,1024]{2,1,0:T(8,128)(2,1)}, bf16[16,32,1024]{2,1,0:T(8,128)(2,1)S(1)}, u32[]{:S(2)}, u32[]{:S(2)}) %collective-permute-start.19) | collective-permute-done | bytes 1048608 | tf_op jit(solution)/shard_map/ppermute | solution.py:24
  166.2 2.6 %add_convert_fusion = bf16[16,32,1024]{2,1,0:T(8,128)(2,1)} fusion(bf16[16,32,1024]{2,1,0:T(8,128)(2,1)S(1)} %collective-permute-done.19, bf16[16,32,1024]{2,1,0:T(8,128)(2,1)} %get-tuple-element.4), kind=kLoop, calls=%fused_computation | loop fusion | flops 2097152 | bytes 3145728 | tf_op jit(solution)/shard_map/convert_element_type | solution.py:279
  168.8 4.5 %all-to-all-start.1 = ((bf16[16,32,1024]{2,1,0:T(8,128)(2,1)}), bf16[16,32,1024]{2,1,0:T(8,128)(2,1)S(1)}, u32[]{:S(2)}, u32[]{:S(2)}) async-start(bf16[16,32,1024]{2,1,0:T(8,128)(2,1)} %add_convert_fusion), calls=%async_computation.1 | async-start | bytes 2097152 | tf_op jit(solution)/shard_map/all_to_all | solution.py:280
  173.3 15.6 %all-to-all-done.1 = bf16[16,32,1024]{2,1,0:T(8,128)(2,1)S(1)} async-done(((bf16[16,32,1024]{2,1,0:T(8,128)(2,1)}), bf16[16,32,1024]{2,1,0:T(8,128)(2,1)S(1)}, u32[]{:S(2)}, u32[]{:S(2)}) %all-to-all-start.1) | async-done | bytes 1048608 | tf_op jit(solution)/shard_map/all_to_all | solution.py:280
  189.2 1.4 fusion
  (51 shorter events, 5.9 us)
Async XLA Ops:
  0.6 58.8 %copy-start = (bf16[112,3584]{1,0:T(8,128)(2,1)S(1)}, bf16[112,3584]{1,0:T(8,128)(2,1)}, u32[]{:S(2)}) copy-start(bf16[112,3584]{1,0:T(8,128)(2,1)} %param.4) | copy-start | bytes 2408452
  59.4 90.3 %collective-permute-start = (bf16[1024,1792]{1,0:T(8,128)(2,1)}, bf16[1024,1792]{1,0:T(8,128)(2,1)}, u32[]{:S(2)}, u32[]{:S(2)}) collective-permute-start(bf16[1024,1792]{1,0:T(8,128)(2,1)} %bitcast.4.near_hbm), channel_id=1, source_target_pairs={{0,1},{1,0},{2,3},{3,2},{4,5},{5,4},{6,7},{7,6},{8,9},{9,8},{10,11... | collective-permute-start | bytes 11010056 | tf_op jit(solution)/shard_map/ppermute | solution.py:24
  59.4 6.5 %collective-permute-start.1 = (bf16[112,896]{1,0:T(8,128)(2,1)S(1)}, bf16[112,896]{1,0:T(8,128)(2,1)S(1)}, u32[]{:S(2)}, u32[]{:S(2)}) collective-permute-start(bf16[112,896]{1,0:T(8,128)(2,1)S(1)} %constant_dynamic-slice_fusion), channel_id=1, source_target_pairs={{0,0},{1,8},{8,9},{9,1},{16,16},{17,24},{24,25},{25,17},{2,2},{3,1... | collective-permute-start | bytes 602120 | tf_op jit(solution)/shard_map/ppermute | solution.py:256
  61.9 7.0 %collective-permute-start.2 = (bf16[112,896]{1,0:T(8,128)(2,1)S(1)}, bf16[112,896]{1,0:T(8,128)(2,1)S(1)}, u32[]{:S(2)}, u32[]{:S(2)}) collective-permute-start(bf16[112,896]{1,0:T(8,128)(2,1)S(1)} %constant_dynamic-slice_fusion), channel_id=1, source_target_pairs={{0,8},{1,0},{8,1},{9,9},{16,24},{17,16},{24,17},{25,25},{2,10},{3,... | collective-permute-start | bytes 602120 | tf_op jit(solution)/shard_map/ppermute | solution.py:257
  69.0 72.4 %copy-start.1 = (bf16[224,896]{1,0:T(8,128)(2,1)}, bf16[224,896]{1,0:T(8,128)(2,1)S(1)}, u32[]{:S(2)}) copy-start(bf16[224,896]{1,0:T(8,128)(2,1)S(1)} %pad_maximum_fusion.refs_0_) | copy-start | bytes 1204228
  69.0 11.4 %collective-permute-start.3 = (bf16[224,896]{1,0:T(8,128)(2,1)S(1)}, bf16[224,896]{1,0:T(8,128)(2,1)S(1)}, u32[]{:S(2)}, u32[]{:S(2)}) collective-permute-start(bf16[224,896]{1,0:T(8,128)(2,1)S(1)} %pad_maximum_fusion.refs_0_), channel_id=1, source_target_pairs={{0,6},{2,0},{4,2},{6,4},{1,7},{3,1},{5,3},{7,5},{8,14},{10,8},{12,... | collective-permute-start | bytes 1204232 | tf_op jit(solution)/shard_map/ppermute | solution.py:20
  70.3 12.6 %collective-permute-start.4 = (bf16[224,896]{1,0:T(8,128)(2,1)S(1)}, bf16[224,896]{1,0:T(8,128)(2,1)S(1)}, u32[]{:S(2)}, u32[]{:S(2)}) collective-permute-start(bf16[224,896]{1,0:T(8,128)(2,1)S(1)} %pad_maximum_fusion.refs_0_), channel_id=1, source_target_pairs={{0,4},{2,6},{4,0},{6,2},{1,5},{3,7},{5,1},{7,3},{8,12},{10,14},{12... | collective-permute-start | bytes 1204232 | tf_op jit(solution)/shard_map/ppermute | solution.py:20
  71.4 19.6 %collective-permute-start.5 = (bf16[224,896]{1,0:T(8,128)(2,1)S(1)}, bf16[224,896]{1,0:T(8,128)(2,1)S(1)}, u32[]{:S(2)}, u32[]{:S(2)}) collective-permute-start(bf16[224,896]{1,0:T(8,128)(2,1)S(1)} %pad_maximum_fusion.refs_0_), channel_id=1, source_target_pairs={{0,2},{2,4},{4,6},{6,0},{1,3},{3,5},{5,7},{7,1},{8,10},{10,12},{12... | collective-permute-start | bytes 1204232 | tf_op jit(solution)/shard_map/ppermute | solution.py:20
  71.4 20.8 %collective-permute-start.10 = (bf16[224,896]{1,0:T(8,128)(2,1)S(1)}, bf16[224,896]{1,0:T(8,128)(2,1)S(1)}, u32[]{:S(2)}, u32[]{:S(2)}) collective-permute-start(bf16[224,896]{1,0:T(8,128)(2,1)S(1)} %pad_maximum_fusion.refs_0_), channel_id=1, source_target_pairs={{0,32},{32,64},{64,96},{96,0},{1,33},{33,65},{65,97},{97,1},{2,34}... | collective-permute-start | bytes 1204232 | tf_op jit(solution)/shard_map/ppermute | solution.py:20
  80.4 61.0 %copy-start.4 = (bf16[224,896]{1,0:T(8,128)(2,1)}, bf16[224,896]{1,0:T(8,128)(2,1)S(1)}, u32[]{:S(2)}) copy-start(bf16[224,896]{1,0:T(8,128)(2,1)S(1)} %collective-permute-done.3.refs_1_) | copy-start | bytes 1204228
  80.4 13.2 %collective-permute-start.6 = (bf16[224,896]{1,0:T(8,128)(2,1)S(1)}, bf16[224,896]{1,0:T(8,128)(2,1)S(1)}, u32[]{:S(2)}, u32[]{:S(2)}) collective-permute-start(bf16[224,896]{1,0:T(8,128)(2,1)S(1)} %pad_maximum_fusion.refs_0_), channel_id=1, source_target_pairs={{0,96},{32,0},{64,32},{96,64},{1,97},{33,1},{65,33},{97,65},{2,98}... | collective-permute-start | bytes 1204232 | tf_op jit(solution)/shard_map/ppermute | solution.py:20
  82.9 58.6 %copy-start.5 = (bf16[224,896]{1,0:T(8,128)(2,1)}, bf16[224,896]{1,0:T(8,128)(2,1)S(1)}, u32[]{:S(2)}) copy-start(bf16[224,896]{1,0:T(8,128)(2,1)S(1)} %collective-permute-done.4.refs_2_) | copy-start | bytes 1204228
  82.9 17.7 %collective-permute-start.7 = (bf16[224,896]{1,0:T(8,128)(2,1)S(1)}, bf16[224,896]{1,0:T(8,128)(2,1)}, u32[]{:S(2)}, u32[]{:S(2)}) collective-permute-start(bf16[224,896]{1,0:T(8,128)(2,1)S(1)} %collective-permute-done.3.refs_1_), channel_id=1, source_target_pairs={{0,96},{32,0},{64,32},{96,64},{1,97},{33,1},{65,33},{97,65},{2,98}... | collective-permute-start | bytes 1204232 | tf_op jit(solution)/shard_map/ppermute | solution.py:20
  91.0 50.5 %copy-start.6 = (bf16[224,896]{1,0:T(8,128)(2,1)}, bf16[224,896]{1,0:T(8,128)(2,1)S(1)}, u32[]{:S(2)}) copy-start(bf16[224,896]{1,0:T(8,128)(2,1)S(1)} %collective-permute-done.5.refs_3_) | copy-start | bytes 1204228
  91.0 11.7 %collective-permute-start.12 = (bf16[224,896]{1,0:T(8,128)(2,1)S(1)}, bf16[224,896]{1,0:T(8,128)(2,1)S(1)}, u32[]{:S(2)}, u32[]{:S(2)}) collective-permute-start(bf16[224,896]{1,0:T(8,128)(2,1)S(1)} %collective-permute-done.4.refs_2_), channel_id=1, source_target_pairs={{0,32},{32,64},{64,96},{96,0},{1,33},{33,65},{65,97},{97,1},{2,34}... | collective-permute-start | bytes 1204232 | tf_op jit(solution)/shard_map/ppermute | solution.py:20
  92.2 36.3 %copy-start.7 = (bf16[224,896]{1,0:T(8,128)(2,1)}, bf16[224,896]{1,0:T(8,128)(2,1)S(1)}, u32[]{:S(2)}) copy-start(bf16[224,896]{1,0:T(8,128)(2,1)S(1)} %collective-permute-done.10.refs_8_) | copy-start | bytes 1204228
  92.2 15.8 %collective-permute-start.8 = (bf16[224,896]{1,0:T(8,128)(2,1)S(1)}, bf16[224,896]{1,0:T(8,128)(2,1)S(1)}, u32[]{:S(2)}, u32[]{:S(2)}) collective-permute-start(bf16[224,896]{1,0:T(8,128)(2,1)S(1)} %collective-permute-done.4.refs_2_), channel_id=1, source_target_pairs={{0,96},{32,0},{64,32},{96,64},{1,97},{33,1},{65,33},{97,65},{2,98}... | collective-permute-start | bytes 1204232 | tf_op jit(solution)/shard_map/ppermute | solution.py:20
  93.7 26.2 %copy-start.8 = (bf16[224,896]{1,0:T(8,128)(2,1)}, bf16[224,896]{1,0:T(8,128)(2,1)S(1)}, u32[]{:S(2)}) copy-start(bf16[224,896]{1,0:T(8,128)(2,1)S(1)} %collective-permute-done.6.refs_4_) | copy-start | bytes 1204228
  93.7 17.7 %collective-permute-start.13 = (bf16[224,896]{1,0:T(8,128)(2,1)S(1)}, bf16[224,896]{1,0:T(8,128)(2,1)}, u32[]{:S(2)}, u32[]{:S(2)}) collective-permute-start(bf16[224,896]{1,0:T(8,128)(2,1)S(1)} %collective-permute-done.5.refs_3_), channel_id=1, source_target_pairs={{0,32},{32,64},{64,96},{96,0},{1,33},{33,65},{65,97},{97,1},{2,34}... | collective-permute-start | bytes 1204232 | tf_op jit(solution)/shard_map/ppermute | solution.py:20
  100.6 19.2 %collective-permute-start.11 = (bf16[224,896]{1,0:T(8,128)(2,1)S(1)}, bf16[224,896]{1,0:T(8,128)(2,1)S(1)}, u32[]{:S(2)}, u32[]{:S(2)}) collective-permute-start(bf16[224,896]{1,0:T(8,128)(2,1)S(1)} %collective-permute-done.3.refs_1_), channel_id=1, source_target_pairs={{0,32},{32,64},{64,96},{96,0},{1,33},{33,65},{65,97},{97,1},{2,34}... | collective-permute-start | bytes 1204232 | tf_op jit(solution)/shard_map/ppermute | solution.py:20
  102.6 38.9 %copy-start.2 = (bf16[224,896]{1,0:T(8,128)(2,1)}, bf16[224,896]{1,0:T(8,128)(2,1)S(1)}, u32[]{:S(2)}) copy-start(bf16[224,896]{1,0:T(8,128)(2,1)S(1)} %collective-permute-done.12.refs_10_) | copy-start | bytes 1204228
  102.6 25.8 %collective-permute-start.14 = (bf16[224,896]{1,0:T(8,128)(2,1)S(1)}, bf16[224,896]{1,0:T(8,128)(2,1)S(1)}, u32[]{:S(2)}, u32[]{:S(2)}) collective-permute-start(bf16[224,896]{1,0:T(8,128)(2,1)S(1)} %collective-permute-done.10.refs_8_), channel_id=1, source_target_pairs={{0,32},{32,64},{64,96},{96,0},{1,33},{33,65},{65,97},{97,1},{2,34}... | collective-permute-start | bytes 1204232 | tf_op jit(solution)/shard_map/ppermute | solution.py:20
  108.0 33.5 %copy-start.3 = (bf16[224,896]{1,0:T(8,128)(2,1)}, bf16[224,896]{1,0:T(8,128)(2,1)S(1)}, u32[]{:S(2)}) copy-start(bf16[224,896]{1,0:T(8,128)(2,1)S(1)} %collective-permute-done.8.refs_6_) | copy-start | bytes 1204228
  108.0 20.4 %collective-permute-start.9 = (bf16[224,896]{1,0:T(8,128)(2,1)S(1)}, bf16[224,896]{1,0:T(8,128)(2,1)S(1)}, u32[]{:S(2)}, u32[]{:S(2)}) collective-permute-start(bf16[224,896]{1,0:T(8,128)(2,1)S(1)} %collective-permute-done.5.refs_3_), channel_id=1, source_target_pairs={{0,96},{32,0},{64,32},{96,64},{1,97},{33,1},{65,33},{97,65},{2,98}... | collective-permute-start | bytes 1204232 | tf_op jit(solution)/shard_map/ppermute | solution.py:20
  111.3 30.1 %collective-permute-start.15 = (bf16[224,896]{1,0:T(8,128)(2,1)}, bf16[224,896]{1,0:T(8,128)(2,1)}, u32[]{:S(2)}, u32[]{:S(2)}) collective-permute-start(bf16[224,896]{1,0:T(8,128)(2,1)} %collective-permute-done.7.refs_5_), channel_id=1, source_target_pairs={{0,96},{32,0},{64,32},{96,64},{1,97},{33,1},{65,33},{97,65},{2,98}... | collective-permute-start | bytes 1204232 | tf_op jit(solution)/shard_map/ppermute | solution.py:20
  119.8 0.8 copy-start.9
  120.6 20.9 %collective-permute-start.18 = (bf16[224,896]{1,0:T(8,128)(2,1)}, bf16[224,896]{1,0:T(8,128)(2,1)}, u32[]{:S(2)}, u32[]{:S(2)}) collective-permute-start(bf16[224,896]{1,0:T(8,128)(2,1)} %collective-permute-done.13.refs_11_), channel_id=1, source_target_pairs={{0,32},{32,64},{64,96},{96,0},{1,33},{33,65},{65,97},{97,1},{2,34}... | collective-permute-start | bytes 1204232 | tf_op jit(solution)/shard_map/ppermute | solution.py:20
  128.4 13.0 %collective-permute-start.16 = (bf16[112,896]{1,0:T(8,128)(2,1)}, bf16[112,896]{1,0:T(8,128)(2,1)}, u32[]{:S(2)}, u32[]{:S(2)}) collective-permute-start(bf16[112,896]{1,0:T(8,128)(2,1)} %slice.16), channel_id=1, source_target_pairs={{0,32},{32,64},{64,96},{96,0},{1,33},{33,65},{65,97},{97,1},{2,34}... | collective-permute-start | bytes 602120 | tf_op jit(solution)/shard_map/ppermute | solution.py:20
  129.9 11.5 %collective-permute-start.17 = (bf16[112,896]{1,0:T(8,128)(2,1)S(1)}, bf16[112,896]{1,0:T(8,128)(2,1)}, u32[]{:S(2)}, u32[]{:S(2)}) collective-permute-start(bf16[112,896]{1,0:T(8,128)(2,1)S(1)} %slice.17), channel_id=1, source_target_pairs={{0,96},{32,0},{64,32},{96,64},{1,97},{33,1},{65,33},{97,65},{2,98}... | collective-permute-start | bytes 602120 | tf_op jit(solution)/shard_map/ppermute | solution.py:20
  162.4 3.8 %collective-permute-start.19 = (bf16[16,32,1024]{2,1,0:T(8,128)(2,1)}, bf16[16,32,1024]{2,1,0:T(8,128)(2,1)S(1)}, u32[]{:S(2)}, u32[]{:S(2)}) collective-permute-start(bf16[16,32,1024]{2,1,0:T(8,128)(2,1)} %get-tuple-element.5), channel_id=1, source_target_pairs={{0,1},{1,0},{2,3},{3,2},{4,5},{5,4},{6,7},{7,6},{8,9},{9,8},{10,11... | collective-permute-start | bytes 3145736 | tf_op jit(solution)/shard_map/ppermute | solution.py:24
  166.2 7.1 %copy-start.12 = (s32[8,32]{1,0:T(8,128)S(1)}, s32[8,32]{1,0:T(8,128)}, u32[]{:S(2)}) copy-start(s32[8,32]{1,0:T(8,128)} %valid_ref.1) | copy-start | bytes 3076
  168.8 20.1 %all-to-all-start.1 = ((bf16[16,32,1024]{2,1,0:T(8,128)(2,1)}), bf16[16,32,1024]{2,1,0:T(8,128)(2,1)S(1)}, u32[]{:S(2)}, u32[]{:S(2)}) async-start(bf16[16,32,1024]{2,1,0:T(8,128)(2,1)} %add_convert_fusion), calls=%async_computation.1 | async-start | bytes 2097152 | tf_op jit(solution)/shard_map/all_to_all | solution.py:280
  (2 other events, 1.5 us)

commit v6 on v5

--- a/solution.py
+++ b/solution.py
@@ -126,43 +126,35 @@
 
 
 def near_kernel(place_ref, near_hbm, *refs):
-    pieces, (mixed_hbm, w_ref, near_ref, mixed_ref, sems, near_sems, out_sems) = refs[:COUNT], refs[COUNT:]
+    pieces, (mixed_ref, w_ref, near_ref, sems, near_sems) = refs[:COUNT], refs[COUNT:]
     load_weights(place_ref, pieces, w_ref, sems, 0)
     loads = row_loads(near_hbm, near_ref, near_sems)
     for load in loads:
         load.start()
     wait_weights(place_ref, pieces, w_ref, sems, 0)
     rows = near_ref.shape[0] // CHUNKS
-    stores = []
     for n in range(CHUNKS):
         loads[n].wait()
         mixed_ref[n] = times_rows(w_ref, near_ref[n * rows : (n + 1) * rows, :])
-        stores.append(pltpu.make_async_copy(mixed_ref.at[n], mixed_hbm.at[n], out_sems.at[n]))
-        stores[n].start()
-    for store in stores:
-        store.wait()
-
-
-def far_kernel(place_ref, near_hbm, far_hbm, mixed_hbm, *refs):
+
+
+def far_kernel(place_ref, near_hbm, far_hbm, mixed_ref, *refs):
     pieces, outs, scratch = refs[:COUNT], refs[COUNT : COUNT + 2], refs[COUNT + 2 :]
     kept_ref, given_ref = outs
-    w_ref, far_ref, first_ref, mixed_ref, total_ref, table_ref, sems, far_sems, mixed_sems, first_sem = scratch
+    w_ref, far_ref, first_ref, total_ref, table_ref, sems, far_sems, first_sem = scratch
     load_weights(place_ref, pieces, w_ref, sems, 2)
     quarter = w_ref.shape[0]
     slots = table_ref.shape[0]
     rows = slots // CHUNKS
     loads = row_loads(far_hbm, far_ref, far_sems)
-    partials = [pltpu.make_async_copy(mixed_hbm.at[n], mixed_ref.at[n], mixed_sems.at[n]) for n in range(CHUNKS)]
     first = pltpu.make_async_copy(near_hbm.at[:, pl.ds(0, quarter)], first_ref, first_sem.at[0])
     for n in range(CHUNKS):
         loads[n].start()
-        partials[n].start()
     first.start()
     wait_weights(place_ref, pieces, w_ref, sems, 2)
     for n in range(CHUNKS):
         at = slice(n * rows, (n + 1) * rows)
         loads[n].wait()
-        partials[n].wait()
         total_ref[:, at] = (mixed_ref[n] + times_rows(w_ref, far_ref[at, :])).astype(total_ref.dtype)
     first.wait()
     hidden = jnp.where(first_ref[:, :1].astype(jnp.float32) < FILL_TEST, 0.0, HIDDEN)
@@ -194,23 +186,20 @@
     quarter = half // 2
     rows = slots // CHUNKS
     scalars = pl.BlockSpec(memory_space=pltpu.SMEM)
-    limit = pltpu.CompilerParams(vmem_limit_bytes=56 * 2**20)
     four = pltpu.SemaphoreType.DMA((CHUNKS,))
     each = pltpu.SemaphoreType.DMA((COUNT,))
     mixed = pl.pallas_call(
         near_kernel,
         in_specs=[scalars] + [in_hbm()] * (COUNT + 1),
-        out_specs=in_hbm(),
-        out_shape=jax.ShapeDtypeStruct((CHUNKS, quarter, rows), jnp.float32),
+        out_specs=whole(),
+        out_shape=pltpu.VMEM((CHUNKS, quarter, rows), jnp.float32),
         scratch_shapes=[
             pltpu.VMEM((quarter, half), near.dtype),
             pltpu.VMEM((slots, half), near.dtype),
-            pltpu.VMEM((CHUNKS, quarter, rows), jnp.float32),
             each,
             four,
-            four,
-        ],
-        compiler_params=limit,
+        ],
+        compiler_params=pltpu.CompilerParams(vmem_limit_bytes=16 * 2**20),
         cost_estimate=pl.CostEstimate(
             flops=2 * quarter * half * slots, bytes_accessed=12 * 2**20, transcendentals=0
         ),
@@ -218,25 +207,23 @@
     part = slots // 32
     return pl.pallas_call(
         far_kernel,
-        in_specs=[scalars] + [in_hbm()] * (COUNT + 3),
+        in_specs=[scalars, in_hbm(), in_hbm(), whole()] + [in_hbm()] * COUNT,
         out_specs=[whole(), whole()],
         out_shape=[
-            jax.ShapeDtypeStruct((16, part, slots), jnp.bfloat16),
-            jax.ShapeDtypeStruct((16, part, slots), jnp.bfloat16),
+            pltpu.VMEM((16, part, slots), jnp.bfloat16),
+            pltpu.VMEM((16, part, slots), jnp.bfloat16),
         ],
         scratch_shapes=[
             pltpu.VMEM((quarter, half), near.dtype),
             pltpu.VMEM((slots, half), near.dtype),
             pltpu.VMEM((slots, quarter), near.dtype),
-            pltpu.VMEM((CHUNKS, quarter, rows), jnp.float32),
             pltpu.VMEM((quarter, slots), near.dtype),
             pltpu.VMEM((slots, slots), jnp.float32),
             each,
             four,
-            four,
             pltpu.SemaphoreType.DMA((1,)),
         ],
-        compiler_params=limit,
+        compiler_params=pltpu.CompilerParams(vmem_limit_bytes=32 * 2**20),
         cost_estimate=pl.CostEstimate(
             flops=2 * quarter * (half + slots) * slots, bytes_accessed=16 * 2**20, transcendentals=0
         ),

time: 193 us -> 192 us (level)
  local copies, waits for them, and re-layouts: 3 us -> 9.43 us
  Pallas kernels: 24.6 us -> 19.3 us
    unnamed x26 -> x34, local copies, waits for them, and re-layouts: 2.27 us -> 8.04 us
    pallas_call x1, Pallas kernels: 12.6 us -> 9.31 us  [score_parts(): pl.pallas_call(far_kernel, in_specs=[scalars, in_hbm(), in_hbm(), whole()...]
  transfers between devices with their start and end apart: 21 -> 21, of which waited for: 13 -> 13; matrix products, arithmetic and copies ran while one was open for 1% -> 1% of each run, Pallas kernels for 4% -> 3%
where the time goes in v6:
time: 192 us; the launch traced here: 189 us
  waiting for transfers between devices  71.1 us (37%)
  blocking collectives  55 us (29%)
  starting transfers between devices  29.9 us (16%)
  Pallas kernels  19.3 us (10%)
  local copies, waits for them, and re-layouts  9.43 us (5%)
  other arithmetic  3.77 us (2%)
    all_to_all x1, blocking collectives, scored(): lax.all_to_all(outgoing, RESP_AXES, 0, 0, tiled=True)  55 us
    ppermute x16, waiting for transfers between devices, ring(): return lax.ppermute(value, axis, [(i, (i + step) % 4) for i in range(4)])  48 us
    ppermute x16, starting transfers between devices, ring(): return lax.ppermute(value, axis, [(i, (i + step) % 4) for i in range(4)])  19.7 us
    all_to_all x1, waiting for transfers between devices, scored(): lax.all_to_all(half_scores, ('y', 'z'), 0, 0, tiled=True)  15.6 us
    pallas_call x1, Pallas kernels, score_parts(): pl.pallas_call(far_kernel, in_specs=[scalars, in_hbm(), in_hbm(), whole()...  9.31 us
    unnamed x34, local copies, waits for them, and re-layouts  8.04 us
    pallas_call x1, Pallas kernels, score_parts(): pl.pallas_call(near_kernel, in_specs=[scalars] + [in_hbm()] * (COUNT + 1)...  6.29 us
    all_to_all x1, starting transfers between devices, scored(): lax.all_to_all(half_scores, ('y', 'z'), 0, 0, tiled=True)  4.48 us
  transfers between devices with their start and end apart: 21, of which 13 were waited for; matrix products, arithmetic and copies ran while one was open for 1% of the time, Pallas kernels for 3%

profile of v6, /device:TPU:1, one launch (start us, length us, event | category | flops | bytes accessed | tf_op | source)
XLA Modules:
  0.0 189.4 jit_solution(9153739947801430429)
XLA Ops:
  0.6 3.8 %shard_map.50 = bf16[2,2,4,2,32,1792]{5,4,3,2,1,0:T(8,128)(2,1)} custom-call(bf16[8,32,3584]{2,1,0:T(8,128)(2,1)} %rows_ref.1, s32[8,32]{1,0:T(8,128)} %valid_ref.1), custom_call_target="tpu_custom_call" | custom-call | tf_op jit(solution)/shard_map/pallas_call | solution.py:68
  4.4 55.0 %all_to_all.10 = bf16[32,32,1792]{2,1,0:T(8,128)(2,1)} all-to-all(bf16[32,32,1792]{2,1,0:T(8,128)(2,1)} %bitcast.5), channel_id=1, replica_groups=mesh['x'=4,'y'=4,'z'=4,'c'=2] {'y','z','c'}, dimensions={0} | all-to-all | bytes 7340032 | tf_op jit(solution)/shard_map/all_to_all | solution.py:251
  59.4 2.5 %collective-permute-start.1 = (bf16[112,896]{1,0:T(8,128)(2,1)S(1)}, bf16[112,896]{1,0:T(8,128)(2,1)S(1)}, u32[]{:S(2)}, u32[]{:S(2)}) collective-permute-start(bf16[112,896]{1,0:T(8,128)(2,1)S(1)} %constant_dynamic-slice_fusion), channel_id=1, source_target_pairs={{0,0},{1,8},{8,9},{9,1},{16,16},{17,24},{24,25},{25,17},{2,2},{3,1... | collective-permute-start | bytes 602120 | tf_op jit(solution)/shard_map/ppermute | solution.py:243
  61.9 1.9 %collective-permute-start.2 = (bf16[112,896]{1,0:T(8,128)(2,1)S(1)}, bf16[112,896]{1,0:T(8,128)(2,1)S(1)}, u32[]{:S(2)}, u32[]{:S(2)}) collective-permute-start(bf16[112,896]{1,0:T(8,128)(2,1)S(1)} %constant_dynamic-slice_fusion), channel_id=1, source_target_pairs={{0,8},{1,0},{8,1},{9,9},{16,24},{17,16},{24,17},{25,25},{2,10},{3,... | collective-permute-start | bytes 602120 | tf_op jit(solution)/shard_map/ppermute | solution.py:244
  63.9 2.0 %collective-permute-done.1 = bf16[112,896]{1,0:T(8,128)(2,1)S(1)} collective-permute-done((bf16[112,896]{1,0:T(8,128)(2,1)S(1)}, bf16[112,896]{1,0:T(8,128)(2,1)S(1)}, u32[]{:S(2)}, u32[]{:S(2)}) %collective-permute-start.1) | collective-permute-done | bytes 200736 | tf_op jit(solution)/shard_map/ppermute | solution.py:243
  65.9 3.0 %collective-permute-done.2 = bf16[112,896]{1,0:T(8,128)(2,1)S(1)} collective-permute-done((bf16[112,896]{1,0:T(8,128)(2,1)S(1)}, bf16[112,896]{1,0:T(8,128)(2,1)S(1)}, u32[]{:S(2)}, u32[]{:S(2)}) %collective-permute-start.2) | collective-permute-done | bytes 200736 | tf_op jit(solution)/shard_map/ppermute | solution.py:244
  69.0 1.3 collective-permute-start.3
  70.3 1.0 collective-permute-start.4
  71.4 1.2 collective-permute-start.10
  72.6 7.8 %collective-permute-done.3.refs_1_ = bf16[224,896]{1,0:T(8,128)(2,1)S(1)} collective-permute-done((bf16[224,896]{1,0:T(8,128)(2,1)S(1)}, bf16[224,896]{1,0:T(8,128)(2,1)S(1)}, u32[]{:S(2)}, u32[]{:S(2)}) %collective-permute-start.3) | collective-permute-done | bytes 401440 | tf_op jit(solution)/shard_map/ppermute | solution.py:20
  80.4 2.5 %collective-permute-start.6 = (bf16[224,896]{1,0:T(8,128)(2,1)S(1)}, bf16[224,896]{1,0:T(8,128)(2,1)S(1)}, u32[]{:S(2)}, u32[]{:S(2)}) collective-permute-start(bf16[224,896]{1,0:T(8,128)(2,1)S(1)} %pad_maximum_fusion.refs_0_), channel_id=1, source_target_pairs={{0,96},{32,0},{64,32},{96,64},{1,97},{33,1},{65,33},{97,65},{2,98}... | collective-permute-start | bytes 1204232 | tf_op jit(solution)/shard_map/ppermute | solution.py:20
  82.9 2.5 %collective-permute-start.7 = (bf16[224,896]{1,0:T(8,128)(2,1)S(1)}, bf16[224,896]{1,0:T(8,128)(2,1)}, u32[]{:S(2)}, u32[]{:S(2)}) collective-permute-start(bf16[224,896]{1,0:T(8,128)(2,1)S(1)} %collective-permute-done.3.refs_1_), channel_id=1, source_target_pairs={{0,96},{32,0},{64,32},{96,64},{1,97},{33,1},{65,33},{97,65},{2,98}... | collective-permute-start | bytes 1204232 | tf_op jit(solution)/shard_map/ppermute | solution.py:20
  85.4 5.6 %collective-permute-done.5.refs_3_ = bf16[224,896]{1,0:T(8,128)(2,1)S(1)} collective-permute-done((bf16[224,896]{1,0:T(8,128)(2,1)S(1)}, bf16[224,896]{1,0:T(8,128)(2,1)S(1)}, u32[]{:S(2)}, u32[]{:S(2)}) %collective-permute-start.5) | collective-permute-done | bytes 401440 | tf_op jit(solution)/shard_map/ppermute | solution.py:20
  90.9 1.2 collective-permute-start.12
  92.2 1.5 collective-permute-start.8
  94.4 6.2 %collective-permute-done.7.refs_5_ = bf16[224,896]{1,0:T(8,128)(2,1)} collective-permute-done((bf16[224,896]{1,0:T(8,128)(2,1)S(1)}, bf16[224,896]{1,0:T(8,128)(2,1)}, u32[]{:S(2)}, u32[]{:S(2)}) %collective-permute-start.7) | collective-permute-done | bytes 401440 | tf_op jit(solution)/shard_map/ppermute | solution.py:20
  101.5 1.1 collective-permute-done.12.refs_10_
  102.8 5.2 %collective-permute-done.8.refs_6_ = bf16[224,896]{1,0:T(8,128)(2,1)S(1)} collective-permute-done((bf16[224,896]{1,0:T(8,128)(2,1)S(1)}, bf16[224,896]{1,0:T(8,128)(2,1)S(1)}, u32[]{:S(2)}, u32[]{:S(2)}) %collective-permute-start.8) | collective-permute-done | bytes 401440 | tf_op jit(solution)/shard_map/ppermute | solution.py:20
  108.0 3.1 %collective-permute-start.9 = (bf16[224,896]{1,0:T(8,128)(2,1)S(1)}, bf16[224,896]{1,0:T(8,128)(2,1)S(1)}, u32[]{:S(2)}, u32[]{:S(2)}) collective-permute-start(bf16[224,896]{1,0:T(8,128)(2,1)S(1)} %collective-permute-done.5.refs_3_), channel_id=1, source_target_pairs={{0,96},{32,0},{64,32},{96,64},{1,97},{33,1},{65,33},{97,65},{2,98}... | collective-permute-start | bytes 1204232 | tf_op jit(solution)/shard_map/ppermute | solution.py:20
  111.3 1.6 collective-permute-start.15
  112.9 6.9 %collective-permute-done.11.refs_9_ = bf16[224,896]{1,0:T(8,128)(2,1)S(1)} collective-permute-done((bf16[224,896]{1,0:T(8,128)(2,1)S(1)}, bf16[224,896]{1,0:T(8,128)(2,1)S(1)}, u32[]{:S(2)}, u32[]{:S(2)}) %collective-permute-start.11) | collective-permute-done | bytes 401440 | tf_op jit(solution)/shard_map/ppermute | solution.py:20
  122.0 6.4 %collective-permute-done.14.refs_12_ = bf16[224,896]{1,0:T(8,128)(2,1)S(1)} collective-permute-done((bf16[224,896]{1,0:T(8,128)(2,1)S(1)}, bf16[224,896]{1,0:T(8,128)(2,1)S(1)}, u32[]{:S(2)}, u32[]{:S(2)}) %collective-permute-start.14) | collective-permute-done | bytes 401440 | tf_op jit(solution)/shard_map/ppermute | solution.py:20
  130.0 2.7 %collective-permute-start.17 = (bf16[112,896]{1,0:T(8,128)(2,1)}, bf16[112,896]{1,0:T(8,128)(2,1)}, u32[]{:S(2)}, u32[]{:S(2)}) collective-permute-start(bf16[112,896]{1,0:T(8,128)(2,1)} %slice.17), channel_id=1, source_target_pairs={{0,96},{32,0},{64,32},{96,64},{1,97},{33,1},{65,33},{97,65},{2,98}... | collective-permute-start | bytes 602120 | tf_op jit(solution)/shard_map/ppermute | solution.py:20
  132.7 8.6 %collective-permute-done.16.refs_14_ = bf16[112,896]{1,0:T(8,128)(2,1)S(1)} collective-permute-done((bf16[112,896]{1,0:T(8,128)(2,1)}, bf16[112,896]{1,0:T(8,128)(2,1)S(1)}, u32[]{:S(2)}, u32[]{:S(2)}) %collective-permute-start.16) | collective-permute-done | bytes 200736 | tf_op jit(solution)/shard_map/ppermute | solution.py:20
  146.3 6.3 %shard_map.51.mixed_ref = f32[2,896,512]{2,1,0:T(8,128)S(1)} custom-call(s32[3]{0:T(128)S(1)} %pad_add_fusion.place_ref, bf16[1024,1792]{1,0:T(8,128)(2,1)} %bitcast.4.near_hbm, bf16[224,896]{1,0:T(8,128)(2,1)S(1)} %pad_maximum_fusion.refs_0_, bf16[224,896]{1,0:T(8,128)(2,1)S(1)} %collective-permute-done.3.refs_1_, ...), custom_call_target="tpu_custom_call" | custom-call | flops 3288334336 | bytes 12582912 | tf_op jit(solution)/shard_map/pallas_call | solution.py:191
  152.7 9.3 %shard_map.52 = (bf16[16,32,1024]{2,1,0:T(8,128)(2,1)S(1)}, bf16[16,32,1024]{2,1,0:T(8,128)(2,1)S(1)}) custom-call(s32[3]{0:T(128)S(1)} %pad_add_fusion.place_ref, bf16[1024,1792]{1,0:T(8,128)(2,1)} %bitcast.4.near_hbm, bf16[1024,1792]{1,0:T(8,128)(2,1)} %collective-permute-done.far_hbm, f32[2,896,512]{2,1,0:T(8,128)S(1)} %shard_map.51.mixed_ref, ...), custom_call_target="tpu_custom_call" | custom-call | flops 5167382528 | bytes 16777216 | tf_op jit(solution)/shard_map/pallas_call | solution.py:208
  162.0 1.3 collective-permute-start.19
  163.3 2.3 %collective-permute-done.19 = bf16[16,32,1024]{2,1,0:T(8,128)(2,1)S(1)} collective-permute-done((bf16[16,32,1024]{2,1,0:T(8,128)(2,1)S(1)}, bf16[16,32,1024]{2,1,0:T(8,128)(2,1)S(1)}, u32[]{:S(2)}, u32[]{:S(2)}) %collective-permute-start.19) | collective-permute-done | bytes 1048608 | tf_op jit(solution)/shard_map/ppermute | solution.py:24
  165.6 1.4 add_convert_fusion
  167.0 4.5 %all-to-all-start.1 = ((bf16[16,32,1024]{2,1,0:T(8,128)(2,1)}), bf16[16,32,1024]{2,1,0:T(8,128)(2,1)S(1)}, u32[]{:S(2)}, u32[]{:S(2)}) async-start(bf16[16,32,1024]{2,1,0:T(8,128)(2,1)} %add_convert_fusion), calls=%async_computation.1 | async-start | bytes 2097152 | tf_op jit(solution)/shard_map/all_to_all | solution.py:267
  171.5 15.6 %all-to-all-done.1 = bf16[16,32,1024]{2,1,0:T(8,128)(2,1)S(1)} async-done(((bf16[16,32,1024]{2,1,0:T(8,128)(2,1)}), bf16[16,32,1024]{2,1,0:T(8,128)(2,1)S(1)}, u32[]{:S(2)}, u32[]{:S(2)}) %all-to-all-start.1) | async-done | bytes 1048608 | tf_op jit(solution)/shard_map/all_to_all | solution.py:267
  187.4 1.4 fusion
  (59 shorter events, 11.9 us)
Async XLA Ops:
  0.6 58.8 %copy-start = (bf16[112,3584]{1,0:T(8,128)(2,1)S(1)}, bf16[112,3584]{1,0:T(8,128)(2,1)}, u32[]{:S(2)}) copy-start(bf16[112,3584]{1,0:T(8,128)(2,1)} %param.4) | copy-start | bytes 2408452
  59.4 93.2 %collective-permute-start = (bf16[1024,1792]{1,0:T(8,128)(2,1)}, bf16[1024,1792]{1,0:T(8,128)(2,1)}, u32[]{:S(2)}, u32[]{:S(2)}) collective-permute-start(bf16[1024,1792]{1,0:T(8,128)(2,1)} %bitcast.4.near_hbm), channel_id=1, source_target_pairs={{0,1},{1,0},{2,3},{3,2},{4,5},{5,4},{6,7},{7,6},{8,9},{9,8},{10,11... | collective-permute-start | bytes 11010056 | tf_op jit(solution)/shard_map/ppermute | solution.py:24
  59.4 6.5 %collective-permute-start.1 = (bf16[112,896]{1,0:T(8,128)(2,1)S(1)}, bf16[112,896]{1,0:T(8,128)(2,1)S(1)}, u32[]{:S(2)}, u32[]{:S(2)}) collective-permute-start(bf16[112,896]{1,0:T(8,128)(2,1)S(1)} %constant_dynamic-slice_fusion), channel_id=1, source_target_pairs={{0,0},{1,8},{8,9},{9,1},{16,16},{17,24},{24,25},{25,17},{2,2},{3,1... | collective-permute-start | bytes 602120 | tf_op jit(solution)/shard_map/ppermute | solution.py:243
  61.9 7.0 %collective-permute-start.2 = (bf16[112,896]{1,0:T(8,128)(2,1)S(1)}, bf16[112,896]{1,0:T(8,128)(2,1)S(1)}, u32[]{:S(2)}, u32[]{:S(2)}) collective-permute-start(bf16[112,896]{1,0:T(8,128)(2,1)S(1)} %constant_dynamic-slice_fusion), channel_id=1, source_target_pairs={{0,8},{1,0},{8,1},{9,9},{16,24},{17,16},{24,17},{25,25},{2,10},{3,... | collective-permute-start | bytes 602120 | tf_op jit(solution)/shard_map/ppermute | solution.py:244
  69.0 11.4 %collective-permute-start.3 = (bf16[224,896]{1,0:T(8,128)(2,1)S(1)}, bf16[224,896]{1,0:T(8,128)(2,1)S(1)}, u32[]{:S(2)}, u32[]{:S(2)}) collective-permute-start(bf16[224,896]{1,0:T(8,128)(2,1)S(1)} %pad_maximum_fusion.refs_0_), channel_id=1, source_target_pairs={{0,6},{2,0},{4,2},{6,4},{1,7},{3,1},{5,3},{7,5},{8,14},{10,8},{12,... | collective-permute-start | bytes 1204232 | tf_op jit(solution)/shard_map/ppermute | solution.py:20
  70.3 12.6 %collective-permute-start.4 = (bf16[224,896]{1,0:T(8,128)(2,1)S(1)}, bf16[224,896]{1,0:T(8,128)(2,1)S(1)}, u32[]{:S(2)}, u32[]{:S(2)}) collective-permute-start(bf16[224,896]{1,0:T(8,128)(2,1)S(1)} %pad_maximum_fusion.refs_0_), channel_id=1, source_target_pairs={{0,4},{2,6},{4,0},{6,2},{1,5},{3,7},{5,1},{7,3},{8,12},{10,14},{12... | collective-permute-start | bytes 1204232 | tf_op jit(solution)/shard_map/ppermute | solution.py:20
  71.4 19.6 %collective-permute-start.5 = (bf16[224,896]{1,0:T(8,128)(2,1)S(1)}, bf16[224,896]{1,0:T(8,128)(2,1)S(1)}, u32[]{:S(2)}, u32[]{:S(2)}) collective-permute-start(bf16[224,896]{1,0:T(8,128)(2,1)S(1)} %pad_maximum_fusion.refs_0_), channel_id=1, source_target_pairs={{0,2},{2,4},{4,6},{6,0},{1,3},{3,5},{5,7},{7,1},{8,10},{10,12},{12... | collective-permute-start | bytes 1204232 | tf_op jit(solution)/shard_map/ppermute | solution.py:20
  71.4 20.8 %collective-permute-start.10 = (bf16[224,896]{1,0:T(8,128)(2,1)S(1)}, bf16[224,896]{1,0:T(8,128)(2,1)S(1)}, u32[]{:S(2)}, u32[]{:S(2)}) collective-permute-start(bf16[224,896]{1,0:T(8,128)(2,1)S(1)} %pad_maximum_fusion.refs_0_), channel_id=1, source_target_pairs={{0,32},{32,64},{64,96},{96,0},{1,33},{33,65},{65,97},{97,1},{2,34}... | collective-permute-start | bytes 1204232 | tf_op jit(solution)/shard_map/ppermute | solution.py:20
  80.4 13.2 %collective-permute-start.6 = (bf16[224,896]{1,0:T(8,128)(2,1)S(1)}, bf16[224,896]{1,0:T(8,128)(2,1)S(1)}, u32[]{:S(2)}, u32[]{:S(2)}) collective-permute-start(bf16[224,896]{1,0:T(8,128)(2,1)S(1)} %pad_maximum_fusion.refs_0_), channel_id=1, source_target_pairs={{0,96},{32,0},{64,32},{96,64},{1,97},{33,1},{65,33},{97,65},{2,98}... | collective-permute-start | bytes 1204232 | tf_op jit(solution)/shard_map/ppermute | solution.py:20
  82.9 17.7 %collective-permute-start.7 = (bf16[224,896]{1,0:T(8,128)(2,1)S(1)}, bf16[224,896]{1,0:T(8,128)(2,1)}, u32[]{:S(2)}, u32[]{:S(2)}) collective-permute-start(bf16[224,896]{1,0:T(8,128)(2,1)S(1)} %collective-permute-done.3.refs_1_), channel_id=1, source_target_pairs={{0,96},{32,0},{64,32},{96,64},{1,97},{33,1},{65,33},{97,65},{2,98}... | collective-permute-start | bytes 1204232 | tf_op jit(solution)/shard_map/ppermute | solution.py:20
  90.9 11.7 %collective-permute-start.12 = (bf16[224,896]{1,0:T(8,128)(2,1)S(1)}, bf16[224,896]{1,0:T(8,128)(2,1)S(1)}, u32[]{:S(2)}, u32[]{:S(2)}) collective-permute-start(bf16[224,896]{1,0:T(8,128)(2,1)S(1)} %collective-permute-done.4.refs_2_), channel_id=1, source_target_pairs={{0,32},{32,64},{64,96},{96,0},{1,33},{33,65},{65,97},{97,1},{2,34}... | collective-permute-start | bytes 1204232 | tf_op jit(solution)/shard_map/ppermute | solution.py:20
  92.2 37.0 %copy-start.1 = (bf16[224,896]{1,0:T(8,128)(2,1)}, bf16[224,896]{1,0:T(8,128)(2,1)S(1)}, u32[]{:S(2)}) copy-start(bf16[224,896]{1,0:T(8,128)(2,1)S(1)} %collective-permute-done.10.refs_8_) | copy-start | bytes 1204228
  92.2 15.8 %collective-permute-start.8 = (bf16[224,896]{1,0:T(8,128)(2,1)S(1)}, bf16[224,896]{1,0:T(8,128)(2,1)S(1)}, u32[]{:S(2)}, u32[]{:S(2)}) collective-permute-start(bf16[224,896]{1,0:T(8,128)(2,1)S(1)} %collective-permute-done.4.refs_2_), channel_id=1, source_target_pairs={{0,96},{32,0},{64,32},{96,64},{1,97},{33,1},{65,33},{97,65},{2,98}... | collective-permute-start | bytes 1204232 | tf_op jit(solution)/shard_map/ppermute | solution.py:20
  94.4 16.9 %collective-permute-start.13 = (bf16[224,896]{1,0:T(8,128)(2,1)S(1)}, bf16[224,896]{1,0:T(8,128)(2,1)}, u32[]{:S(2)}, u32[]{:S(2)}) collective-permute-start(bf16[224,896]{1,0:T(8,128)(2,1)S(1)} %collective-permute-done.5.refs_3_), channel_id=1, source_target_pairs={{0,32},{32,64},{64,96},{96,0},{1,33},{33,65},{65,97},{97,1},{2,34}... | collective-permute-start | bytes 1204232 | tf_op jit(solution)/shard_map/ppermute | solution.py:20
  100.6 19.2 %collective-permute-start.11 = (bf16[224,896]{1,0:T(8,128)(2,1)S(1)}, bf16[224,896]{1,0:T(8,128)(2,1)S(1)}, u32[]{:S(2)}, u32[]{:S(2)}) collective-permute-start(bf16[224,896]{1,0:T(8,128)(2,1)S(1)} %collective-permute-done.3.refs_1_), channel_id=1, source_target_pairs={{0,32},{32,64},{64,96},{96,0},{1,33},{33,65},{65,97},{97,1},{2,34}... | collective-permute-start | bytes 1204232 | tf_op jit(solution)/shard_map/ppermute | solution.py:20
  102.6 25.8 %collective-permute-start.14 = (bf16[224,896]{1,0:T(8,128)(2,1)S(1)}, bf16[224,896]{1,0:T(8,128)(2,1)S(1)}, u32[]{:S(2)}, u32[]{:S(2)}) collective-permute-start(bf16[224,896]{1,0:T(8,128)(2,1)S(1)} %collective-permute-done.10.refs_8_), channel_id=1, source_target_pairs={{0,32},{32,64},{64,96},{96,0},{1,33},{33,65},{65,97},{97,1},{2,34}... | collective-permute-start | bytes 1204232 | tf_op jit(solution)/shard_map/ppermute | solution.py:20
  108.0 21.2 %collective-permute-start.9 = (bf16[224,896]{1,0:T(8,128)(2,1)S(1)}, bf16[224,896]{1,0:T(8,128)(2,1)S(1)}, u32[]{:S(2)}, u32[]{:S(2)}) collective-permute-start(bf16[224,896]{1,0:T(8,128)(2,1)S(1)} %collective-permute-done.5.refs_3_), channel_id=1, source_target_pairs={{0,96},{32,0},{64,32},{96,64},{1,97},{33,1},{65,33},{97,65},{2,98}... | collective-permute-start | bytes 1204232 | tf_op jit(solution)/shard_map/ppermute | solution.py:20
  111.3 30.0 %collective-permute-start.15 = (bf16[224,896]{1,0:T(8,128)(2,1)}, bf16[224,896]{1,0:T(8,128)(2,1)}, u32[]{:S(2)}, u32[]{:S(2)}) collective-permute-start(bf16[224,896]{1,0:T(8,128)(2,1)} %collective-permute-done.7.refs_5_), channel_id=1, source_target_pairs={{0,96},{32,0},{64,32},{96,64},{1,97},{33,1},{65,33},{97,65},{2,98}... | collective-permute-start | bytes 1204232 | tf_op jit(solution)/shard_map/ppermute | solution.py:20
  120.6 20.8 %collective-permute-start.18 = (bf16[224,896]{1,0:T(8,128)(2,1)}, bf16[224,896]{1,0:T(8,128)(2,1)}, u32[]{:S(2)}, u32[]{:S(2)}) collective-permute-start(bf16[224,896]{1,0:T(8,128)(2,1)} %collective-permute-done.13.refs_11_), channel_id=1, source_target_pairs={{0,32},{32,64},{64,96},{96,0},{1,33},{33,65},{65,97},{97,1},{2,34}... | collective-permute-start | bytes 1204232 | tf_op jit(solution)/shard_map/ppermute | solution.py:20
  129.2 12.1 %collective-permute-start.16 = (bf16[112,896]{1,0:T(8,128)(2,1)}, bf16[112,896]{1,0:T(8,128)(2,1)S(1)}, u32[]{:S(2)}, u32[]{:S(2)}) collective-permute-start(bf16[112,896]{1,0:T(8,128)(2,1)} %slice.16), channel_id=1, source_target_pairs={{0,32},{32,64},{64,96},{96,0},{1,33},{33,65},{65,97},{97,1},{2,34}... | collective-permute-start | bytes 602120 | tf_op jit(solution)/shard_map/ppermute | solution.py:20
  130.0 11.4 %collective-permute-start.17 = (bf16[112,896]{1,0:T(8,128)(2,1)}, bf16[112,896]{1,0:T(8,128)(2,1)}, u32[]{:S(2)}, u32[]{:S(2)}) collective-permute-start(bf16[112,896]{1,0:T(8,128)(2,1)} %slice.17), channel_id=1, source_target_pairs={{0,96},{32,0},{64,32},{96,64},{1,97},{33,1},{65,33},{97,65},{2,98}... | collective-permute-start | bytes 602120 | tf_op jit(solution)/shard_map/ppermute | solution.py:20
  141.3 1.0 copy-start.2
  142.3 1.0 copy-start.5
  143.3 1.0 copy-start.8
  146.3 6.3 %copy-start.3 = (bf16[224,896]{1,0:T(8,128)(2,1)S(1)}, bf16[224,896]{1,0:T(8,128)(2,1)}, u32[]{:S(2)}) copy-start(bf16[224,896]{1,0:T(8,128)(2,1)} %copy-done.1) | copy-start | bytes 1204228
  146.3 6.3 %copy-start.6 = (bf16[224,896]{1,0:T(8,128)(2,1)S(1)}, bf16[224,896]{1,0:T(8,128)(2,1)}, u32[]{:S(2)}) copy-start(bf16[224,896]{1,0:T(8,128)(2,1)} %copy-done.4) | copy-start | bytes 1204228
  146.3 6.3 %copy-start.9 = (bf16[224,896]{1,0:T(8,128)(2,1)S(1)}, bf16[224,896]{1,0:T(8,128)(2,1)}, u32[]{:S(2)}) copy-start(bf16[224,896]{1,0:T(8,128)(2,1)} %copy-done.7) | copy-start | bytes 1204228
  146.3 6.4 %copy-start.12 = (bf16[224,896]{1,0:T(8,128)(2,1)S(1)}, bf16[224,896]{1,0:T(8,128)(2,1)}, u32[]{:S(2)}) copy-start(bf16[224,896]{1,0:T(8,128)(2,1)} %copy-done.10) | copy-start | bytes 1204228
  146.3 6.4 %copy-start.15 = (bf16[224,896]{1,0:T(8,128)(2,1)S(1)}, bf16[224,896]{1,0:T(8,128)(2,1)}, u32[]{:S(2)}) copy-start(bf16[224,896]{1,0:T(8,128)(2,1)} %copy-done.13) | copy-start | bytes 1204228
  162.0 3.6 %collective-permute-start.19 = (bf16[16,32,1024]{2,1,0:T(8,128)(2,1)S(1)}, bf16[16,32,1024]{2,1,0:T(8,128)(2,1)S(1)}, u32[]{:S(2)}, u32[]{:S(2)}) collective-permute-start(bf16[16,32,1024]{2,1,0:T(8,128)(2,1)S(1)} %get-tuple-element.5), channel_id=1, source_target_pairs={{0,1},{1,0},{2,3},{3,2},{4,5},{5,4},{6,7},{7,6},{8,9},{9,8},{10,11... | collective-permute-start | bytes 3145736 | tf_op jit(solution)/shard_map/ppermute | solution.py:24
  165.6 5.9 %copy-start.16 = (s32[8,32]{1,0:T(8,128)S(1)}, s32[8,32]{1,0:T(8,128)}, u32[]{:S(2)}) copy-start(s32[8,32]{1,0:T(8,128)} %valid_ref.1) | copy-start | bytes 3076
  167.0 20.1 %all-to-all-start.1 = ((bf16[16,32,1024]{2,1,0:T(8,128)(2,1)}), bf16[16,32,1024]{2,1,0:T(8,128)(2,1)S(1)}, u32[]{:S(2)}, u32[]{:S(2)}) async-start(bf16[16,32,1024]{2,1,0:T(8,128)(2,1)} %add_convert_fusion), calls=%async_computation.1 | async-start | bytes 2097152 | tf_op jit(solution)/shard_map/all_to_all | solution.py:267
  (6 other events, 5.0 us)

commit v7 on v6

--- a/solution.py
+++ b/solution.py
@@ -199,7 +199,7 @@
             each,
             four,
         ],
-        compiler_params=pltpu.CompilerParams(vmem_limit_bytes=16 * 2**20),
+        compiler_params=pltpu.CompilerParams(vmem_limit_bytes=12 * 2**20),
         cost_estimate=pl.CostEstimate(
             flops=2 * quarter * half * slots, bytes_accessed=12 * 2**20, transcendentals=0
         ),
@@ -223,7 +223,7 @@
             four,
             pltpu.SemaphoreType.DMA((1,)),
         ],
-        compiler_params=pltpu.CompilerParams(vmem_limit_bytes=32 * 2**20),
+        compiler_params=pltpu.CompilerParams(vmem_limit_bytes=24 * 2**20),
         cost_estimate=pl.CostEstimate(
             flops=2 * quarter * (half + slots) * slots, bytes_accessed=16 * 2**20, transcendentals=0
         ),
@@ -244,7 +244,7 @@
     part_b = lax.ppermute(slab, ("y", "c"), slab_pairs(1))
     outgoing = pack(embeddings, valid_mask)
     at_home = c == y % 2
-    own = jnp.concatenate([jnp.where(at_home, part_a, part_b), jnp.where(at_home, part_b, part_a)])
+    own = jnp.where(at_home, jnp.concatenate([part_a, part_b]), jnp.concatenate([part_b, part_a]))
     chain = [own]
     for step in (-1, 2, 1):
         chain.append(ring(own, "z", step))

time: 192 us -> 192 us (level)
  no operation moved by 1% of the time
where the time goes in v7:
time: 192 us; the launch traced here: 189 us
  waiting for transfers between devices  71.1 us (37%)
  blocking collectives  55 us (29%)
  starting transfers between devices  29.9 us (16%)
  Pallas kernels  19.4 us (10%)
  local copies, waits for them, and re-layouts  9.44 us (5%)
  other arithmetic  3.76 us (2%)
    all_to_all x1, blocking collectives, scored(): lax.all_to_all(outgoing, RESP_AXES, 0, 0, tiled=True)  55 us
    ppermute x16, waiting for transfers between devices, ring(): return lax.ppermute(value, axis, [(i, (i + step) % 4) for i in range(4)])  48 us
    ppermute x16, starting transfers between devices, ring(): return lax.ppermute(value, axis, [(i, (i + step) % 4) for i in range(4)])  19.7 us
    all_to_all x1, waiting for transfers between devices, scored(): lax.all_to_all(half_scores, ('y', 'z'), 0, 0, tiled=True)  15.6 us
    pallas_call x1, Pallas kernels, score_parts(): pl.pallas_call(far_kernel, in_specs=[scalars, in_hbm(), in_hbm(), whole()...  9.31 us
    unnamed x34, local copies, waits for them, and re-layouts  8.03 us
    pallas_call x1, Pallas kernels, score_parts(): pl.pallas_call(near_kernel, in_specs=[scalars] + [in_hbm()] * (COUNT + 1)...  6.29 us
    all_to_all x1, starting transfers between devices, scored(): lax.all_to_all(half_scores, ('y', 'z'), 0, 0, tiled=True)  4.48 us
  transfers between devices with their start and end apart: 21, of which 13 were waited for; matrix products, arithmetic and copies ran while one was open for 1% of the time, Pallas kernels for 3%

profile of v7, /device:TPU:1, one launch (start us, length us, event | category | flops | bytes accessed | tf_op | source)
XLA Modules:
  0.0 189.4 jit_solution(9265596833989797751)
XLA Ops:
  0.6 3.8 %shard_map.50 = bf16[2,2,4,2,32,1792]{5,4,3,2,1,0:T(8,128)(2,1)} custom-call(bf16[8,32,3584]{2,1,0:T(8,128)(2,1)} %rows_ref.1, s32[8,32]{1,0:T(8,128)} %valid_ref.1), custom_call_target="tpu_custom_call" | custom-call | tf_op jit(solution)/shard_map/pallas_call | solution.py:68
  4.4 55.0 %all_to_all.10 = bf16[32,32,1792]{2,1,0:T(8,128)(2,1)} all-to-all(bf16[32,32,1792]{2,1,0:T(8,128)(2,1)} %bitcast.5), channel_id=1, replica_groups=mesh['x'=4,'y'=4,'z'=4,'c'=2] {'y','z','c'}, dimensions={0} | all-to-all | bytes 7340032 | tf_op jit(solution)/shard_map/all_to_all | solution.py:251
  59.4 2.5 %collective-permute-start.1 = (bf16[112,896]{1,0:T(8,128)(2,1)S(1)}, bf16[112,896]{1,0:T(8,128)(2,1)S(1)}, u32[]{:S(2)}, u32[]{:S(2)}) collective-permute-start(bf16[112,896]{1,0:T(8,128)(2,1)S(1)} %constant_dynamic-slice_fusion), channel_id=1, source_target_pairs={{0,0},{1,8},{8,9},{9,1},{16,16},{17,24},{24,25},{25,17},{2,2},{3,1... | collective-permute-start | bytes 602120 | tf_op jit(solution)/shard_map/ppermute | solution.py:243
  61.9 1.9 %collective-permute-start.2 = (bf16[112,896]{1,0:T(8,128)(2,1)S(1)}, bf16[112,896]{1,0:T(8,128)(2,1)S(1)}, u32[]{:S(2)}, u32[]{:S(2)}) collective-permute-start(bf16[112,896]{1,0:T(8,128)(2,1)S(1)} %constant_dynamic-slice_fusion), channel_id=1, source_target_pairs={{0,8},{1,0},{8,1},{9,9},{16,24},{17,16},{24,17},{25,25},{2,10},{3,... | collective-permute-start | bytes 602120 | tf_op jit(solution)/shard_map/ppermute | solution.py:244
  63.9 2.0 %collective-permute-done.1 = bf16[112,896]{1,0:T(8,128)(2,1)S(1)} collective-permute-done((bf16[112,896]{1,0:T(8,128)(2,1)S(1)}, bf16[112,896]{1,0:T(8,128)(2,1)S(1)}, u32[]{:S(2)}, u32[]{:S(2)}) %collective-permute-start.1) | collective-permute-done | bytes 200736 | tf_op jit(solution)/shard_map/ppermute | solution.py:243
  65.9 3.0 %collective-permute-done.2 = bf16[112,896]{1,0:T(8,128)(2,1)S(1)} collective-permute-done((bf16[112,896]{1,0:T(8,128)(2,1)S(1)}, bf16[112,896]{1,0:T(8,128)(2,1)S(1)}, u32[]{:S(2)}, u32[]{:S(2)}) %collective-permute-start.2) | collective-permute-done | bytes 200736 | tf_op jit(solution)/shard_map/ppermute | solution.py:244
  69.0 1.3 collective-permute-start.3
  70.3 1.0 collective-permute-start.4
  71.4 1.2 collective-permute-start.10
  72.6 7.8 %collective-permute-done.3.refs_1_ = bf16[224,896]{1,0:T(8,128)(2,1)S(1)} collective-permute-done((bf16[224,896]{1,0:T(8,128)(2,1)S(1)}, bf16[224,896]{1,0:T(8,128)(2,1)S(1)}, u32[]{:S(2)}, u32[]{:S(2)}) %collective-permute-start.3) | collective-permute-done | bytes 401440 | tf_op jit(solution)/shard_map/ppermute | solution.py:20
  80.4 2.5 %collective-permute-start.6 = (bf16[224,896]{1,0:T(8,128)(2,1)S(1)}, bf16[224,896]{1,0:T(8,128)(2,1)S(1)}, u32[]{:S(2)}, u32[]{:S(2)}) collective-permute-start(bf16[224,896]{1,0:T(8,128)(2,1)S(1)} %maximum_select_fusion.refs_0_), channel_id=1, source_target_pairs={{0,96},{32,0},{64,32},{96,64},{1,97},{33,1},{65,33},{97,65},{2,98}... | collective-permute-start | bytes 1204232 | tf_op jit(solution)/shard_map/ppermute | solution.py:20
  82.9 2.5 %collective-permute-start.7 = (bf16[224,896]{1,0:T(8,128)(2,1)S(1)}, bf16[224,896]{1,0:T(8,128)(2,1)}, u32[]{:S(2)}, u32[]{:S(2)}) collective-permute-start(bf16[224,896]{1,0:T(8,128)(2,1)S(1)} %collective-permute-done.3.refs_1_), channel_id=1, source_target_pairs={{0,96},{32,0},{64,32},{96,64},{1,97},{33,1},{65,33},{97,65},{2,98}... | collective-permute-start | bytes 1204232 | tf_op jit(solution)/shard_map/ppermute | solution.py:20
  85.4 5.6 %collective-permute-done.5.refs_3_ = bf16[224,896]{1,0:T(8,128)(2,1)S(1)} collective-permute-done((bf16[224,896]{1,0:T(8,128)(2,1)S(1)}, bf16[224,896]{1,0:T(8,128)(2,1)S(1)}, u32[]{:S(2)}, u32[]{:S(2)}) %collective-permute-start.5) | collective-permute-done | bytes 401440 | tf_op jit(solution)/shard_map/ppermute | solution.py:20
  90.9 1.2 collective-permute-start.12
  92.2 1.5 collective-permute-start.8
  94.4 6.2 %collective-permute-done.7.refs_5_ = bf16[224,896]{1,0:T(8,128)(2,1)} collective-permute-done((bf16[224,896]{1,0:T(8,128)(2,1)S(1)}, bf16[224,896]{1,0:T(8,128)(2,1)}, u32[]{:S(2)}, u32[]{:S(2)}) %collective-permute-start.7) | collective-permute-done | bytes 401440 | tf_op jit(solution)/shard_map/ppermute | solution.py:20
  101.5 1.1 collective-permute-done.12.refs_10_
  102.7 5.2 %collective-permute-done.8.refs_6_ = bf16[224,896]{1,0:T(8,128)(2,1)S(1)} collective-permute-done((bf16[224,896]{1,0:T(8,128)(2,1)S(1)}, bf16[224,896]{1,0:T(8,128)(2,1)S(1)}, u32[]{:S(2)}, u32[]{:S(2)}) %collective-permute-start.8) | collective-permute-done | bytes 401440 | tf_op jit(solution)/shard_map/ppermute | solution.py:20
  108.0 3.1 %collective-permute-start.9 = (bf16[224,896]{1,0:T(8,128)(2,1)S(1)}, bf16[224,896]{1,0:T(8,128)(2,1)S(1)}, u32[]{:S(2)}, u32[]{:S(2)}) collective-permute-start(bf16[224,896]{1,0:T(8,128)(2,1)S(1)} %collective-permute-done.5.refs_3_), channel_id=1, source_target_pairs={{0,96},{32,0},{64,32},{96,64},{1,97},{33,1},{65,33},{97,65},{2,98}... | collective-permute-start | bytes 1204232 | tf_op jit(solution)/shard_map/ppermute | solution.py:20
  111.3 1.6 collective-permute-start.15
  112.9 6.9 %collective-permute-done.11.refs_9_ = bf16[224,896]{1,0:T(8,128)(2,1)S(1)} collective-permute-done((bf16[224,896]{1,0:T(8,128)(2,1)S(1)}, bf16[224,896]{1,0:T(8,128)(2,1)S(1)}, u32[]{:S(2)}, u32[]{:S(2)}) %collective-permute-start.11) | collective-permute-done | bytes 401440 | tf_op jit(solution)/shard_map/ppermute | solution.py:20
  122.1 6.4 %collective-permute-done.14.refs_12_ = bf16[224,896]{1,0:T(8,128)(2,1)S(1)} collective-permute-done((bf16[224,896]{1,0:T(8,128)(2,1)S(1)}, bf16[224,896]{1,0:T(8,128)(2,1)S(1)}, u32[]{:S(2)}, u32[]{:S(2)}) %collective-permute-start.14) | collective-permute-done | bytes 401440 | tf_op jit(solution)/shard_map/ppermute | solution.py:20
  130.0 2.7 %collective-permute-start.17 = (bf16[112,896]{1,0:T(8,128)(2,1)}, bf16[112,896]{1,0:T(8,128)(2,1)}, u32[]{:S(2)}, u32[]{:S(2)}) collective-permute-start(bf16[112,896]{1,0:T(8,128)(2,1)} %slice.17), channel_id=1, source_target_pairs={{0,96},{32,0},{64,32},{96,64},{1,97},{33,1},{65,33},{97,65},{2,98}... | collective-permute-start | bytes 602120 | tf_op jit(solution)/shard_map/ppermute | solution.py:20
  132.7 8.6 %collective-permute-done.16.refs_14_ = bf16[112,896]{1,0:T(8,128)(2,1)S(1)} collective-permute-done((bf16[112,896]{1,0:T(8,128)(2,1)}, bf16[112,896]{1,0:T(8,128)(2,1)S(1)}, u32[]{:S(2)}, u32[]{:S(2)}) %collective-permute-start.16) | collective-permute-done | bytes 200736 | tf_op jit(solution)/shard_map/ppermute | solution.py:20
  146.3 6.3 %shard_map.51.mixed_ref = f32[2,896,512]{2,1,0:T(8,128)S(1)} custom-call(s32[3]{0:T(128)S(1)} %pad_add_fusion.place_ref, bf16[1024,1792]{1,0:T(8,128)(2,1)} %bitcast.4.near_hbm, bf16[224,896]{1,0:T(8,128)(2,1)S(1)} %maximum_select_fusion.refs_0_, bf16[224,896]{1,0:T(8,128)(2,1)S(1)} %collective-permute-done.3.refs_1_, ...), custom_call_target="tpu_custom_call" | custom-call | flops 3288334336 | bytes 12582912 | tf_op jit(solution)/shard_map/pallas_call | solution.py:191
  152.7 9.3 %shard_map.52 = (bf16[16,32,1024]{2,1,0:T(8,128)(2,1)S(1)}, bf16[16,32,1024]{2,1,0:T(8,128)(2,1)S(1)}) custom-call(s32[3]{0:T(128)S(1)} %pad_add_fusion.place_ref, bf16[1024,1792]{1,0:T(8,128)(2,1)} %bitcast.4.near_hbm, bf16[1024,1792]{1,0:T(8,128)(2,1)} %collective-permute-done.far_hbm, f32[2,896,512]{2,1,0:T(8,128)S(1)} %shard_map.51.mixed_ref, ...), custom_call_target="tpu_custom_call" | custom-call | flops 5167382528 | bytes 16777216 | tf_op jit(solution)/shard_map/pallas_call | solution.py:208
  162.0 1.3 collective-permute-start.19
  163.3 2.3 %collective-permute-done.19 = bf16[16,32,1024]{2,1,0:T(8,128)(2,1)S(1)} collective-permute-done((bf16[16,32,1024]{2,1,0:T(8,128)(2,1)S(1)}, bf16[16,32,1024]{2,1,0:T(8,128)(2,1)S(1)}, u32[]{:S(2)}, u32[]{:S(2)}) %collective-permute-start.19) | collective-permute-done | bytes 1048608 | tf_op jit(solution)/shard_map/ppermute | solution.py:24
  165.6 1.4 add_convert_fusion
  167.0 4.5 %all-to-all-start.1 = ((bf16[16,32,1024]{2,1,0:T(8,128)(2,1)}), bf16[16,32,1024]{2,1,0:T(8,128)(2,1)S(1)}, u32[]{:S(2)}, u32[]{:S(2)}) async-start(bf16[16,32,1024]{2,1,0:T(8,128)(2,1)} %add_convert_fusion), calls=%async_computation.1 | async-start | bytes 2097152 | tf_op jit(solution)/shard_map/all_to_all | solution.py:267
  171.5 15.6 %all-to-all-done.1 = bf16[16,32,1024]{2,1,0:T(8,128)(2,1)S(1)} async-done(((bf16[16,32,1024]{2,1,0:T(8,128)(2,1)}), bf16[16,32,1024]{2,1,0:T(8,128)(2,1)S(1)}, u32[]{:S(2)}, u32[]{:S(2)}) %all-to-all-start.1) | async-done | bytes 1048608 | tf_op jit(solution)/shard_map/all_to_all | solution.py:267
  187.4 1.4 fusion
  (58 shorter events, 11.9 us)
Async XLA Ops:
  0.6 58.8 %copy-start = (bf16[112,3584]{1,0:T(8,128)(2,1)S(1)}, bf16[112,3584]{1,0:T(8,128)(2,1)}, u32[]{:S(2)}) copy-start(bf16[112,3584]{1,0:T(8,128)(2,1)} %param.4) | copy-start | bytes 2408452
  59.4 93.2 %collective-permute-start = (bf16[1024,1792]{1,0:T(8,128)(2,1)}, bf16[1024,1792]{1,0:T(8,128)(2,1)}, u32[]{:S(2)}, u32[]{:S(2)}) collective-permute-start(bf16[1024,1792]{1,0:T(8,128)(2,1)} %bitcast.4.near_hbm), channel_id=1, source_target_pairs={{0,1},{1,0},{2,3},{3,2},{4,5},{5,4},{6,7},{7,6},{8,9},{9,8},{10,11... | collective-permute-start | bytes 11010056 | tf_op jit(solution)/shard_map/ppermute | solution.py:24
  59.4 6.5 %collective-permute-start.1 = (bf16[112,896]{1,0:T(8,128)(2,1)S(1)}, bf16[112,896]{1,0:T(8,128)(2,1)S(1)}, u32[]{:S(2)}, u32[]{:S(2)}) collective-permute-start(bf16[112,896]{1,0:T(8,128)(2,1)S(1)} %constant_dynamic-slice_fusion), channel_id=1, source_target_pairs={{0,0},{1,8},{8,9},{9,1},{16,16},{17,24},{24,25},{25,17},{2,2},{3,1... | collective-permute-start | bytes 602120 | tf_op jit(solution)/shard_map/ppermute | solution.py:243
  61.9 7.0 %collective-permute-start.2 = (bf16[112,896]{1,0:T(8,128)(2,1)S(1)}, bf16[112,896]{1,0:T(8,128)(2,1)S(1)}, u32[]{:S(2)}, u32[]{:S(2)}) collective-permute-start(bf16[112,896]{1,0:T(8,128)(2,1)S(1)} %constant_dynamic-slice_fusion), channel_id=1, source_target_pairs={{0,8},{1,0},{8,1},{9,9},{16,24},{17,16},{24,17},{25,25},{2,10},{3,... | collective-permute-start | bytes 602120 | tf_op jit(solution)/shard_map/ppermute | solution.py:244
  69.0 11.4 %collective-permute-start.3 = (bf16[224,896]{1,0:T(8,128)(2,1)S(1)}, bf16[224,896]{1,0:T(8,128)(2,1)S(1)}, u32[]{:S(2)}, u32[]{:S(2)}) collective-permute-start(bf16[224,896]{1,0:T(8,128)(2,1)S(1)} %maximum_select_fusion.refs_0_), channel_id=1, source_target_pairs={{0,6},{2,0},{4,2},{6,4},{1,7},{3,1},{5,3},{7,5},{8,14},{10,8},{12,... | collective-permute-start | bytes 1204232 | tf_op jit(solution)/shard_map/ppermute | solution.py:20
  70.3 12.6 %collective-permute-start.4 = (bf16[224,896]{1,0:T(8,128)(2,1)S(1)}, bf16[224,896]{1,0:T(8,128)(2,1)S(1)}, u32[]{:S(2)}, u32[]{:S(2)}) collective-permute-start(bf16[224,896]{1,0:T(8,128)(2,1)S(1)} %maximum_select_fusion.refs_0_), channel_id=1, source_target_pairs={{0,4},{2,6},{4,0},{6,2},{1,5},{3,7},{5,1},{7,3},{8,12},{10,14},{12... | collective-permute-start | bytes 1204232 | tf_op jit(solution)/shard_map/ppermute | solution.py:20
  71.4 19.6 %collective-permute-start.5 = (bf16[224,896]{1,0:T(8,128)(2,1)S(1)}, bf16[224,896]{1,0:T(8,128)(2,1)S(1)}, u32[]{:S(2)}, u32[]{:S(2)}) collective-permute-start(bf16[224,896]{1,0:T(8,128)(2,1)S(1)} %maximum_select_fusion.refs_0_), channel_id=1, source_target_pairs={{0,2},{2,4},{4,6},{6,0},{1,3},{3,5},{5,7},{7,1},{8,10},{10,12},{12... | collective-permute-start | bytes 1204232 | tf_op jit(solution)/shard_map/ppermute | solution.py:20
  71.4 20.8 %collective-permute-start.10 = (bf16[224,896]{1,0:T(8,128)(2,1)S(1)}, bf16[224,896]{1,0:T(8,128)(2,1)S(1)}, u32[]{:S(2)}, u32[]{:S(2)}) collective-permute-start(bf16[224,896]{1,0:T(8,128)(2,1)S(1)} %maximum_select_fusion.refs_0_), channel_id=1, source_target_pairs={{0,32},{32,64},{64,96},{96,0},{1,33},{33,65},{65,97},{97,1},{2,34}... | collective-permute-start | bytes 1204232 | tf_op jit(solution)/shard_map/ppermute | solution.py:20
  80.4 13.2 %collective-permute-start.6 = (bf16[224,896]{1,0:T(8,128)(2,1)S(1)}, bf16[224,896]{1,0:T(8,128)(2,1)S(1)}, u32[]{:S(2)}, u32[]{:S(2)}) collective-permute-start(bf16[224,896]{1,0:T(8,128)(2,1)S(1)} %maximum_select_fusion.refs_0_), channel_id=1, source_target_pairs={{0,96},{32,0},{64,32},{96,64},{1,97},{33,1},{65,33},{97,65},{2,98}... | collective-permute-start | bytes 1204232 | tf_op jit(solution)/shard_map/ppermute | solution.py:20
  82.9 17.7 %collective-permute-start.7 = (bf16[224,896]{1,0:T(8,128)(2,1)S(1)}, bf16[224,896]{1,0:T(8,128)(2,1)}, u32[]{:S(2)}, u32[]{:S(2)}) collective-permute-start(bf16[224,896]{1,0:T(8,128)(2,1)S(1)} %collective-permute-done.3.refs_1_), channel_id=1, source_target_pairs={{0,96},{32,0},{64,32},{96,64},{1,97},{33,1},{65,33},{97,65},{2,98}... | collective-permute-start | bytes 1204232 | tf_op jit(solution)/shard_map/ppermute | solution.py:20
  90.9 11.7 %collective-permute-start.12 = (bf16[224,896]{1,0:T(8,128)(2,1)S(1)}, bf16[224,896]{1,0:T(8,128)(2,1)S(1)}, u32[]{:S(2)}, u32[]{:S(2)}) collective-permute-start(bf16[224,896]{1,0:T(8,128)(2,1)S(1)} %collective-permute-done.4.refs_2_), channel_id=1, source_target_pairs={{0,32},{32,64},{64,96},{96,0},{1,33},{33,65},{65,97},{97,1},{2,34}... | collective-permute-start | bytes 1204232 | tf_op jit(solution)/shard_map/ppermute | solution.py:20
  92.2 37.0 %copy-start.1 = (bf16[224,896]{1,0:T(8,128)(2,1)}, bf16[224,896]{1,0:T(8,128)(2,1)S(1)}, u32[]{:S(2)}) copy-start(bf16[224,896]{1,0:T(8,128)(2,1)S(1)} %collective-permute-done.10.refs_8_) | copy-start | bytes 1204228
  92.2 15.8 %collective-permute-start.8 = (bf16[224,896]{1,0:T(8,128)(2,1)S(1)}, bf16[224,896]{1,0:T(8,128)(2,1)S(1)}, u32[]{:S(2)}, u32[]{:S(2)}) collective-permute-start(bf16[224,896]{1,0:T(8,128)(2,1)S(1)} %collective-permute-done.4.refs_2_), channel_id=1, source_target_pairs={{0,96},{32,0},{64,32},{96,64},{1,97},{33,1},{65,33},{97,65},{2,98}... | collective-permute-start | bytes 1204232 | tf_op jit(solution)/shard_map/ppermute | solution.py:20
  94.4 16.9 %collective-permute-start.13 = (bf16[224,896]{1,0:T(8,128)(2,1)S(1)}, bf16[224,896]{1,0:T(8,128)(2,1)}, u32[]{:S(2)}, u32[]{:S(2)}) collective-permute-start(bf16[224,896]{1,0:T(8,128)(2,1)S(1)} %collective-permute-done.5.refs_3_), channel_id=1, source_target_pairs={{0,32},{32,64},{64,96},{96,0},{1,33},{33,65},{65,97},{97,1},{2,34}... | collective-permute-start | bytes 1204232 | tf_op jit(solution)/shard_map/ppermute | solution.py:20
  100.6 19.2 %collective-permute-start.11 = (bf16[224,896]{1,0:T(8,128)(2,1)S(1)}, bf16[224,896]{1,0:T(8,128)(2,1)S(1)}, u32[]{:S(2)}, u32[]{:S(2)}) collective-permute-start(bf16[224,896]{1,0:T(8,128)(2,1)S(1)} %collective-permute-done.3.refs_1_), channel_id=1, source_target_pairs={{0,32},{32,64},{64,96},{96,0},{1,33},{33,65},{65,97},{97,1},{2,34}... | collective-permute-start | bytes 1204232 | tf_op jit(solution)/shard_map/ppermute | solution.py:20
  102.6 25.8 %collective-permute-start.14 = (bf16[224,896]{1,0:T(8,128)(2,1)S(1)}, bf16[224,896]{1,0:T(8,128)(2,1)S(1)}, u32[]{:S(2)}, u32[]{:S(2)}) collective-permute-start(bf16[224,896]{1,0:T(8,128)(2,1)S(1)} %collective-permute-done.10.refs_8_), channel_id=1, source_target_pairs={{0,32},{32,64},{64,96},{96,0},{1,33},{33,65},{65,97},{97,1},{2,34}... | collective-permute-start | bytes 1204232 | tf_op jit(solution)/shard_map/ppermute | solution.py:20
  108.0 21.2 %collective-permute-start.9 = (bf16[224,896]{1,0:T(8,128)(2,1)S(1)}, bf16[224,896]{1,0:T(8,128)(2,1)S(1)}, u32[]{:S(2)}, u32[]{:S(2)}) collective-permute-start(bf16[224,896]{1,0:T(8,128)(2,1)S(1)} %collective-permute-done.5.refs_3_), channel_id=1, source_target_pairs={{0,96},{32,0},{64,32},{96,64},{1,97},{33,1},{65,33},{97,65},{2,98}... | collective-permute-start | bytes 1204232 | tf_op jit(solution)/shard_map/ppermute | solution.py:20
  111.3 30.0 %collective-permute-start.15 = (bf16[224,896]{1,0:T(8,128)(2,1)}, bf16[224,896]{1,0:T(8,128)(2,1)}, u32[]{:S(2)}, u32[]{:S(2)}) collective-permute-start(bf16[224,896]{1,0:T(8,128)(2,1)} %collective-permute-done.7.refs_5_), channel_id=1, source_target_pairs={{0,96},{32,0},{64,32},{96,64},{1,97},{33,1},{65,33},{97,65},{2,98}... | collective-permute-start | bytes 1204232 | tf_op jit(solution)/shard_map/ppermute | solution.py:20
  120.6 20.8 %collective-permute-start.18 = (bf16[224,896]{1,0:T(8,128)(2,1)}, bf16[224,896]{1,0:T(8,128)(2,1)}, u32[]{:S(2)}, u32[]{:S(2)}) collective-permute-start(bf16[224,896]{1,0:T(8,128)(2,1)} %collective-permute-done.13.refs_11_), channel_id=1, source_target_pairs={{0,32},{32,64},{64,96},{96,0},{1,33},{33,65},{65,97},{97,1},{2,34}... | collective-permute-start | bytes 1204232 | tf_op jit(solution)/shard_map/ppermute | solution.py:20
  129.2 12.2 %collective-permute-start.16 = (bf16[112,896]{1,0:T(8,128)(2,1)}, bf16[112,896]{1,0:T(8,128)(2,1)S(1)}, u32[]{:S(2)}, u32[]{:S(2)}) collective-permute-start(bf16[112,896]{1,0:T(8,128)(2,1)} %slice.16), channel_id=1, source_target_pairs={{0,32},{32,64},{64,96},{96,0},{1,33},{33,65},{65,97},{97,1},{2,34}... | collective-permute-start | bytes 602120 | tf_op jit(solution)/shard_map/ppermute | solution.py:20
  130.0 11.4 %collective-permute-start.17 = (bf16[112,896]{1,0:T(8,128)(2,1)}, bf16[112,896]{1,0:T(8,128)(2,1)}, u32[]{:S(2)}, u32[]{:S(2)}) collective-permute-start(bf16[112,896]{1,0:T(8,128)(2,1)} %slice.17), channel_id=1, source_target_pairs={{0,96},{32,0},{64,32},{96,64},{1,97},{33,1},{65,33},{97,65},{2,98}... | collective-permute-start | bytes 602120 | tf_op jit(solution)/shard_map/ppermute | solution.py:20
  141.3 1.0 copy-start.2
  142.3 1.0 copy-start.5
  144.3 1.0 copy-start.11
  146.3 6.3 %copy-start.3 = (bf16[224,896]{1,0:T(8,128)(2,1)S(1)}, bf16[224,896]{1,0:T(8,128)(2,1)}, u32[]{:S(2)}) copy-start(bf16[224,896]{1,0:T(8,128)(2,1)} %copy-done.1) | copy-start | bytes 1204228
  146.3 6.3 %copy-start.6 = (bf16[224,896]{1,0:T(8,128)(2,1)S(1)}, bf16[224,896]{1,0:T(8,128)(2,1)}, u32[]{:S(2)}) copy-start(bf16[224,896]{1,0:T(8,128)(2,1)} %copy-done.4) | copy-start | bytes 1204228
  146.3 6.3 %copy-start.9 = (bf16[224,896]{1,0:T(8,128)(2,1)S(1)}, bf16[224,896]{1,0:T(8,128)(2,1)}, u32[]{:S(2)}) copy-start(bf16[224,896]{1,0:T(8,128)(2,1)} %copy-done.7) | copy-start | bytes 1204228
  146.3 6.4 %copy-start.12 = (bf16[224,896]{1,0:T(8,128)(2,1)S(1)}, bf16[224,896]{1,0:T(8,128)(2,1)}, u32[]{:S(2)}) copy-start(bf16[224,896]{1,0:T(8,128)(2,1)} %copy-done.10) | copy-start | bytes 1204228
  146.3 6.4 %copy-start.15 = (bf16[224,896]{1,0:T(8,128)(2,1)S(1)}, bf16[224,896]{1,0:T(8,128)(2,1)}, u32[]{:S(2)}) copy-start(bf16[224,896]{1,0:T(8,128)(2,1)} %copy-done.13) | copy-start | bytes 1204228
  162.0 3.6 %collective-permute-start.19 = (bf16[16,32,1024]{2,1,0:T(8,128)(2,1)S(1)}, bf16[16,32,1024]{2,1,0:T(8,128)(2,1)S(1)}, u32[]{:S(2)}, u32[]{:S(2)}) collective-permute-start(bf16[16,32,1024]{2,1,0:T(8,128)(2,1)S(1)} %get-tuple-element.5), channel_id=1, source_target_pairs={{0,1},{1,0},{2,3},{3,2},{4,5},{5,4},{6,7},{7,6},{8,9},{9,8},{10,11... | collective-permute-start | bytes 3145736 | tf_op jit(solution)/shard_map/ppermute | solution.py:24
  165.6 5.9 %copy-start.16 = (s32[8,32]{1,0:T(8,128)S(1)}, s32[8,32]{1,0:T(8,128)}, u32[]{:S(2)}) copy-start(s32[8,32]{1,0:T(8,128)} %valid_ref.1) | copy-start | bytes 3076
  167.0 20.1 %all-to-all-start.1 = ((bf16[16,32,1024]{2,1,0:T(8,128)(2,1)}), bf16[16,32,1024]{2,1,0:T(8,128)(2,1)S(1)}, u32[]{:S(2)}, u32[]{:S(2)}) async-start(bf16[16,32,1024]{2,1,0:T(8,128)(2,1)} %add_convert_fusion), calls=%async_computation.1 | async-start | bytes 2097152 | tf_op jit(solution)/shard_map/all_to_all | solution.py:267
  (6 other events, 5.0 us)
